TPU v7x, 32 devices: a whole 2x2x4 slice. The times are simulated.
32 devices in a mesh: col: 4 (over y, x), sec: 8 (over z, core).
Axes of the slice: x: 2, y: 2, z: 4, core: 2. Of those that a mesh axis runs over, the one named last changes fastest.
Arguments:
- thermal_state: float32 [128, 64, 256], P('sec', 'col'), may hold values from -6 to 6
- flow_vector: float32 [2, 128, 64, 256], P(None, 'sec', 'col'), may hold values from -5 to 5
- vertical_spreading: float32 [128, 64, 256], P('sec', 'col'), may hold values from 0.05 to 0.5
- solute_fields: float32 [32, 128, 64, 256], P('sec', None, 'col'), may hold values from 0.1 to 2
- linear_exchange_speeds: float32 [32, 32], replicated, may hold values from -1 to 1
- newton_preconditioner: float32 [32, 32], replicated, may hold values from -0.6 to 1.2
- absorption_speed: float32 [32], replicated, may hold values from 0.2 to 2
- water_indicator: int32 [64, 256], P('col'), may hold values from 0 to 1, as said below
Outputs:
- thermal_revised: float32 [128, 64, 256], P('sec', 'col')
- velocity_next: float32 [2, 128, 64, 256], P(None, 'sec', 'col')
- diffusivity_next: float32 [128, 64, 256], P('sec', 'col')
- solute_revised: float32 [32, 128, 64, 256], P('sec', None, 'col')
Inputs may be any that keep to these rules, and one draw needn't show every extreme that they name: `water_indicator`: in each block of 16 consecutive longitudes, between 1536 and 3072 columns are wet, and some block holds exactly 3072 wet columns.
All inputs are finite; a program needn't handle non-finite values.
Results may differ from a plain program's by a relative error of at most 0.0001.
Values sent between devices are 32-bit elements; how exact they have to be, the bound alone decides.
No kernel may reach another device: no remote copies, remote signals or barrier semaphores. Data moves between devices by JAX's collectives and lax.ppermute only.
A program may use at most 128 MiB of HBM per device.

v0:
```python
import functools

import jax
import jax.numpy as jnp
from jax import lax
from jax.experimental import pallas as pl
from jax.experimental.pallas import tpu as pltpu
from jax.sharding import PartitionSpec as P


NEWTON = 2
CORIOLIS = 0.8
MIXING = 0.1
ADVECTION = 0.2
VERTICAL_MIX = 0.3
WATER_ABSORB = 0.02
PIGMENT_ABSORB = 0.06
CHLOROPHYLL_WARM = 10.0
LANES = 128
ROWS = 8


def shifted(block, axis, distance):
    devices = range(lax.axis_size(axis))
    route = [(i - distance, i) for i in devices if i - distance in devices]
    return lax.ppermute(block, axis, route)


def around(block, axis, distance):
    count = lax.axis_size(axis)
    return lax.ppermute(block, axis, [(i, (i + distance) % count) for i in range(count)])


def chemical_change(center, eastern, western, east_flow, north_flow):
    northern = jnp.concatenate([center[..., 1:], center[..., -1:]], axis=-1)
    southern = jnp.concatenate([center[..., :1], center[..., :-1]], axis=-1)
    laplace = eastern + western + northern + southern - 4.0 * center
    return MIXING * laplace - 0.5 * ADVECTION * (
        east_flow * (eastern - western) + north_flow * (northern - southern)
    )


def edges_kernel(n, level, turn, *refs):
    cur = refs[:n]
    head, tail = refs[n : n + 2]
    held, nl, across, _ = cur[0].shape
    for d in range(n):
        for i in range(held):
            for l in range(nl):
                at = (d * held + i) * nl + l
                head[at : at + 1, :] = cur[d][i, l, 0:1, :]
                tail[at : at + 1, :] = cur[d][i, l, across - 1 : across, :]
    if level is not None:
        for d in range(n):
            refs[n + 2][d * held : (d + 1) * held] = cur[(d + turn) % n][:, level : level + 1]


def chunk_edges(blocks, level, turn):
    n = len(blocks)
    held, nl, across, lat = blocks[0].shape
    shapes = [jax.ShapeDtypeStruct((n * held * nl, lat), jnp.float32)] * 2
    if level is not None:
        shapes.append(jax.ShapeDtypeStruct((n * held, 1, across, lat), jnp.float32))
    return pl.pallas_call(
        functools.partial(edges_kernel, n, level, turn),
        in_specs=[pl.BlockSpec(memory_space=pltpu.VMEM)] * n,
        out_specs=[pl.BlockSpec(memory_space=pltpu.VMEM)] * len(shapes),
        out_shape=shapes,
        cost_estimate=pl.CostEstimate(
            flops=10**8, bytes_accessed=4 * n * blocks[0].size, transcendentals=0
        ),
        name="edges",
    )(*blocks)


def react_kernel(n, nl, q, *refs):
    me_ref, tile_ref, shift_ref = refs[:3]
    cur = refs[3 : 3 + n]
    below = refs[3 + n : 3 + 2 * n]
    above = refs[3 + 2 * n : 3 + 3 * n]
    rest = refs[3 + 3 * n :]
    east_halo, west_halo, east, north, kmix, water, speeds, precon, rates, pick = rest[:10]
    outs = rest[10 : 10 + n]
    pigment = rest[10 + n]
    moved, done, packed = rest[11 + n :]
    held, _, across, lat = cur[0].shape
    tracers = n * held
    halves = across // ROWS

    row_at = lax.broadcasted_iota(jnp.int32, (across, lat), 0)
    lane_at = lax.broadcasted_iota(jnp.int32, (across, lat), 1)
    wet = water[...]
    for l in range(nl):
        u = (0.5 * ADVECTION) * wet * east[l]
        v = (0.5 * ADVECTION) * wet * north[l]
        mix = MIXING * wet
        up = wet * kmix[q * nl + l + 1]
        down = wet * kmix[q * nl + l]
        to_east = mix - u
        to_west = mix + u
        last = lane_at == lat - 1
        first = lane_at == 0
        middle = 1.0 - 4.0 * mix - up - down
        to_north = mix - v
        to_south = mix + v
        middle = middle + jnp.where(last, to_north, 0.0) + jnp.where(first, to_south, 0.0)
        to_north = jnp.where(last, 0.0, to_north)
        to_south = jnp.where(first, 0.0, to_south)
        for d in range(n):
            for i in range(held):
                t = d * held + i
                c = cur[d][i, l]
                lower = cur[d][i, l - 1] if l > 0 else below[d][i, 0]
                upper = cur[d][i, l + 1] if l < nl - 1 else above[d][i, 0]
                at = t * nl + l
                e = jnp.where(
                    row_at == across - 1, east_halo[at : at + 1, :], pltpu.roll(c, across - 1, 0)
                )
                w = jnp.where(row_at == 0, west_halo[at : at + 1, :], pltpu.roll(c, 1, 0))
                value = middle * c + to_east * e + to_west * w
                value = value + to_north * pltpu.roll(c, lat - 1, 1) + to_south * pltpu.roll(c, 1, 1)
                value = value + up * upper + down * lower
                for h in range(halves):
                    moved[l * halves + h, t * ROWS : (t + 1) * ROWS, :] = value[
                        h * ROWS : (h + 1) * ROWS
                    ]

    def product(weights, x):
        high = x.astype(jnp.bfloat16)
        low = (x - high.astype(jnp.float32)).astype(jnp.bfloat16)
        return jnp.dot(
            weights[...],
            jnp.concatenate([high, low, high], axis=0),
            preferred_element_type=jnp.float32,
        )

    def uptake(x):
        square = x * x
        return rates[...] * (square / (1.0 + square))

    def react(j, carry):
        start = moved[j]
        current = start
        for step in range(NEWTON):
            misfit = uptake(current) - product(speeds, current)
            if step > 0:
                misfit = misfit + (current - start)
            current = current - product(precon, misfit)
        l = j // halves
        h = j % halves
        for t in range(tracers):
            at = pl.multiple_of((t * nl + l) * across + h * ROWS, ROWS)
            for s in range(lat // LANES):
                done[s, pl.ds(at, ROWS), :] = current[
                    t * ROWS : (t + 1) * ROWS, s * LANES : (s + 1) * LANES
                ]
        return carry

    lax.fori_loop(0, nl * halves, react, 0)

    me = me_ref[0]
    for l in range(nl):
        at = pl.multiple_of((me * (held * nl) + l) * across, ROWS)
        for s in range(lat // LANES):
            pigment[l, :, s * LANES : (s + 1) * LANES] = done[s, pl.ds(at, across), :]

    lane = lax.broadcasted_iota(jnp.int32, (ROWS, LANES), 1)
    parts = lat // LANES

    def pack(x, carry):
        for s in range(parts):
            segment = x * parts + s
            tile = pl.multiple_of(tile_ref[segment] * LANES, LANES)
            tail = pl.multiple_of(tile_ref[segment] * LANES + LANES, LANES)
            keep = lane < shift_ref[segment]
            index = jnp.broadcast_to(pick[pl.ds(segment, 1), :], (ROWS, LANES))
            for g in range(tracers * nl // ROWS):
                value = done[s, pl.ds(g * ROWS * across + x, ROWS, stride=across), :]
                value = jnp.take_along_axis(value, index, axis=1, mode="promise_in_bounds")
                here = (slice(g * ROWS, (g + 1) * ROWS), pl.ds(tile, LANES))
                packed[here] = jnp.where(keep, packed[here], value)
                packed[g * ROWS : (g + 1) * ROWS, pl.ds(tail, LANES)] = value
        return carry

    lax.fori_loop(0, across, pack, 0)
    for d in range(n):
        outs[d][...] = packed[d * held * nl : (d + 1) * held * nl, : outs[d].shape[1]]


def react_chunk(q, nl, me, tiles, shifts, blocks, below, above, halos, fields, cap):
    n = len(blocks)
    held, _, across, lat = blocks[0].shape
    east, north, kmix, water, speeds, precon, rates, pick = fields
    rows = n * held * ROWS
    whole = pl.BlockSpec(memory_space=pltpu.VMEM)

    def level(spec_at):
        return pl.BlockSpec((held, 1, across, lat), lambda i, *_: (0, spec_at, 0, 0))

    def all_of(x):
        return pl.BlockSpec(x.shape, lambda i, *_: (0,) * x.ndim)

    ins = list(blocks)
    specs = [all_of(b) for b in blocks]
    for source, at in (below, above):
        for d in range(n):
            if isinstance(source, list):
                ins.append(source[d])
                specs.append(level(at))
            else:
                ins.append(source)
                specs.append(
                    pl.BlockSpec((held, 1, across, lat), lambda i, *_, d=d: (d, 0, 0, 0))
                )
    for x in halos:
        ins.append(x)
        specs.append(all_of(x))
    for x in (east, north):
        ins.append(x)
        specs.append(pl.BlockSpec((nl, across, lat), lambda i, *_: (q, 0, 0)))
    for x in (kmix, water, speeds, precon, rates, pick):
        ins.append(x)
        specs.append(all_of(x))
    out_block = jax.ShapeDtypeStruct((held * nl, cap), jnp.float32)
    shapes = [out_block] * n + [jax.ShapeDtypeStruct((nl, across, lat), jnp.float32)]
    lanes = (cap // LANES + 2) * LANES
    flops = 2 * 12 * rows * rows * lat * nl * (across // ROWS)
    return pl.pallas_call(
        functools.partial(react_kernel, n, nl, q),
        grid_spec=pltpu.PrefetchScalarGridSpec(
            num_scalar_prefetch=3,
            grid=(1,),
            in_specs=specs,
            out_specs=[
                pl.BlockSpec(s.shape, lambda i, *_, k=len(s.shape): (0,) * k) for s in shapes
            ],
            scratch_shapes=[
                pltpu.VMEM((nl * (across // ROWS), rows, lat), jnp.float32),
                pltpu.VMEM((lat // LANES, n * held * nl * across, LANES), jnp.float32),
                pltpu.VMEM((n * held * nl, lanes), jnp.float32),
            ],
        ),
        out_shape=shapes,
        cost_estimate=pl.CostEstimate(
            flops=flops, bytes_accessed=4 * 3 * rows * nl * across * lat // ROWS, transcendentals=0
        ),
        name="react",
    )(me, tiles, shifts, *ins)


def unpack_kernel(n, has_base, *refs):
    _, tile_ref = refs[:2]
    received = refs[2 : 2 + n]
    solute, water, pick, second = refs[2 + n : 6 + n]
    out, slots, spread = refs[6 + n + has_base :]
    held, nl, across, lat = solute.shape
    cap = received[0].shape[1]
    d = pl.program_id(0)
    for k in range(n):

        @pl.when(d == k)
        def _():
            slots[:, :cap] = received[k][...]

    parts = lat // LANES
    for x in range(across):
        for s in range(parts):
            segment = x * parts + s
            tile = pl.multiple_of(tile_ref[segment] * LANES, LANES)
            tail = pl.multiple_of(tile_ref[segment] * LANES + LANES, LANES)
            index = jnp.broadcast_to(pick[segment : segment + 1, :], (ROWS, LANES))
            later = jnp.broadcast_to(second[segment : segment + 1, :], (ROWS, LANES)) > 0
            for g in range(held * nl // ROWS):
                group = slice(g * ROWS, (g + 1) * ROWS)
                a = jnp.take_along_axis(
                    slots[group, pl.ds(tile, LANES)], index, axis=1, mode="promise_in_bounds"
                )
                b = jnp.take_along_axis(
                    slots[group, pl.ds(tail, LANES)], index, axis=1, mode="promise_in_bounds"
                )
                spread[s, pl.ds(g * ROWS * across + x, ROWS, stride=across), :] = jnp.where(
                    later, b, a
                )
    wet = water[...] > 0.5
    for i in range(held):
        for l in range(nl):
            at = (i * nl + l) * across
            for s in range(parts):
                lanes = slice(s * LANES, (s + 1) * LANES)
                out[i, l, :, lanes] = jnp.where(
                    wet[:, lanes], spread[s, at : at + across, :], solute[i, l, :, lanes]
                )


def unpack_chunk(q, parts, me, tiles, received, solute, water, pick, second, base):
    n = len(received)
    held, depth, across, lat = solute.shape
    nl = depth // n // parts
    cap = received[0].shape[1]

    def all_of(x):
        return pl.BlockSpec(x.shape, lambda d, *_: (0,) * x.ndim)

    place = pl.BlockSpec(
        (held, nl, across, lat), lambda d, me, *_: (0, lax.rem(me[0] + d, n) * parts + q, 0, 0)
    )
    specs = [all_of(x) for x in received] + [place, all_of(water), all_of(pick), all_of(second)]
    ins = [*received, solute, water, pick, second]
    aliases = {}
    if base is not None:
        aliases = {2 + len(ins): 0}
        ins.append(base)
        specs.append(pl.BlockSpec(memory_space=pl.ANY))
    return pl.pallas_call(
        functools.partial(unpack_kernel, n, base is not None),
        grid_spec=pltpu.PrefetchScalarGridSpec(
            num_scalar_prefetch=2,
            grid=(n,),
            in_specs=specs,
            out_specs=place,
            scratch_shapes=[
                pltpu.VMEM((held * nl, (cap // LANES + 2) * LANES), jnp.float32),
                pltpu.VMEM((lat // LANES, held * nl * across, LANES), jnp.float32),
            ],
        ),
        out_shape=jax.ShapeDtypeStruct(solute.shape, jnp.float32),
        input_output_aliases=aliases,
        cost_estimate=pl.CostEstimate(
            flops=100 * solute.size, bytes_accessed=12 * solute.size // parts, transcendentals=0
        ),
        name="unpack",
    )(me, tiles, *ins)


def relative(x, me, n, axis):
    x = jnp.flip(x, axis)
    return lax.dynamic_slice_in_dim(jnp.concatenate([x, x], axis), n - 1 - me, n, axis)


def halves_of(x):
    high = lax.reduce_precision(x, 8, 7)
    low = x - high
    return jnp.concatenate([high, high, low], axis=1).astype(jnp.bfloat16)


def plan(held, levels):
    nl = max(levels // 4, ROWS // held)
    parts = levels // nl
    inner = list(range(1, parts - 1))
    return nl, parts, inner + [q for q in range(parts) if q not in inner]


def on_device(
    thermal_state,
    flow_vector,
    vertical_spreading,
    solute_fields,
    linear_exchange_speeds,
    newton_preconditioner,
    absorption_speed,
    water_indicator,
):
    n = lax.axis_size("sec")
    me = lax.axis_index("sec")
    held, depth, across, lat = solute_fields.shape
    tracers = n * held
    levels = depth // n
    nl, parts, order = plan(held, levels)
    me_at = jnp.reshape(me, (1,)).astype(jnp.int32)

    flow_after = shifted(flow_vector[:, :1], "sec", -1)
    before = shifted(
        jnp.concatenate([flow_vector[:, -1:], vertical_spreading[None, -1:]], axis=0), "sec", 1
    )
    thermal_west = around(thermal_state[:, -1:], "col", 1)
    thermal_east = around(thermal_state[:, :1], "col", -1)

    blocks = {}
    for q in range(parts):
        blocks[q] = []
        for d in range(n):
            to = lax.rem(me + d, n)
            block = lax.dynamic_slice_in_dim(solute_fields, to * levels + q * nl, nl, 1)
            blocks[q].append(around(block, "sec", d) if d else block)

    latitude = jnp.pi * (jnp.arange(lat).astype(jnp.float32) + 0.5) / lat - jnp.pi / 2
    rotation = CORIOLIS * jnp.sin(latitude)
    shortwave = jnp.cos(latitude)
    divisor = 1.0 + rotation * rotation

    def turned(flow):
        return ((flow[0] + rotation * flow[1]) / divisor, (flow[1] - rotation * flow[0]) / divisor)

    def mixed(this, below, spread):
        shear = (this[0] - below[0]) ** 2 + (this[1] - below[1]) ** 2
        return 0.5 * spread + 0.5 * shear / (1.0 + shear)

    east, north = turned(flow_vector)
    after = turned(flow_after)
    ahead = turned(before[:2])
    below = tuple(jnp.concatenate([f[1:], g], axis=0) for f, g in zip((east, north), after))
    spreading = mixed((east, north), below, vertical_spreading)
    level_at = me * levels + jnp.arange(levels)
    kmix = jnp.where((level_at < depth - 1)[:, None, None], VERTICAL_MIX * spreading, 0.0)
    ahead_mix = VERTICAL_MIX * mixed(ahead, (east[:1], north[:1]), before[2])
    kmix = jnp.concatenate([jnp.where(me > 0, ahead_mix, 0.0), kmix], axis=0)
    thermal_carried = thermal_state + chemical_change(
        thermal_state,
        jnp.concatenate([thermal_state[:, 1:], thermal_east], axis=1),
        jnp.concatenate([thermal_west, thermal_state[:, :-1]], axis=1),
        east,
        north,
    )

    water = water_indicator.astype(jnp.float32)
    cap = -(-3 * across * lat // 4 // LANES) * LANES
    wet = (water_indicator > 0).astype(jnp.int32).reshape(-1, LANES)
    within = jnp.cumsum(wet, axis=1) - wet
    count = jnp.sum(wet, axis=1)
    offset = jnp.cumsum(count) - count
    tiles = offset // LANES
    shifts = offset % LANES
    slot = within + shifts[:, None]
    lane = jnp.arange(LANES, dtype=jnp.int32)
    hit = (slot % LANES)[:, None, :] == lane[None, :, None]
    gather = jnp.sum(
        jnp.where(hit & (wet > 0)[:, None, :], lane[None, None, :], 0), axis=2, dtype=jnp.int32
    )
    spread_at = slot % LANES
    spread_later = slot // LANES

    speeds = linear_exchange_speeds.reshape(n, held, n, held)
    precon = newton_preconditioner.reshape(n, held, n, held)
    speeds = relative(relative(speeds, me, n, 0), me, n, 2).reshape(tracers, tracers)
    precon = relative(relative(precon, me, n, 0), me, n, 2).reshape(tracers, tracers)
    rates = relative(absorption_speed.reshape(n, held), me, n, 0).reshape(tracers)
    row = jnp.arange(tracers * ROWS, dtype=jnp.int32)
    copy = (row[:, None] // ROWS == jnp.arange(tracers)[None, :]).astype(jnp.float32)
    same = row[:, None] % ROWS == row[None, :] % ROWS

    def widened(x):
        x = jnp.dot(copy, x, precision=lax.Precision.HIGHEST)
        x = jnp.dot(x, copy.T, precision=lax.Precision.HIGHEST)
        return halves_of(jnp.where(same, x, 0.0))

    speeds = widened(speeds)
    precon = widened(precon)
    rates = jnp.dot(
        copy, jnp.broadcast_to(rates[:, None], (tracers, lat)), precision=lax.Precision.HIGHEST
    )

    fields = (east, north, kmix, water, speeds, precon, rates, gather)
    edges = {}
    for q in range(parts):
        level, turn = {0: (0, 1), parts - 1: (nl - 1, n - 1)}.get(q, (None, 0))
        edges[q] = list(chunk_edges(blocks[q], level, turn))
        edges[q][0] = around(edges[q][0], "col", -1)
        edges[q][1] = around(edges[q][1], "col", 1)
    if parts == 1:
        edges[0].append(jnp.concatenate([b[:, -1:] for b in blocks[0][-1:] + blocks[0][:-1]], 0))
    above_all = shifted(edges[0][2], "sec", -1)
    below_all = shifted(edges[parts - 1][-1], "sec", 1)

    pigments = {}
    returned = {}
    for q in order:
        below = (blocks[q - 1], nl - 1) if q > 0 else (below_all, 0)
        above = (blocks[q + 1], 0) if q < parts - 1 else (above_all, 0)
        *packed, pigments[q] = react_chunk(
            q, nl, me_at, tiles, shifts, blocks[q], below, above, edges[q][:2], fields, cap
        )
        returned[q] = []
        for d, x in enumerate(packed):
            returned[q].append(around(x, "sec", -d) if d else x)

    pigment = jnp.concatenate([pigments[q] for q in range(parts)], axis=0)
    square = pigment * pigment
    absorb = WATER_ABSORB + PIGMENT_ABSORB * square / (1.0 + square)
    depth_here = jnp.cumsum(absorb, axis=0)
    total = depth_here[-1]
    over = 0.0
    for d in range(1, n):
        over = over + shifted(total, "sec", d)
    depth_to = over[None] + depth_here
    warming = shortwave * (jnp.exp(-(depth_to - absorb)) - jnp.exp(-depth_to))
    thermal_revised = thermal_carried + CHLOROPHYLL_WARM * water * warming

    solute_revised = None
    for q in order:
        solute_revised = unpack_chunk(
            q, parts, me_at, tiles, returned[q], solute_fields, water, spread_at, spread_later,
            solute_revised,
        )
    return thermal_revised, jnp.stack([east, north]), spreading, solute_revised


def solution(mesh):
    placed = (
        P("sec", "col", None),
        P(None, "sec", "col", None),
        P("sec", "col", None),
        P("sec", None, "col", None),
        P(),
        P(),
        P(),
        P("col", None),
    )
    return jax.shard_map(
        on_device,
        mesh=mesh,
        in_specs=placed,
        out_specs=(
            P("sec", "col", None),
            P(None, "sec", "col", None),
            P("sec", "col", None),
            P("sec", None, "col", None),
        ),
        check_vma=False,
    )
```

profile of v0, /device:TPU:0, one launch (start us, length us, event | category | flops | bytes accessed | tf_op | source)
XLA Modules:
  0.0 466.5 jit_solution(9590540989842811273)
XLA Ops:
  10.9 4.7 collective-permute-start.8
  39.5 12.9 %collective-permute-done.12.refs_4_.refs_23_.refs_7_ = f32[4,4,16,256]{3,2,1,0:T(8,128)} collective-permute-done((f32[4,4,16,256]{3,2,1,0:T(8,128)S(1)}, f32[4,4,16,256]{3,2,1,0:T(8,128)}, u32[]{:S(2)}, u32[]{:S(2)}) %collective-permute-start.12) | collective-permute-done | bytes 262176 | tf_op jit(solution)/shard_map/ppermute | solution.py:31
  56.0 20.4 %collective-permute-start.3 = (f32[4,4,16,256]{3,2,1,0:T(8,128)}, f32[4,4,16,256]{3,2,1,0:T(8,128)S(1)}, u32[]{:S(2)}, u32[]{:S(2)}) collective-permute-start(f32[4,4,16,256]{3,2,1,0:T(8,128)} %get-tuple-element.129), channel_id=1, source_target_pairs={{0,2},{1,3},{2,4},{3,5},{4,6},{5,7},{6,0},{7,1},{8,10},{9,11},{10,... | collective-permute-start | bytes 786440 | tf_op jit(solution)/shard_map/ppermute | solution.py:31
  76.4 8.1 %collective-permute-start.23 = (f32[4,4,16,256]{3,2,1,0:T(8,128)S(1)}, f32[4,4,16,256]{3,2,1,0:T(8,128)S(1)}, u32[]{:S(2)}, u32[]{:S(2)}) collective-permute-start(f32[4,4,16,256]{3,2,1,0:T(8,128)S(1)} %get-tuple-element.100), channel_id=1, source_target_pairs={{0,7},{1,0},{2,1},{3,2},{4,3},{5,4},{6,5},{7,6},{8,15},{9,8},{10,9... | collective-permute-start | bytes 786440 | tf_op jit(solution)/shard_map/ppermute | solution.py:31
  84.5 7.2 %collective-permute-done.5.refs_4_.refs_7_.refs_15_ = f32[4,4,16,256]{3,2,1,0:T(8,128)S(1)} collective-permute-done((f32[4,4,16,256]{3,2,1,0:T(8,128)S(1)}, f32[4,4,16,256]{3,2,1,0:T(8,128)S(1)}, u32[]{:S(2)}, u32[]{:S(2)}) %collective-permute-start.5) | collective-permute-done | bytes 262176 | tf_op jit(solution)/shard_map/ppermute | solution.py:31
  91.8 9.1 %collective-permute-done.4.refs_3_.refs_6_.refs_14_ = f32[4,4,16,256]{3,2,1,0:T(8,128)S(1)} collective-permute-done((f32[4,4,16,256]{3,2,1,0:T(8,128)}, f32[4,4,16,256]{3,2,1,0:T(8,128)S(1)}, u32[]{:S(2)}, u32[]{:S(2)}) %collective-permute-start.4) | collective-permute-done | bytes 262176 | tf_op jit(solution)/shard_map/ppermute | solution.py:31
  100.9 8.0 %collective-permute-start.32 = (f32[4,4,16,256]{3,2,1,0:T(8,128)}, f32[4,4,16,256]{3,2,1,0:T(8,128)}, u32[]{:S(2)}, u32[]{:S(2)}) collective-permute-start(f32[4,4,16,256]{3,2,1,0:T(8,128)} %get-tuple-element.103), channel_id=1, source_target_pairs={{0,5},{1,6},{2,7},{3,0},{4,1},{5,2},{6,3},{7,4},{8,13},{9,14},{10,... | collective-permute-start | bytes 786440 | tf_op jit(solution)/shard_map/ppermute | solution.py:31
  117.4 15.8 %collective-permute-start.20 = (f32[4,4,16,256]{3,2,1,0:T(8,128)}, f32[4,4,16,256]{3,2,1,0:T(8,128)}, u32[]{:S(2)}, u32[]{:S(2)}) collective-permute-start(f32[4,4,16,256]{3,2,1,0:T(8,128)} %get-tuple-element.111), channel_id=1, source_target_pairs={{0,4},{1,5},{2,6},{3,7},{4,0},{5,1},{6,2},{7,3},{8,12},{9,13},{10,... | collective-permute-start | bytes 786440 | tf_op jit(solution)/shard_map/ppermute | solution.py:31
  133.2 8.2 %collective-permute-done.31.refs_23_.refs_4_.refs_7_.refs_15_ = f32[4,4,16,256]{3,2,1,0:T(8,128)} collective-permute-done((f32[4,4,16,256]{3,2,1,0:T(8,128)}, f32[4,4,16,256]{3,2,1,0:T(8,128)}, u32[]{:S(2)}, u32[]{:S(2)}) %collective-permute-start.31) | collective-permute-done | bytes 262176 | tf_op jit(solution)/shard_map/ppermute | solution.py:31
  141.4 9.3 %collective-permute-start.19 = (f32[4,4,16,256]{3,2,1,0:T(8,128)}, f32[4,4,16,256]{3,2,1,0:T(8,128)}, u32[]{:S(2)}, u32[]{:S(2)}) collective-permute-start(f32[4,4,16,256]{3,2,1,0:T(8,128)} %get-tuple-element.112), channel_id=1, source_target_pairs={{0,3},{1,4},{2,5},{3,6},{4,7},{5,0},{6,1},{7,2},{8,11},{9,12},{10,... | collective-permute-start | bytes 786440 | tf_op jit(solution)/shard_map/ppermute | solution.py:31
  150.7 8.7 %collective-permute-start.18 = (f32[4,4,16,256]{3,2,1,0:T(8,128)}, f32[4,4,16,256]{3,2,1,0:T(8,128)}, u32[]{:S(2)}, u32[]{:S(2)}) collective-permute-start(f32[4,4,16,256]{3,2,1,0:T(8,128)} %get-tuple-element.113), channel_id=1, source_target_pairs={{0,2},{1,3},{2,4},{3,5},{4,6},{5,7},{6,0},{7,1},{8,10},{9,11},{10,... | collective-permute-start | bytes 786440 | tf_op jit(solution)/shard_map/ppermute | solution.py:31
  160.9 13.9 %collective-permute-start.9 = (f32[4,4,16,256]{3,2,1,0:T(8,128)}, f32[4,4,16,256]{3,2,1,0:T(8,128)}, u32[]{:S(2)}, u32[]{:S(2)}) collective-permute-start(f32[4,4,16,256]{3,2,1,0:T(8,128)} %get-tuple-element.123), channel_id=1, source_target_pairs={{0,1},{1,2},{2,3},{3,4},{4,5},{5,6},{6,7},{7,0},{8,9},{9,10},{10,1... | collective-permute-start | bytes 786440 | tf_op jit(solution)/shard_map/ppermute | solution.py:31
  174.8 5.9 %collective-permute-done.20.refs_23_.refs_4_.refs_7_.refs_15_ = f32[4,4,16,256]{3,2,1,0:T(8,128)} collective-permute-done((f32[4,4,16,256]{3,2,1,0:T(8,128)}, f32[4,4,16,256]{3,2,1,0:T(8,128)}, u32[]{:S(2)}, u32[]{:S(2)}) %collective-permute-start.20) | collective-permute-done | bytes 262176 | tf_op jit(solution)/shard_map/ppermute | solution.py:31
  181.1 5.2 %collective-permute-done.19.refs_22_.refs_3_.refs_6_.refs_14_ = f32[4,4,16,256]{3,2,1,0:T(8,128)} collective-permute-done((f32[4,4,16,256]{3,2,1,0:T(8,128)}, f32[4,4,16,256]{3,2,1,0:T(8,128)}, u32[]{:S(2)}, u32[]{:S(2)}) %collective-permute-start.19) | collective-permute-done | bytes 262176 | tf_op jit(solution)/shard_map/ppermute | solution.py:31
  216.1 19.4 %react.5 = (f32[16,3072]{1,0:T(8,128)}, f32[16,3072]{1,0:T(8,128)}, f32[16,3072]{1,0:T(8,128)}, f32[16,3072]{1,0:T(8,128)}, f32[16,3072]{1,0:T(8,128)}, /*index=...) custom-call(s32[1]{0:T(128)} %bitcast.2.refs_0_, s32[32]{0:T(128)} %and_select_fusion.3.refs_1_, ...), custom_call_target="tpu_custom_call" | custom-call | flops 3221225472 | bytes 6291456 | tf_op jit(solution)/shard_map/react/pallas_call | solution.py:228
  238.3 19.3 %react.6 = (f32[16,3072]{1,0:T(8,128)}, f32[16,3072]{1,0:T(8,128)}, f32[16,3072]{1,0:T(8,128)}, f32[16,3072]{1,0:T(8,128)}, f32[16,3072]{1,0:T(8,128)}, /*index=...) custom-call(s32[1]{0:T(128)} %bitcast.2.refs_0_, s32[32]{0:T(128)} %and_select_fusion.3.refs_1_, ...), custom_call_target="tpu_custom_call" | custom-call | flops 3221225472 | bytes 6291456 | tf_op jit(solution)/shard_map/react/pallas_call | solution.py:228
  261.3 19.3 %react.4 = (f32[16,3072]{1,0:T(8,128)}, f32[16,3072]{1,0:T(8,128)}, f32[16,3072]{1,0:T(8,128)}, f32[16,3072]{1,0:T(8,128)}, f32[16,3072]{1,0:T(8,128)}, /*index=...) custom-call(s32[1]{0:T(128)} %bitcast.2.refs_0_, s32[32]{0:T(128)} %and_select_fusion.3.refs_1_, ...), custom_call_target="tpu_custom_call" | custom-call | flops 3221225472 | bytes 6291456 | tf_op jit(solution)/shard_map/react/pallas_call | solution.py:228
  282.6 19.3 %react.7 = (f32[16,3072]{1,0:T(8,128)}, f32[16,3072]{1,0:T(8,128)}, f32[16,3072]{1,0:T(8,128)}, f32[16,3072]{1,0:T(8,128)}, f32[16,3072]{1,0:T(8,128)}, /*index=...) custom-call(s32[1]{0:T(128)} %bitcast.2.refs_0_, s32[32]{0:T(128)} %and_select_fusion.3.refs_1_, ...), custom_call_target="tpu_custom_call" | custom-call | flops 3221225472 | bytes 6291456 | tf_op jit(solution)/shard_map/react/pallas_call | solution.py:228
  310.2 15.5 %collective-permute-done.73.refs_6_ = f32[16,3072]{1,0:T(8,128)S(1)} collective-permute-done((f32[16,3072]{1,0:T(8,128)}, f32[16,3072]{1,0:T(8,128)S(1)}, u32[]{:S(2)}, u32[]{:S(2)}) %collective-permute-start.73) | collective-permute-done | bytes 196640 | tf_op jit(solution)/shard_map/ppermute | solution.py:31
  327.6 10.1 %collective-permute-start.66 = (f32[16,3072]{1,0:T(8,128)}, f32[16,3072]{1,0:T(8,128)S(1)}, u32[]{:S(2)}, u32[]{:S(2)}) collective-permute-start(f32[16,3072]{1,0:T(8,128)} %get-tuple-element.84), channel_id=1, source_target_pairs={{0,4},{1,5},{2,6},{3,7},{4,0},{5,1},{6,2},{7,3},{8,12},{9,13},{10,... | collective-permute-start | bytes 589832 | tf_op jit(solution)/shard_map/ppermute | solution.py:31
  340.4 6.6 %collective-permute-start.69 = (f32[16,3072]{1,0:T(8,128)}, f32[16,3072]{1,0:T(8,128)S(1)}, u32[]{:S(2)}, u32[]{:S(2)}) collective-permute-start(f32[16,3072]{1,0:T(8,128)} %get-tuple-element.87), channel_id=1, source_target_pairs={{0,1},{1,2},{2,3},{3,4},{4,5},{5,6},{6,7},{7,0},{8,9},{9,10},{10,1... | collective-permute-start | bytes 589832 | tf_op jit(solution)/shard_map/ppermute | solution.py:31
  347.0 5.0 %collective-permute-start.48 = (f32[16,256]{1,0:T(8,128)}, f32[16,256]{1,0:T(8,128)S(1)}, u32[]{:S(2)}, u32[]{:S(2)}) collective-permute-start(f32[16,256]{1,0:T(8,128)} %slice_bitcast_fusion), channel_id=1, source_target_pairs={{0,7},{8,15},{16,23},{24,31}} | collective-permute-start | bytes 49160 | tf_op jit(solution)/shard_map/ppermute | solution.py:26
  352.0 6.6 %collective-permute-done.66.refs_6_ = f32[16,3072]{1,0:T(8,128)S(1)} collective-permute-done((f32[16,3072]{1,0:T(8,128)}, f32[16,3072]{1,0:T(8,128)S(1)}, u32[]{:S(2)}, u32[]{:S(2)}) %collective-permute-start.66) | collective-permute-done | bytes 196640 | tf_op jit(solution)/shard_map/ppermute | solution.py:31
  371.3 8.4 %collective-permute-done.44 = f32[16,256]{1,0:T(8,128)S(1)} collective-permute-done((f32[16,256]{1,0:T(8,128)}, f32[16,256]{1,0:T(8,128)S(1)}, u32[]{:S(2)}, u32[]{:S(2)}) %collective-permute-start.44) | collective-permute-done | bytes 16416 | tf_op jit(solution)/shard_map/ppermute | solution.py:26
  379.7 9.8 %collective-permute-start.43 = (f32[16,256]{1,0:T(8,128)}, f32[16,256]{1,0:T(8,128)S(1)}, u32[]{:S(2)}, u32[]{:S(2)}) collective-permute-start(f32[16,256]{1,0:T(8,128)} %slice_bitcast_fusion), channel_id=1, source_target_pairs={{0,2},{1,3},{2,4},{3,5},{4,6},{5,7},{8,10},{9,11},{10,12},{11,13},... | collective-permute-start | bytes 49160 | tf_op jit(solution)/shard_map/ppermute | solution.py:26
  389.5 8.2 %unpack.4.refs_14_ = f32[4,128,16,256]{3,2,1,0:T(8,128)} custom-call(s32[1]{0:T(128)} %bitcast.2.refs_0_, s32[32]{0:T(128)} %and_select_fusion.3.refs_1_, f32[16,3072]{1,0:T(8,128)} %get-tuple-element.88.refs_2_, f32[16,3072]{1,0:T(8,128)} %copy-done.23, f32[16,3072]{1,0:T(8,128)} %copy-done.24, f32[16,3072]{1,0:T(8,128)} %copy-done.25, ...), custom_call_target="tpu_custom_call" | custom-call | flops 209715200 | bytes 6291456 | tf_op jit(solution)/shard_map/unpack/pallas_call | solution.py:314
  399.2 8.4 %unpack.5.refs_14_ = f32[4,128,16,256]{3,2,1,0:T(8,128)} custom-call(s32[1]{0:T(128)} %bitcast.2.refs_0_, s32[32]{0:T(128)} %and_select_fusion.3.refs_1_, f32[16,3072]{1,0:T(8,128)} %get-tuple-element.80.refs_2_, f32[16,3072]{1,0:T(8,128)} %copy-done.30, f32[16,3072]{1,0:T(8,128)} %copy-done.32, ...), custom_call_target="tpu_custom_call", output_to_operand_aliasing={{}: (14, {})} | custom-call | flops 209715200 | bytes 6291456 | tf_op jit(solution)/shard_map/unpack/pallas_call | solution.py:314
  416.3 6.4 %collective-permute-done.60.refs_7_ = f32[16,3072]{1,0:T(8,128)S(1)} collective-permute-done((f32[16,3072]{1,0:T(8,128)}, f32[16,3072]{1,0:T(8,128)S(1)}, u32[]{:S(2)}, u32[]{:S(2)}) %collective-permute-start.60) | collective-permute-done | bytes 196640 | tf_op jit(solution)/shard_map/ppermute | solution.py:31
  426.6 13.0 %collective-permute-start.53 = (f32[16,3072]{1,0:T(8,128)}, f32[16,3072]{1,0:T(8,128)}, u32[]{:S(2)}, u32[]{:S(2)}) collective-permute-start(f32[16,3072]{1,0:T(8,128)} %get-tuple-element.69), channel_id=1, source_target_pairs={{0,3},{1,4},{2,5},{3,6},{4,7},{5,0},{6,1},{7,2},{8,11},{9,12},{10,... | collective-permute-start | bytes 589832 | tf_op jit(solution)/shard_map/ppermute | solution.py:31
  443.7 8.2 %unpack.6.refs_14_ = f32[4,128,16,256]{3,2,1,0:T(8,128)} custom-call(s32[1]{0:T(128)} %bitcast.2.refs_0_, s32[32]{0:T(128)} %and_select_fusion.3.refs_1_, f32[16,3072]{1,0:T(8,128)} %get-tuple-element.72.refs_2_, f32[16,3072]{1,0:T(8,128)} %copy-done.26, f32[16,3072]{1,0:T(8,128)} %collective-permute-done.57.refs_4_, ...), custom_call_target="tpu_custom_call", output_to_operand_aliasing={{}: (14, {})} | custom-call | flops 209715200 | bytes 6291456 | tf_op jit(solution)/shard_map/unpack/pallas_call | solution.py:314
  451.9 6.1 %collective-permute-done.52.refs_6_ = f32[16,3072]{1,0:T(8,128)} collective-permute-done((f32[16,3072]{1,0:T(8,128)}, f32[16,3072]{1,0:T(8,128)}, u32[]{:S(2)}, u32[]{:S(2)}) %collective-permute-start.52) | collective-permute-done | bytes 196640 | tf_op jit(solution)/shard_map/ppermute | solution.py:31
  458.2 8.2 %unpack.7 = f32[4,128,16,256]{3,2,1,0:T(8,128)} custom-call(s32[1]{0:T(128)} %bitcast.2.refs_0_, s32[32]{0:T(128)} %and_select_fusion.3.refs_1_, f32[16,3072]{1,0:T(8,128)} %get-tuple-element.64.refs_2_, f32[16,3072]{1,0:T(8,128)} %copy-done.36, f32[16,3072]{1,0:T(8,128)} %copy-done.39, ...), custom_call_target="tpu_custom_call", output_to_operand_aliasing={{}: (14, {})} | custom-call | flops 209715200 | bytes 6291456 | tf_op jit(solution)/shard_map/unpack/pallas_call | solution.py:314
  (367 shorter events, 129.3 us)
Async XLA Ops:
  2.1 32.1 %collective-permute-start.27 = (f32[2,1,16,256]{3,2,1,0:T(8,128)}, f32[2,1,16,256]{3,2,1,0:T(8,128)}, u32[]{:S(2)}, u32[]{:S(2)}) collective-permute-start(f32[2,1,16,256]{3,2,1,0:T(8,128)} %get-tuple-element.137), channel_id=1, source_target_pairs={{1,0},{2,1},{3,2},{4,3},{5,4},{6,5},{7,6},{9,8},{10,9},{11,10},{12... | collective-permute-start | bytes 98312 | tf_op jit(solution)/shard_map/ppermute | solution.py:26
  4.1 31.6 %collective-permute-start.26 = (f32[3,1,16,256]{3,2,1,0:T(8,128)S(1)}, f32[3,1,16,256]{3,2,1,0:T(8,128)S(1)}, u32[]{:S(2)}, u32[]{:S(2)}) collective-permute-start(f32[3,1,16,256]{3,2,1,0:T(8,128)S(1)} %pad_maximum_fusion.8), channel_id=1, source_target_pairs={{0,1},{1,2},{2,3},{3,4},{4,5},{5,6},{6,7},{8,9},{9,10},{10,11},{11... | collective-permute-start | bytes 147464 | tf_op jit(solution)/shard_map/ppermute | solution.py:26
  15.8 36.7 %collective-permute-start.12 = (f32[4,4,16,256]{3,2,1,0:T(8,128)S(1)}, f32[4,4,16,256]{3,2,1,0:T(8,128)}, u32[]{:S(2)}, u32[]{:S(2)}) collective-permute-start(f32[4,4,16,256]{3,2,1,0:T(8,128)S(1)} %get-tuple-element.120), channel_id=1, source_target_pairs={{0,4},{1,5},{2,6},{3,7},{4,0},{5,1},{6,2},{7,3},{8,12},{9,13},{10,... | collective-permute-start | bytes 786440 | tf_op jit(solution)/shard_map/ppermute | solution.py:31
  38.2 38.2 %collective-permute-start.7 = (f32[4,4,16,256]{3,2,1,0:T(8,128)}, f32[4,4,16,256]{3,2,1,0:T(8,128)S(1)}, u32[]{:S(2)}, u32[]{:S(2)}) collective-permute-start(f32[4,4,16,256]{3,2,1,0:T(8,128)} %get-tuple-element.125), channel_id=1, source_target_pairs={{0,6},{1,7},{2,0},{3,1},{4,2},{5,3},{6,4},{7,5},{8,14},{9,15},{10,... | collective-permute-start | bytes 786440 | tf_op jit(solution)/shard_map/ppermute | solution.py:31
  39.5 36.8 %collective-permute-start.6 = (f32[4,4,16,256]{3,2,1,0:T(8,128)S(1)}, f32[4,4,16,256]{3,2,1,0:T(8,128)S(1)}, u32[]{:S(2)}, u32[]{:S(2)}) collective-permute-start(f32[4,4,16,256]{3,2,1,0:T(8,128)S(1)} %get-tuple-element.126), channel_id=1, source_target_pairs={{0,5},{1,6},{2,7},{3,0},{4,1},{5,2},{6,3},{7,4},{8,13},{9,14},{10,... | collective-permute-start | bytes 786440 | tf_op jit(solution)/shard_map/ppermute | solution.py:31
  52.5 39.2 %collective-permute-start.5 = (f32[4,4,16,256]{3,2,1,0:T(8,128)S(1)}, f32[4,4,16,256]{3,2,1,0:T(8,128)S(1)}, u32[]{:S(2)}, u32[]{:S(2)}) collective-permute-start(f32[4,4,16,256]{3,2,1,0:T(8,128)S(1)} %get-tuple-element.127), channel_id=1, source_target_pairs={{0,4},{1,5},{2,6},{3,7},{4,0},{5,1},{6,2},{7,3},{8,12},{9,13},{10,... | collective-permute-start | bytes 786440 | tf_op jit(solution)/shard_map/ppermute | solution.py:31
  56.0 44.9 %collective-permute-start.4 = (f32[4,4,16,256]{3,2,1,0:T(8,128)}, f32[4,4,16,256]{3,2,1,0:T(8,128)S(1)}, u32[]{:S(2)}, u32[]{:S(2)}) collective-permute-start(f32[4,4,16,256]{3,2,1,0:T(8,128)} %get-tuple-element.128), channel_id=1, source_target_pairs={{0,3},{1,4},{2,5},{3,6},{4,7},{5,0},{6,1},{7,2},{8,11},{9,12},{10,... | collective-permute-start | bytes 786440 | tf_op jit(solution)/shard_map/ppermute | solution.py:31
  56.0 44.9 %collective-permute-start.3 = (f32[4,4,16,256]{3,2,1,0:T(8,128)}, f32[4,4,16,256]{3,2,1,0:T(8,128)S(1)}, u32[]{:S(2)}, u32[]{:S(2)}) collective-permute-start(f32[4,4,16,256]{3,2,1,0:T(8,128)} %get-tuple-element.129), channel_id=1, source_target_pairs={{0,2},{1,3},{2,4},{3,5},{4,6},{5,7},{6,0},{7,1},{8,10},{9,11},{10,... | collective-permute-start | bytes 786440 | tf_op jit(solution)/shard_map/ppermute | solution.py:31
  76.4 32.5 %collective-permute-start.2 = (f32[4,4,16,256]{3,2,1,0:T(8,128)}, f32[4,4,16,256]{3,2,1,0:T(8,128)S(1)}, u32[]{:S(2)}, u32[]{:S(2)}) collective-permute-start(f32[4,4,16,256]{3,2,1,0:T(8,128)} %get-tuple-element.130), channel_id=1, source_target_pairs={{0,1},{1,2},{2,3},{3,4},{4,5},{5,6},{6,7},{7,0},{8,9},{9,10},{10,1... | collective-permute-start | bytes 786440 | tf_op jit(solution)/shard_map/ppermute | solution.py:31
  76.4 36.6 %collective-permute-start.23 = (f32[4,4,16,256]{3,2,1,0:T(8,128)S(1)}, f32[4,4,16,256]{3,2,1,0:T(8,128)S(1)}, u32[]{:S(2)}, u32[]{:S(2)}) collective-permute-start(f32[4,4,16,256]{3,2,1,0:T(8,128)S(1)} %get-tuple-element.100), channel_id=1, source_target_pairs={{0,7},{1,0},{2,1},{3,2},{4,3},{5,4},{6,5},{7,6},{8,15},{9,8},{10,9... | collective-permute-start | bytes 786440 | tf_op jit(solution)/shard_map/ppermute | solution.py:31
  108.9 32.5 %collective-permute-start.31 = (f32[4,4,16,256]{3,2,1,0:T(8,128)}, f32[4,4,16,256]{3,2,1,0:T(8,128)}, u32[]{:S(2)}, u32[]{:S(2)}) collective-permute-start(f32[4,4,16,256]{3,2,1,0:T(8,128)} %get-tuple-element.104), channel_id=1, source_target_pairs={{0,4},{1,5},{2,6},{3,7},{4,0},{5,1},{6,2},{7,3},{8,12},{9,13},{10,... | collective-permute-start | bytes 786440 | tf_op jit(solution)/shard_map/ppermute | solution.py:31
  113.0 37.7 %collective-permute-start.30 = (f32[4,4,16,256]{3,2,1,0:T(8,128)}, f32[4,4,16,256]{3,2,1,0:T(8,128)}, u32[]{:S(2)}, u32[]{:S(2)}) collective-permute-start(f32[4,4,16,256]{3,2,1,0:T(8,128)} %get-tuple-element.105), channel_id=1, source_target_pairs={{0,3},{1,4},{2,5},{3,6},{4,7},{5,0},{6,1},{7,2},{8,11},{9,12},{10,... | collective-permute-start | bytes 786440 | tf_op jit(solution)/shard_map/ppermute | solution.py:31
  114.4 45.1 %collective-permute-start.22 = (f32[4,4,16,256]{3,2,1,0:T(8,128)}, f32[4,4,16,256]{3,2,1,0:T(8,128)}, u32[]{:S(2)}, u32[]{:S(2)}) collective-permute-start(f32[4,4,16,256]{3,2,1,0:T(8,128)} %get-tuple-element.109), channel_id=1, source_target_pairs={{0,6},{1,7},{2,0},{3,1},{4,2},{5,3},{6,4},{7,5},{8,14},{9,15},{10,... | collective-permute-start | bytes 786440 | tf_op jit(solution)/shard_map/ppermute | solution.py:31
  116.9 44.0 %collective-permute-start.21 = (f32[4,4,16,256]{3,2,1,0:T(8,128)}, f32[4,4,16,256]{3,2,1,0:T(8,128)S(1)}, u32[]{:S(2)}, u32[]{:S(2)}) collective-permute-start(f32[4,4,16,256]{3,2,1,0:T(8,128)} %get-tuple-element.110), channel_id=1, source_target_pairs={{0,5},{1,6},{2,7},{3,0},{4,1},{5,2},{6,3},{7,4},{8,13},{9,14},{10,... | collective-permute-start | bytes 786440 | tf_op jit(solution)/shard_map/ppermute | solution.py:31
  117.4 63.3 %collective-permute-start.20 = (f32[4,4,16,256]{3,2,1,0:T(8,128)}, f32[4,4,16,256]{3,2,1,0:T(8,128)}, u32[]{:S(2)}, u32[]{:S(2)}) collective-permute-start(f32[4,4,16,256]{3,2,1,0:T(8,128)} %get-tuple-element.111), channel_id=1, source_target_pairs={{0,4},{1,5},{2,6},{3,7},{4,0},{5,1},{6,2},{7,3},{8,12},{9,13},{10,... | collective-permute-start | bytes 786440 | tf_op jit(solution)/shard_map/ppermute | solution.py:31
  141.4 44.9 %collective-permute-start.19 = (f32[4,4,16,256]{3,2,1,0:T(8,128)}, f32[4,4,16,256]{3,2,1,0:T(8,128)}, u32[]{:S(2)}, u32[]{:S(2)}) collective-permute-start(f32[4,4,16,256]{3,2,1,0:T(8,128)} %get-tuple-element.112), channel_id=1, source_target_pairs={{0,3},{1,4},{2,5},{3,6},{4,7},{5,0},{6,1},{7,2},{8,11},{9,12},{10,... | collective-permute-start | bytes 786440 | tf_op jit(solution)/shard_map/ppermute | solution.py:31
  150.7 35.5 %collective-permute-start.18 = (f32[4,4,16,256]{3,2,1,0:T(8,128)}, f32[4,4,16,256]{3,2,1,0:T(8,128)}, u32[]{:S(2)}, u32[]{:S(2)}) collective-permute-start(f32[4,4,16,256]{3,2,1,0:T(8,128)} %get-tuple-element.113), channel_id=1, source_target_pairs={{0,2},{1,3},{2,4},{3,5},{4,6},{5,7},{6,0},{7,1},{8,10},{9,11},{10,... | collective-permute-start | bytes 786440 | tf_op jit(solution)/shard_map/ppermute | solution.py:31
  160.9 45.5 %collective-permute-start.9 = (f32[4,4,16,256]{3,2,1,0:T(8,128)}, f32[4,4,16,256]{3,2,1,0:T(8,128)}, u32[]{:S(2)}, u32[]{:S(2)}) collective-permute-start(f32[4,4,16,256]{3,2,1,0:T(8,128)} %get-tuple-element.123), channel_id=1, source_target_pairs={{0,1},{1,2},{2,3},{3,4},{4,5},{5,6},{6,7},{7,0},{8,9},{9,10},{10,1... | collective-permute-start | bytes 786440 | tf_op jit(solution)/shard_map/ppermute | solution.py:31
  206.4 95.5 %collective-permute-start = (f32[16,1,256]{2,1,0:T(1,128)}, f32[16,1,256]{2,1,0:T(1,128)S(1)}, u32[]{:S(2)}, u32[]{:S(2)}) collective-permute-start(f32[16,1,256]{2,1,0:T(1,128)} %get-tuple-element.140), channel_id=1, source_target_pairs={{0,24},{8,0},{16,8},{24,16},{1,25},{9,1},{17,9},{25,17},{2,26},{10... | collective-permute-start | bytes 49160 | tf_op jit(solution)/shard_map/ppermute | solution.py:31
  207.8 49.8 %collective-permute-start.24 = (f32[128,256]{1,0:T(8,128)}, f32[128,256]{1,0:T(8,128)S(1)}, u32[]{:S(2)}, u32[]{:S(2)}) collective-permute-start(f32[128,256]{1,0:T(8,128)} %get-tuple-element.51), channel_id=1, source_target_pairs={{0,24},{8,0},{16,8},{24,16},{1,25},{9,1},{17,9},{25,17},{2,26},{10... | collective-permute-start | bytes 393224 | tf_op jit(solution)/shard_map/ppermute | solution.py:31
  214.0 46.7 %collective-permute-start.16 = (f32[32,1,16,256]{3,2,1,0:T(8,128)}, f32[32,1,16,256]{3,2,1,0:T(8,128)}, u32[]{:S(2)}, u32[]{:S(2)}) collective-permute-start(f32[32,1,16,256]{3,2,1,0:T(8,128)} %get-tuple-element.50), channel_id=1, source_target_pairs={{0,1},{1,2},{2,3},{3,4},{4,5},{5,6},{6,7},{8,9},{9,10},{10,11},{11... | collective-permute-start | bytes 1572872 | tf_op jit(solution)/shard_map/ppermute | solution.py:26
  237.0 43.9 %collective-permute-start.39 = (f32[32,1,16,256]{3,2,1,0:T(8,128)}, f32[32,1,16,256]{3,2,1,0:T(8,128)}, u32[]{:S(2)}, u32[]{:S(2)}) collective-permute-start(f32[32,1,16,256]{3,2,1,0:T(8,128)} %get-tuple-element.60), channel_id=1, source_target_pairs={{1,0},{2,1},{3,2},{4,3},{5,4},{6,5},{7,6},{9,8},{10,9},{11,10},{12... | collective-permute-start | bytes 1572872 | tf_op jit(solution)/shard_map/ppermute | solution.py:26
  257.7 46.5 %collective-permute-start.1 = (f32[16,1,256]{2,1,0:T(1,128)S(1)}, f32[16,1,256]{2,1,0:T(1,128)S(1)}, u32[]{:S(2)}, u32[]{:S(2)}) collective-permute-start(f32[16,1,256]{2,1,0:T(1,128)S(1)} %copy-done.54), channel_id=1, source_target_pairs={{0,8},{8,16},{16,24},{24,0},{1,9},{9,17},{17,25},{25,1},{2,10},{10... | collective-permute-start | bytes 49160 | tf_op jit(solution)/shard_map/ppermute | solution.py:31
  305.6 32.2 %collective-permute-start.76 = (f32[16,3072]{1,0:T(8,128)}, f32[16,3072]{1,0:T(8,128)S(1)}, u32[]{:S(2)}, u32[]{:S(2)}) collective-permute-start(f32[16,3072]{1,0:T(8,128)} %get-tuple-element.95), channel_id=1, source_target_pairs={{0,1},{1,2},{2,3},{3,4},{4,5},{5,6},{6,7},{7,0},{8,9},{9,10},{10,1... | collective-permute-start | bytes 589832 | tf_op jit(solution)/shard_map/ppermute | solution.py:31
  306.7 33.6 %collective-permute-start.63 = (f32[16,3072]{1,0:T(8,128)}, f32[16,3072]{1,0:T(8,128)S(1)}, u32[]{:S(2)}, u32[]{:S(2)}) collective-permute-start(f32[16,3072]{1,0:T(8,128)} %get-tuple-element.81), channel_id=1, source_target_pairs={{0,7},{1,0},{2,1},{3,2},{4,3},{5,4},{6,5},{7,6},{8,15},{9,8},{10,9... | collective-permute-start | bytes 589832 | tf_op jit(solution)/shard_map/ppermute | solution.py:31
  327.6 30.9 %collective-permute-start.66 = (f32[16,3072]{1,0:T(8,128)}, f32[16,3072]{1,0:T(8,128)S(1)}, u32[]{:S(2)}, u32[]{:S(2)}) collective-permute-start(f32[16,3072]{1,0:T(8,128)} %get-tuple-element.84), channel_id=1, source_target_pairs={{0,4},{1,5},{2,6},{3,7},{4,0},{5,1},{6,2},{7,3},{8,12},{9,13},{10,... | collective-permute-start | bytes 589832 | tf_op jit(solution)/shard_map/ppermute | solution.py:31
  363.1 46.8 %collective-permute-start.56 = (f32[16,3072]{1,0:T(8,128)}, f32[16,3072]{1,0:T(8,128)S(1)}, u32[]{:S(2)}, u32[]{:S(2)}) collective-permute-start(f32[16,3072]{1,0:T(8,128)} %get-tuple-element.73), channel_id=1, source_target_pairs={{0,7},{1,0},{2,1},{3,2},{4,3},{5,4},{6,5},{7,6},{8,15},{9,8},{10,9... | collective-permute-start | bytes 589832 | tf_op jit(solution)/shard_map/ppermute | solution.py:31
  363.2 47.2 %collective-permute-start.57 = (f32[16,3072]{1,0:T(8,128)}, f32[16,3072]{1,0:T(8,128)}, u32[]{:S(2)}, u32[]{:S(2)}) collective-permute-start(f32[16,3072]{1,0:T(8,128)} %get-tuple-element.74), channel_id=1, source_target_pairs={{0,6},{1,7},{2,0},{3,1},{4,2},{5,3},{6,4},{7,5},{8,14},{9,15},{10,... | collective-permute-start | bytes 589832 | tf_op jit(solution)/shard_map/ppermute | solution.py:31
  364.0 46.4 %collective-permute-start.58 = (f32[16,3072]{1,0:T(8,128)}, f32[16,3072]{1,0:T(8,128)}, u32[]{:S(2)}, u32[]{:S(2)}) collective-permute-start(f32[16,3072]{1,0:T(8,128)} %get-tuple-element.75), channel_id=1, source_target_pairs={{0,5},{1,6},{2,7},{3,0},{4,1},{5,2},{6,3},{7,4},{8,13},{9,14},{10,... | collective-permute-start | bytes 589832 | tf_op jit(solution)/shard_map/ppermute | solution.py:31
  364.1 49.8 %collective-permute-start.59 = (f32[16,3072]{1,0:T(8,128)}, f32[16,3072]{1,0:T(8,128)}, u32[]{:S(2)}, u32[]{:S(2)}) collective-permute-start(f32[16,3072]{1,0:T(8,128)} %get-tuple-element.76), channel_id=1, source_target_pairs={{0,4},{1,5},{2,6},{3,7},{4,0},{5,1},{6,2},{7,3},{8,12},{9,13},{10,... | collective-permute-start | bytes 589832 | tf_op jit(solution)/shard_map/ppermute | solution.py:31
  422.7 35.4 %collective-permute-start.52 = (f32[16,3072]{1,0:T(8,128)}, f32[16,3072]{1,0:T(8,128)}, u32[]{:S(2)}, u32[]{:S(2)}) collective-permute-start(f32[16,3072]{1,0:T(8,128)} %get-tuple-element.68), channel_id=1, source_target_pairs={{0,4},{1,5},{2,6},{3,7},{4,0},{5,1},{6,2},{7,3},{8,12},{9,13},{10,... | collective-permute-start | bytes 589832 | tf_op jit(solution)/shard_map/ppermute | solution.py:31
  426.6 31.7 %collective-permute-start.53 = (f32[16,3072]{1,0:T(8,128)}, f32[16,3072]{1,0:T(8,128)}, u32[]{:S(2)}, u32[]{:S(2)}) collective-permute-start(f32[16,3072]{1,0:T(8,128)} %get-tuple-element.69), channel_id=1, source_target_pairs={{0,3},{1,4},{2,5},{3,6},{4,7},{5,0},{6,1},{7,2},{8,11},{9,12},{10,... | collective-permute-start | bytes 589832 | tf_op jit(solution)/shard_map/ppermute | solution.py:31
  (126 other events, 3685.3 us)
where the time goes:
time: 468 us; the launch traced here: 466 us
  starting transfers between devices  207 us (44%)
  Pallas kernels  120 us (26%)
  waiting for transfers between devices  102 us (22%)
  local copies, waits for them, and re-layouts  16.6 us (4%)
  other arithmetic  14.3 us (3%)
    ppermute x66, starting transfers between devices, around(): lax.ppermute(block, axis, [(i, (i + distance) % count) for i in range(cou...  177 us
    ppermute x66, waiting for transfers between devices, around(): lax.ppermute(block, axis, [(i, (i + distance) % count) for i in range(cou...  93.8 us
    pallas_call x4, Pallas kernels, react_chunk(): pl.pallas_call(functools.partial(react_kernel, n, nl, q), grid_spec=pltpu...  77.2 us
    pallas_call x4, Pallas kernels, unpack_chunk(): pl.pallas_call(functools.partial(unpack_kernel, n, base is not None), gri...  33.1 us
    ppermute x11, starting transfers between devices, shifted(): return lax.ppermute(block, axis, route)  31 us
    pallas_call x4, Pallas kernels, chunk_edges(): pl.pallas_call(functools.partial(edges_kernel, n, level, turn), in_specs=...  9.75 us
  transfers between devices with their start and end apart: 77, of which 17 were waited for; matrix products, arithmetic and copies ran while one was open for 7% of the time, Pallas kernels for 24%

commit v1 on v0

--- a/solution.py
+++ b/solution.py
@@ -73,16 +73,17 @@
     )(*blocks)
 
 
-def react_kernel(n, nl, q, *refs):
+def react_kernel(n, nl, q, closing, *refs):
     me_ref, tile_ref, shift_ref = refs[:3]
     cur = refs[3 : 3 + n]
     below = refs[3 + n : 3 + 2 * n]
     above = refs[3 + 2 * n : 3 + 3 * n]
     rest = refs[3 + 3 * n :]
     east_halo, west_halo, east, north, kmix, water, speeds, precon, rates, pick = rest[:10]
-    outs = rest[10 : 10 + n]
-    pigment = rest[10 + n]
-    moved, done, packed = rest[11 + n :]
+    before = rest[10]
+    outs = rest[11 : 11 + n]
+    absorbs, total = rest[11 + n : 13 + n]
+    moved, done, packed = rest[13 + n :]
     held, _, across, lat = cur[0].shape
     tracers = n * held
     halves = across // ROWS
@@ -159,10 +160,17 @@
     lax.fori_loop(0, nl * halves, react, 0)
 
     me = me_ref[0]
-    for l in range(nl):
-        at = pl.multiple_of((me * (held * nl) + l) * across, ROWS)
-        for s in range(lat // LANES):
-            pigment[l, :, s * LANES : (s + 1) * LANES] = done[s, pl.ds(at, across), :]
+    for s in range(lat // LANES):
+        lanes = slice(s * LANES, (s + 1) * LANES)
+        column = before[:, lanes]
+        for l in range(nl):
+            at = pl.multiple_of((me * (held * nl) + l) * across, ROWS)
+            pigment = done[s, pl.ds(at, across), :]
+            square = pigment * pigment
+            absorb = WATER_ABSORB + PIGMENT_ABSORB * square / (1.0 + square)
+            absorbs[l, :, lanes] = absorb
+            column = column + absorb
+        total[:, lanes] = column
 
     lane = lax.broadcasted_iota(jnp.int32, (ROWS, LANES), 1)
     parts = lat // LANES
@@ -183,11 +191,17 @@
         return carry
 
     lax.fori_loop(0, across, pack, 0)
+    cap = outs[0].shape[1] - (across * lat // (held * nl) if closing else 0)
     for d in range(n):
-        outs[d][...] = packed[d * held * nl : (d + 1) * held * nl, : outs[d].shape[1]]
-
-
-def react_chunk(q, nl, me, tiles, shifts, blocks, below, above, halos, fields, cap):
+        outs[d][:, :cap] = packed[d * held * nl : (d + 1) * held * nl, :cap]
+        if closing:
+            for k in range(across // (held * nl)):
+                outs[d][:, cap + k * lat : cap + (k + 1) * lat] = total[
+                    k * held * nl : (k + 1) * held * nl, :
+                ]
+
+
+def react_chunk(q, nl, me, tiles, shifts, blocks, below, above, halos, fields, before, cap, closing):
     n = len(blocks)
     held, _, across, lat = blocks[0].shape
     east, north, kmix, water, speeds, precon, rates, pick = fields
@@ -218,15 +232,17 @@
     for x in (east, north):
         ins.append(x)
         specs.append(pl.BlockSpec((nl, across, lat), lambda i, *_: (q, 0, 0)))
-    for x in (kmix, water, speeds, precon, rates, pick):
+    for x in (kmix, water, speeds, precon, rates, pick, before):
         ins.append(x)
         specs.append(all_of(x))
-    out_block = jax.ShapeDtypeStruct((held * nl, cap), jnp.float32)
-    shapes = [out_block] * n + [jax.ShapeDtypeStruct((nl, across, lat), jnp.float32)]
+    wide = cap + (across * lat // (held * nl) if closing else 0)
+    shapes = [jax.ShapeDtypeStruct((held * nl, wide), jnp.float32)] * n
+    shapes.append(jax.ShapeDtypeStruct((nl, across, lat), jnp.float32))
+    shapes.append(jax.ShapeDtypeStruct((across, lat), jnp.float32))
     lanes = (cap // LANES + 2) * LANES
     flops = 2 * 12 * rows * rows * lat * nl * (across // ROWS)
     return pl.pallas_call(
-        functools.partial(react_kernel, n, nl, q),
+        functools.partial(react_kernel, n, nl, q, closing),
         grid_spec=pltpu.PrefetchScalarGridSpec(
             num_scalar_prefetch=3,
             grid=(1,),
@@ -248,19 +264,18 @@
     )(me, tiles, shifts, *ins)
 
 
-def unpack_kernel(n, has_base, *refs):
+def unpack_kernel(n, cap, has_base, *refs):
     _, tile_ref = refs[:2]
     received = refs[2 : 2 + n]
     solute, water, pick, second = refs[2 + n : 6 + n]
     out, slots, spread = refs[6 + n + has_base :]
     held, nl, across, lat = solute.shape
-    cap = received[0].shape[1]
     d = pl.program_id(0)
     for k in range(n):
 
         @pl.when(d == k)
         def _():
-            slots[:, :cap] = received[k][...]
+            slots[:, :cap] = received[k][:, :cap]
 
     parts = lat // LANES
     for x in range(across):
@@ -292,11 +307,10 @@
                 )
 
 
-def unpack_chunk(q, parts, me, tiles, received, solute, water, pick, second, base):
+def unpack_chunk(q, parts, me, tiles, received, solute, water, pick, second, base, cap):
     n = len(received)
     held, depth, across, lat = solute.shape
     nl = depth // n // parts
-    cap = received[0].shape[1]
 
     def all_of(x):
         return pl.BlockSpec(x.shape, lambda d, *_: (0,) * x.ndim)
@@ -312,7 +326,7 @@
         ins.append(base)
         specs.append(pl.BlockSpec(memory_space=pl.ANY))
     return pl.pallas_call(
-        functools.partial(unpack_kernel, n, base is not None),
+        functools.partial(unpack_kernel, n, cap, base is not None),
         grid_spec=pltpu.PrefetchScalarGridSpec(
             num_scalar_prefetch=2,
             grid=(n,),
@@ -347,7 +361,7 @@
     nl = max(levels // 4, ROWS // held)
     parts = levels // nl
     inner = list(range(1, parts - 1))
-    return nl, parts, inner + [q for q in range(parts) if q not in inner]
+    return nl, parts, inner + [q for q in (parts - 1, 0) if q not in inner][: parts - len(inner)]
 
 
 def on_device(
@@ -368,20 +382,25 @@
     nl, parts, order = plan(held, levels)
     me_at = jnp.reshape(me, (1,)).astype(jnp.int32)
 
+    blocks = {}
+    raw = solute_fields
+    for q in range(parts):
+        sends = []
+        for d in range(n):
+            to = lax.rem(me + d, n)
+            sends.append(lax.dynamic_slice_in_dim(raw, to * levels + q * nl, nl, 1))
+        if q == 0:
+            raw, *sends = lax.optimization_barrier((raw, *sends))
+        blocks[q] = sends[:1]
+        for d in range(1, n):
+            blocks[q].append(around(sends[d], "sec", d))
+
     flow_after = shifted(flow_vector[:, :1], "sec", -1)
     before = shifted(
         jnp.concatenate([flow_vector[:, -1:], vertical_spreading[None, -1:]], axis=0), "sec", 1
     )
     thermal_west = around(thermal_state[:, -1:], "col", 1)
     thermal_east = around(thermal_state[:, :1], "col", -1)
-
-    blocks = {}
-    for q in range(parts):
-        blocks[q] = []
-        for d in range(n):
-            to = lax.rem(me + d, n)
-            block = lax.dynamic_slice_in_dim(solute_fields, to * levels + q * nl, nl, 1)
-            blocks[q].append(around(block, "sec", d) if d else block)
 
     latitude = jnp.pi * (jnp.arange(lat).astype(jnp.float32) + 0.5) / lat - jnp.pi / 2
     rotation = CORIOLIS * jnp.sin(latitude)
@@ -461,27 +480,27 @@
     above_all = shifted(edges[0][2], "sec", -1)
     below_all = shifted(edges[parts - 1][-1], "sec", 1)
 
-    pigments = {}
+    absorbs = {}
     returned = {}
+    total = jnp.zeros((across, lat), jnp.float32)
     for q in order:
         below = (blocks[q - 1], nl - 1) if q > 0 else (below_all, 0)
         above = (blocks[q + 1], 0) if q < parts - 1 else (above_all, 0)
-        *packed, pigments[q] = react_chunk(
-            q, nl, me_at, tiles, shifts, blocks[q], below, above, edges[q][:2], fields, cap
+        *packed, absorbs[q], total = react_chunk(
+            q, nl, me_at, tiles, shifts, blocks[q], below, above, edges[q][:2], fields, total,
+            cap, q == order[-1],
         )
         returned[q] = []
         for d, x in enumerate(packed):
             returned[q].append(around(x, "sec", -d) if d else x)
 
-    pigment = jnp.concatenate([pigments[q] for q in range(parts)], axis=0)
-    square = pigment * pigment
-    absorb = WATER_ABSORB + PIGMENT_ABSORB * square / (1.0 + square)
-    depth_here = jnp.cumsum(absorb, axis=0)
-    total = depth_here[-1]
+    absorb = jnp.concatenate([absorbs[q] for q in range(parts)], axis=0)
     over = 0.0
     for d in range(1, n):
-        over = over + shifted(total, "sec", d)
-    depth_to = over[None] + depth_here
+        sums = returned[order[-1]][d][:, cap:]
+        sums = [sums[:, k : k + lat] for k in range(0, sums.shape[1], lat)]
+        over = over + jnp.where(lax.rem(me + d, n) < me, jnp.concatenate(sums, axis=0), 0.0)
+    depth_to = over[None] + jnp.cumsum(absorb, axis=0)
     warming = shortwave * (jnp.exp(-(depth_to - absorb)) - jnp.exp(-depth_to))
     thermal_revised = thermal_carried + CHLOROPHYLL_WARM * water * warming
 
@@ -489,7 +508,7 @@
     for q in order:
         solute_revised = unpack_chunk(
             q, parts, me_at, tiles, returned[q], solute_fields, water, spread_at, spread_later,
-            solute_revised,
+            solute_revised, cap,
         )
     return thermal_revised, jnp.stack([east, north]), spreading, solute_revised
 

time: 468 us -> 430 us (0.919)
  starting transfers between devices: 207 us -> 174 us
  waiting for transfers between devices: 102 us -> 93.5 us
  local copies, waits for them, and re-layouts: 16.6 us -> 23.1 us
    ppermute x66, starting transfers between devices: 177 us -> 151 us  [around(): lax.ppermute(block, axis, [(i, (i + distance) % count) for i in range(cou...]
    ppermute x11 -> x4, waiting for transfers between devices: 8.42 us -> 0.01 us  [shifted(): return lax.ppermute(block, axis, route)]
    ppermute x11 -> x4, starting transfers between devices: 31 us -> 22.8 us  [shifted(): return lax.ppermute(block, axis, route)]
    dynamic_slice x2 -> x3, local copies, waits for them, and re-layouts: 7.98 us -> 9.56 us  [on_device(): sends.append(lax.dynamic_slice_in_dim(raw, to * levels + q * nl, nl, 1))]
  transfers between devices with their start and end apart: 77 -> 70, of which waited for: 17 -> 9; matrix products, arithmetic and copies ran while one was open for 7% -> 8% of each run, Pallas kernels for 24% -> 28%
where the time goes in v1:
time: 430 us; the launch traced here: 429 us
  starting transfers between devices  174 us (40%)
  Pallas kernels  121 us (28%)
  waiting for transfers between devices  93.5 us (22%)
  local copies, waits for them, and re-layouts  23.1 us (5%)
  other arithmetic  12.9 us (3%)
    ppermute x66, starting transfers between devices, around(): lax.ppermute(block, axis, [(i, (i + distance) % count) for i in range(cou...  151 us
    ppermute x66, waiting for transfers between devices, around(): lax.ppermute(block, axis, [(i, (i + distance) % count) for i in range(cou...  93.5 us
    pallas_call x4, Pallas kernels, react_chunk(): pl.pallas_call(functools.partial(react_kernel, n, nl, q, closing), grid_s...  77.4 us
    pallas_call x4, Pallas kernels, unpack_chunk(): pl.pallas_call(functools.partial(unpack_kernel, n, cap, base is not None)...  33.4 us
    ppermute x4, starting transfers between devices, shifted(): return lax.ppermute(block, axis, route)  22.8 us
    pallas_call x4, Pallas kernels, chunk_edges(): pl.pallas_call(functools.partial(edges_kernel, n, level, turn), in_specs=...  9.78 us
    dynamic_slice x3, local copies, waits for them, and re-layouts, on_device(): sends.append(lax.dynamic_slice_in_dim(raw, to * levels + q * nl, nl, 1))  9.56 us
  transfers between devices with their start and end apart: 70, of which 9 were waited for; matrix products, arithmetic and copies ran while one was open for 8% of the time, Pallas kernels for 28%

profile of v1, /device:TPU:0, one launch (start us, length us, event | category | flops | bytes accessed | tf_op | source)
XLA Modules:
  0.0 428.6 jit_solution(7879004178456158388)
XLA Ops:
  3.4 3.0 collective-permute-start.26
  29.0 4.4 %constant_dynamic-slice_fusion = (f32[4,4,16,256]{3,2,1,0:T(8,128)S(1)}, f32[4,4,16,256]{3,2,1,0:T(8,128)S(1)}, f32[4,4,16,256]{3,2,1,0:T(8,128)}, f32[4,4,16,25...) fusion(f32[4,128,16,256]{3,2,1,0:T(8,128)} %refs_10_.7, ...), kind=kLoop, calls=%fused_computation.90 | loop fusion | bytes 9437256 | tf_op jit(solution)/shard_map/dynamic_slice | solution.py:391
  42.2 12.1 %collective-permute-done.5.refs_4_.refs_15_.refs_7_ = f32[4,4,16,256]{3,2,1,0:T(8,128)S(1)} collective-permute-done((f32[4,4,16,256]{3,2,1,0:T(8,128)S(1)}, f32[4,4,16,256]{3,2,1,0:T(8,128)S(1)}, u32[]{:S(2)}, u32[]{:S(2)}) %collective-permute-start.5) | collective-permute-done | bytes 262176 | tf_op jit(solution)/shard_map/ppermute | solution.py:31
  54.3 18.2 %collective-permute-start.34 = (f32[4,4,16,256]{3,2,1,0:T(8,128)S(1)}, f32[4,4,16,256]{3,2,1,0:T(8,128)S(1)}, u32[]{:S(2)}, u32[]{:S(2)}) collective-permute-start(f32[4,4,16,256]{3,2,1,0:T(8,128)S(1)} %get-tuple-element.124), channel_id=1, source_target_pairs={{0,7},{1,0},{2,1},{3,2},{4,3},{5,4},{6,5},{7,6},{8,15},{9,8},{10,9... | collective-permute-start | bytes 786440 | tf_op jit(solution)/shard_map/ppermute | solution.py:31
  73.2 4.8 %collective-permute-start.31 = (f32[4,4,16,256]{3,2,1,0:T(8,128)}, f32[4,4,16,256]{3,2,1,0:T(8,128)}, u32[]{:S(2)}, u32[]{:S(2)}) collective-permute-start(f32[4,4,16,256]{3,2,1,0:T(8,128)} %get-tuple-element.127), channel_id=1, source_target_pairs={{0,4},{1,5},{2,6},{3,7},{4,0},{5,1},{6,2},{7,3},{8,12},{9,13},{10,... | collective-permute-start | bytes 786440 | tf_op jit(solution)/shard_map/ppermute | solution.py:31
  78.0 22.0 %collective-permute-start.23 = (f32[4,4,16,256]{3,2,1,0:T(8,128)}, f32[4,4,16,256]{3,2,1,0:T(8,128)}, u32[]{:S(2)}, u32[]{:S(2)}) collective-permute-start(f32[4,4,16,256]{3,2,1,0:T(8,128)} %get-tuple-element.132), channel_id=1, source_target_pairs={{0,7},{1,0},{2,1},{3,2},{4,3},{5,4},{6,5},{7,6},{8,15},{9,8},{10,9... | collective-permute-start | bytes 786440 | tf_op jit(solution)/shard_map/ppermute | solution.py:31
  102.3 16.2 %collective-permute-done.31.refs_4_.refs_23_.refs_7_.refs_15_ = f32[4,4,16,256]{3,2,1,0:T(8,128)} collective-permute-done((f32[4,4,16,256]{3,2,1,0:T(8,128)}, f32[4,4,16,256]{3,2,1,0:T(8,128)}, u32[]{:S(2)}, u32[]{:S(2)}) %collective-permute-start.31) | collective-permute-done | bytes 262176 | tf_op jit(solution)/shard_map/ppermute | solution.py:31
  118.5 12.7 %collective-permute-start.19 = (f32[4,4,16,256]{3,2,1,0:T(8,128)}, f32[4,4,16,256]{3,2,1,0:T(8,128)}, u32[]{:S(2)}, u32[]{:S(2)}) collective-permute-start(f32[4,4,16,256]{3,2,1,0:T(8,128)} %get-tuple-element.136), channel_id=1, source_target_pairs={{0,3},{1,4},{2,5},{3,6},{4,7},{5,0},{6,1},{7,2},{8,11},{9,12},{10,... | collective-permute-start | bytes 786440 | tf_op jit(solution)/shard_map/ppermute | solution.py:31
  131.2 8.8 %collective-permute-start.18 = (f32[4,4,16,256]{3,2,1,0:T(8,128)}, f32[4,4,16,256]{3,2,1,0:T(8,128)}, u32[]{:S(2)}, u32[]{:S(2)}) collective-permute-start(f32[4,4,16,256]{3,2,1,0:T(8,128)} %get-tuple-element.137), channel_id=1, source_target_pairs={{0,2},{1,3},{2,4},{3,5},{4,6},{5,7},{6,0},{7,1},{8,10},{9,11},{10,... | collective-permute-start | bytes 786440 | tf_op jit(solution)/shard_map/ppermute | solution.py:31
  141.6 25.3 %collective-permute-done.20.refs_4_.refs_7_.refs_15_.refs_23_ = f32[4,4,16,256]{3,2,1,0:T(8,128)} collective-permute-done((f32[4,4,16,256]{3,2,1,0:T(8,128)}, f32[4,4,16,256]{3,2,1,0:T(8,128)}, u32[]{:S(2)}, u32[]{:S(2)}) %collective-permute-start.20) | collective-permute-done | bytes 262176 | tf_op jit(solution)/shard_map/ppermute | solution.py:31
  167.0 4.0 collective-permute-done.19.refs_3_.refs_6_.refs_14_.refs_22_
  174.2 11.3 %collective-permute-done.29.refs_2_.refs_21_.refs_5_.refs_13_ = f32[4,4,16,256]{3,2,1,0:T(8,128)} collective-permute-done((f32[4,4,16,256]{3,2,1,0:T(8,128)}, f32[4,4,16,256]{3,2,1,0:T(8,128)}, u32[]{:S(2)}, u32[]{:S(2)}) %collective-permute-start.29) | collective-permute-done | bytes 262176 | tf_op jit(solution)/shard_map/ppermute | solution.py:31
  194.0 3.1 collective-permute-start.15
  197.1 2.8 collective-permute-start.14
  203.1 19.3 %react.4 = (f32[16,3072]{1,0:T(8,128)}, f32[16,3072]{1,0:T(8,128)}, f32[16,3072]{1,0:T(8,128)}, f32[16,3072]{1,0:T(8,128)}, f32[16,3072]{1,0:T(8,128)}, /*index=...) custom-call(s32[1]{0:T(128)} %bitcast.2.refs_0_, ...), custom_call_target="tpu_custom_call" | custom-call | flops 3221225472 | bytes 6291456 | tf_op jit(solution)/shard_map/react/pallas_call | solution.py:244
  230.0 19.4 %react.5 = (f32[16,3072]{1,0:T(8,128)}, f32[16,3072]{1,0:T(8,128)}, f32[16,3072]{1,0:T(8,128)}, f32[16,3072]{1,0:T(8,128)}, f32[16,3072]{1,0:T(8,128)}, /*index=...) custom-call(s32[1]{0:T(128)} %bitcast.2.refs_0_, ...), custom_call_target="tpu_custom_call" | custom-call | flops 3221225472 | bytes 6291456 | tf_op jit(solution)/shard_map/react/pallas_call | solution.py:244
  250.7 2.7 collective-permute-start.68
  257.9 14.6 %collective-permute-done.68.refs_8_ = f32[16,3072]{1,0:T(8,128)S(1)} collective-permute-done((f32[16,3072]{1,0:T(8,128)}, f32[16,3072]{1,0:T(8,128)S(1)}, u32[]{:S(2)}, u32[]{:S(2)}) %collective-permute-start.68) | collective-permute-done | bytes 196640 | tf_op jit(solution)/shard_map/ppermute | solution.py:31
  279.2 17.2 %collective-permute-start.16 = (f32[32,1,16,256]{3,2,1,0:T(8,128)}, f32[32,1,16,256]{3,2,1,0:T(8,128)}, u32[]{:S(2)}, u32[]{:S(2)}) collective-permute-start(f32[32,1,16,256]{3,2,1,0:T(8,128)} %get-tuple-element.71), channel_id=1, source_target_pairs={{0,1},{1,2},{2,3},{3,4},{4,5},{5,6},{6,7},{8,9},{9,10},{10,11},{11... | collective-permute-start | bytes 1572872 | tf_op jit(solution)/shard_map/ppermute | solution.py:26
  299.0 2.9 collective-permute-start.36
  302.0 8.4 %unpack.4.refs_14_ = f32[4,128,16,256]{3,2,1,0:T(8,128)} custom-call(s32[1]{0:T(128)} %bitcast.2.refs_0_, s32[32]{0:T(128)} %and_select_fusion.3.refs_1_, f32[16,3072]{1,0:T(8,128)} %get-tuple-element.112.refs_2_, f32[16,3072]{1,0:T(8,128)} %copy-done.24, f32[16,3072]{1,0:T(8,128)} %copy-done.25, f32[16,3072]{1,0:T(8,128)} %collective-permute-done.65.refs_5_, ...), custom_call_target="tpu_custom_call" | custom-call | flops 209715200 | bytes 6291456 | tf_op jit(solution)/shard_map/unpack/pallas_call | solution.py:328
  310.4 3.0 collective-permute-start.24
  313.4 8.4 %unpack.5.refs_14_ = f32[4,128,16,256]{3,2,1,0:T(8,128)} custom-call(s32[1]{0:T(128)} %bitcast.2.refs_0_, s32[32]{0:T(128)} %and_select_fusion.3.refs_1_, f32[16,3072]{1,0:T(8,128)} %get-tuple-element.104.refs_2_, f32[16,3072]{1,0:T(8,128)} %copy-done.32, f32[16,3072]{1,0:T(8,128)} %copy-done.34, ...), custom_call_target="tpu_custom_call", output_to_operand_aliasing={{}: (14, {})} | custom-call | flops 209715200 | bytes 6291456 | tf_op jit(solution)/shard_map/unpack/pallas_call | solution.py:328
  322.8 19.3 %react.6 = (f32[16,3072]{1,0:T(8,128)}, f32[16,3072]{1,0:T(8,128)}, f32[16,3072]{1,0:T(8,128)}, f32[16,3072]{1,0:T(8,128)}, f32[16,3072]{1,0:T(8,128)}, /*index=...) custom-call(s32[1]{0:T(128)} %bitcast.2.refs_0_, ...), custom_call_target="tpu_custom_call" | custom-call | flops 3221225472 | bytes 6291456 | tf_op jit(solution)/shard_map/react/pallas_call | solution.py:244
  342.1 2.8 collective-permute-start.49
  347.6 19.5 %react.7 = (f32[16,3328]{1,0:T(8,128)}, f32[16,3328]{1,0:T(8,128)}, f32[16,3328]{1,0:T(8,128)}, f32[16,3328]{1,0:T(8,128)}, f32[16,3328]{1,0:T(8,128)}, /*index=...) custom-call(s32[1]{0:T(128)} %bitcast.2.refs_0_, ...), custom_call_target="tpu_custom_call" | custom-call | flops 3221225472 | bytes 6291456 | tf_op jit(solution)/shard_map/react/pallas_call | solution.py:244
  373.3 2.7 collective-permute-start.43
  376.7 3.3 collective-permute-start.44
  380.1 16.5 %collective-permute-start.45 = (f32[16,3328]{1,0:T(8,128)}, f32[16,3328]{1,0:T(8,128)S(1)}, u32[]{:S(2)}, u32[]{:S(2)}) collective-permute-start(f32[16,3328]{1,0:T(8,128)} %get-tuple-element.87), channel_id=1, source_target_pairs={{0,4},{1,5},{2,6},{3,7},{4,0},{5,1},{6,2},{7,3},{8,12},{9,13},{10,... | collective-permute-start | bytes 638984 | tf_op jit(solution)/shard_map/ppermute | solution.py:31
  398.9 8.2 %unpack.6.refs_14_ = f32[4,128,16,256]{3,2,1,0:T(8,128)} custom-call(s32[1]{0:T(128)} %bitcast.2.refs_0_, s32[32]{0:T(128)} %and_select_fusion.3.refs_1_, f32[16,3072]{1,0:T(8,128)} %get-tuple-element.96.refs_2_, f32[16,3072]{1,0:T(8,128)} %copy-done.26, f32[16,3072]{1,0:T(8,128)} %copy-done.27, ...), custom_call_target="tpu_custom_call", output_to_operand_aliasing={{}: (14, {})} | custom-call | flops 209715200 | bytes 6291456 | tf_op jit(solution)/shard_map/unpack/pallas_call | solution.py:328
  409.8 6.7 %collective-permute-done.45.refs_6_ = f32[16,3328]{1,0:T(8,128)S(1)} collective-permute-done((f32[16,3328]{1,0:T(8,128)}, f32[16,3328]{1,0:T(8,128)S(1)}, u32[]{:S(2)}, u32[]{:S(2)}) %collective-permute-start.45) | collective-permute-done | bytes 213024 | tf_op jit(solution)/shard_map/ppermute | solution.py:31
  419.1 8.4 %unpack.7 = f32[4,128,16,256]{3,2,1,0:T(8,128)} custom-call(s32[1]{0:T(128)} %bitcast.2.refs_0_, s32[32]{0:T(128)} %and_select_fusion.3.refs_1_, f32[16,3328]{1,0:T(8,128)} %get-tuple-element.95.refs_2_, f32[16,3328]{1,0:T(8,128)} %copy-done.19, f32[16,3328]{1,0:T(8,128)} %copy-done.20, f32[16,3328]{1,0:T(8,128)} %copy-done.21, ...), custom_call_target="tpu_custom_call", output_to_operand_aliasing={{}: (14, {})} | custom-call | flops 209715200 | bytes 6291456 | tf_op jit(solution)/shard_map/unpack/pallas_call | solution.py:328
  (308 shorter events, 94.7 us)
Async XLA Ops:
  1.4 34.4 %collective-permute-start.27 = (f32[2,1,16,256]{3,2,1,0:T(8,128)S(1)}, f32[2,1,16,256]{3,2,1,0:T(8,128)S(1)}, u32[]{:S(2)}, u32[]{:S(2)}) collective-permute-start(f32[2,1,16,256]{3,2,1,0:T(8,128)S(1)} %get-tuple-element.161), channel_id=1, source_target_pairs={{1,0},{2,1},{3,2},{4,3},{5,4},{6,5},{7,6},{9,8},{10,9},{11,10},{12... | collective-permute-start | bytes 98312 | tf_op jit(solution)/shard_map/ppermute | solution.py:26
  3.4 33.7 %collective-permute-start.26 = (f32[3,1,16,256]{3,2,1,0:T(8,128)S(1)}, f32[3,1,16,256]{3,2,1,0:T(8,128)S(1)}, u32[]{:S(2)}, u32[]{:S(2)}) collective-permute-start(f32[3,1,16,256]{3,2,1,0:T(8,128)S(1)} %pad_maximum_fusion.8), channel_id=1, source_target_pairs={{0,1},{1,2},{2,3},{3,4},{4,5},{5,6},{6,7},{8,9},{9,10},{10,11},{11... | collective-permute-start | bytes 147464 | tf_op jit(solution)/shard_map/ppermute | solution.py:26
  9.2 29.9 %collective-permute-start.2 = (f32[4,4,16,256]{3,2,1,0:T(8,128)}, f32[4,4,16,256]{3,2,1,0:T(8,128)}, u32[]{:S(2)}, u32[]{:S(2)}) collective-permute-start(f32[4,4,16,256]{3,2,1,0:T(8,128)} %get-tuple-element.63), channel_id=1, source_target_pairs={{0,1},{1,2},{2,3},{3,4},{4,5},{5,6},{6,7},{7,0},{8,9},{9,10},{10,1... | collective-permute-start | bytes 786440 | tf_op jit(solution)/shard_map/ppermute | solution.py:31
  11.9 29.8 %collective-permute-start.3 = (f32[4,4,16,256]{3,2,1,0:T(8,128)}, f32[4,4,16,256]{3,2,1,0:T(8,128)}, u32[]{:S(2)}, u32[]{:S(2)}) collective-permute-start(f32[4,4,16,256]{3,2,1,0:T(8,128)} %get-tuple-element.64), channel_id=1, source_target_pairs={{0,2},{1,3},{2,4},{3,5},{4,6},{5,7},{6,0},{7,1},{8,10},{9,11},{10,... | collective-permute-start | bytes 786440 | tf_op jit(solution)/shard_map/ppermute | solution.py:31
  13.5 28.5 %collective-permute-start.4 = (f32[4,4,16,256]{3,2,1,0:T(8,128)}, f32[4,4,16,256]{3,2,1,0:T(8,128)}, u32[]{:S(2)}, u32[]{:S(2)}) collective-permute-start(f32[4,4,16,256]{3,2,1,0:T(8,128)} %get-tuple-element.65), channel_id=1, source_target_pairs={{0,3},{1,4},{2,5},{3,6},{4,7},{5,0},{6,1},{7,2},{8,11},{9,12},{10,... | collective-permute-start | bytes 786440 | tf_op jit(solution)/shard_map/ppermute | solution.py:31
  37.1 35.4 %collective-permute-start.6 = (f32[4,4,16,256]{3,2,1,0:T(8,128)S(1)}, f32[4,4,16,256]{3,2,1,0:T(8,128)S(1)}, u32[]{:S(2)}, u32[]{:S(2)}) collective-permute-start(f32[4,4,16,256]{3,2,1,0:T(8,128)S(1)} %get-tuple-element.67), channel_id=1, source_target_pairs={{0,5},{1,6},{2,7},{3,0},{4,1},{5,2},{6,3},{7,4},{8,13},{9,14},{10,... | collective-permute-start | bytes 786440 | tf_op jit(solution)/shard_map/ppermute | solution.py:31
  39.1 33.9 %collective-permute-start.7 = (f32[4,4,16,256]{3,2,1,0:T(8,128)}, f32[4,4,16,256]{3,2,1,0:T(8,128)S(1)}, u32[]{:S(2)}, u32[]{:S(2)}) collective-permute-start(f32[4,4,16,256]{3,2,1,0:T(8,128)} %get-tuple-element.68), channel_id=1, source_target_pairs={{0,6},{1,7},{2,0},{3,1},{4,2},{5,3},{6,4},{7,5},{8,14},{9,15},{10,... | collective-permute-start | bytes 786440 | tf_op jit(solution)/shard_map/ppermute | solution.py:31
  41.7 31.4 %collective-permute-start.8 = (f32[4,4,16,256]{3,2,1,0:T(8,128)}, f32[4,4,16,256]{3,2,1,0:T(8,128)S(1)}, u32[]{:S(2)}, u32[]{:S(2)}) collective-permute-start(f32[4,4,16,256]{3,2,1,0:T(8,128)} %get-tuple-element.69), channel_id=1, source_target_pairs={{0,7},{1,0},{2,1},{3,2},{4,3},{5,4},{6,5},{7,6},{8,15},{9,8},{10,9... | collective-permute-start | bytes 786440 | tf_op jit(solution)/shard_map/ppermute | solution.py:31
  42.0 36.0 %collective-permute-start.13 = (f32[4,4,16,256]{3,2,1,0:T(8,128)S(1)}, f32[4,4,16,256]{3,2,1,0:T(8,128)S(1)}, u32[]{:S(2)}, u32[]{:S(2)}) collective-permute-start(f32[4,4,16,256]{3,2,1,0:T(8,128)S(1)} %get-tuple-element.142), channel_id=1, source_target_pairs={{0,5},{1,6},{2,7},{3,0},{4,1},{5,2},{6,3},{7,4},{8,13},{9,14},{10,... | collective-permute-start | bytes 786440 | tf_op jit(solution)/shard_map/ppermute | solution.py:31
  73.1 28.5 %collective-permute-start.32 = (f32[4,4,16,256]{3,2,1,0:T(8,128)}, f32[4,4,16,256]{3,2,1,0:T(8,128)}, u32[]{:S(2)}, u32[]{:S(2)}) collective-permute-start(f32[4,4,16,256]{3,2,1,0:T(8,128)} %get-tuple-element.126), channel_id=1, source_target_pairs={{0,5},{1,6},{2,7},{3,0},{4,1},{5,2},{6,3},{7,4},{8,13},{9,14},{10,... | collective-permute-start | bytes 786440 | tf_op jit(solution)/shard_map/ppermute | solution.py:31
  73.2 45.3 %collective-permute-start.31 = (f32[4,4,16,256]{3,2,1,0:T(8,128)}, f32[4,4,16,256]{3,2,1,0:T(8,128)}, u32[]{:S(2)}, u32[]{:S(2)}) collective-permute-start(f32[4,4,16,256]{3,2,1,0:T(8,128)} %get-tuple-element.127), channel_id=1, source_target_pairs={{0,4},{1,5},{2,6},{3,7},{4,0},{5,1},{6,2},{7,3},{8,12},{9,13},{10,... | collective-permute-start | bytes 786440 | tf_op jit(solution)/shard_map/ppermute | solution.py:31
  77.9 40.5 %collective-permute-start.30 = (f32[4,4,16,256]{3,2,1,0:T(8,128)}, f32[4,4,16,256]{3,2,1,0:T(8,128)}, u32[]{:S(2)}, u32[]{:S(2)}) collective-permute-start(f32[4,4,16,256]{3,2,1,0:T(8,128)} %get-tuple-element.128), channel_id=1, source_target_pairs={{0,3},{1,4},{2,5},{3,6},{4,7},{5,0},{6,1},{7,2},{8,11},{9,12},{10,... | collective-permute-start | bytes 786440 | tf_op jit(solution)/shard_map/ppermute | solution.py:31
  78.0 53.2 %collective-permute-start.23 = (f32[4,4,16,256]{3,2,1,0:T(8,128)}, f32[4,4,16,256]{3,2,1,0:T(8,128)}, u32[]{:S(2)}, u32[]{:S(2)}) collective-permute-start(f32[4,4,16,256]{3,2,1,0:T(8,128)} %get-tuple-element.132), channel_id=1, source_target_pairs={{0,7},{1,0},{2,1},{3,2},{4,3},{5,4},{6,5},{7,6},{8,15},{9,8},{10,9... | collective-permute-start | bytes 786440 | tf_op jit(solution)/shard_map/ppermute | solution.py:31
  100.0 40.0 %collective-permute-start.22 = (f32[4,4,16,256]{3,2,1,0:T(8,128)}, f32[4,4,16,256]{3,2,1,0:T(8,128)}, u32[]{:S(2)}, u32[]{:S(2)}) collective-permute-start(f32[4,4,16,256]{3,2,1,0:T(8,128)} %get-tuple-element.133), channel_id=1, source_target_pairs={{0,6},{1,7},{2,0},{3,1},{4,2},{5,3},{6,4},{7,5},{8,14},{9,15},{10,... | collective-permute-start | bytes 786440 | tf_op jit(solution)/shard_map/ppermute | solution.py:31
  101.6 39.1 %collective-permute-start.21 = (f32[4,4,16,256]{3,2,1,0:T(8,128)}, f32[4,4,16,256]{3,2,1,0:T(8,128)S(1)}, u32[]{:S(2)}, u32[]{:S(2)}) collective-permute-start(f32[4,4,16,256]{3,2,1,0:T(8,128)} %get-tuple-element.134), channel_id=1, source_target_pairs={{0,5},{1,6},{2,7},{3,0},{4,1},{5,2},{6,3},{7,4},{8,13},{9,14},{10,... | collective-permute-start | bytes 786440 | tf_op jit(solution)/shard_map/ppermute | solution.py:31
  118.5 48.5 %collective-permute-start.20 = (f32[4,4,16,256]{3,2,1,0:T(8,128)}, f32[4,4,16,256]{3,2,1,0:T(8,128)}, u32[]{:S(2)}, u32[]{:S(2)}) collective-permute-start(f32[4,4,16,256]{3,2,1,0:T(8,128)} %get-tuple-element.135), channel_id=1, source_target_pairs={{0,4},{1,5},{2,6},{3,7},{4,0},{5,1},{6,2},{7,3},{8,12},{9,13},{10,... | collective-permute-start | bytes 786440 | tf_op jit(solution)/shard_map/ppermute | solution.py:31
  118.5 52.4 %collective-permute-start.19 = (f32[4,4,16,256]{3,2,1,0:T(8,128)}, f32[4,4,16,256]{3,2,1,0:T(8,128)}, u32[]{:S(2)}, u32[]{:S(2)}) collective-permute-start(f32[4,4,16,256]{3,2,1,0:T(8,128)} %get-tuple-element.136), channel_id=1, source_target_pairs={{0,3},{1,4},{2,5},{3,6},{4,7},{5,0},{6,1},{7,2},{8,11},{9,12},{10,... | collective-permute-start | bytes 786440 | tf_op jit(solution)/shard_map/ppermute | solution.py:31
  131.2 39.7 %collective-permute-start.18 = (f32[4,4,16,256]{3,2,1,0:T(8,128)}, f32[4,4,16,256]{3,2,1,0:T(8,128)}, u32[]{:S(2)}, u32[]{:S(2)}) collective-permute-start(f32[4,4,16,256]{3,2,1,0:T(8,128)} %get-tuple-element.137), channel_id=1, source_target_pairs={{0,2},{1,3},{2,4},{3,5},{4,6},{5,7},{6,0},{7,1},{8,10},{9,11},{10,... | collective-permute-start | bytes 786440 | tf_op jit(solution)/shard_map/ppermute | solution.py:31
  140.0 31.0 %collective-permute-start.17 = (f32[4,4,16,256]{3,2,1,0:T(8,128)}, f32[4,4,16,256]{3,2,1,0:T(8,128)}, u32[]{:S(2)}, u32[]{:S(2)}) collective-permute-start(f32[4,4,16,256]{3,2,1,0:T(8,128)} %get-tuple-element.138), channel_id=1, source_target_pairs={{0,1},{1,2},{2,3},{3,4},{4,5},{5,6},{6,7},{7,0},{8,9},{9,10},{10,1... | collective-permute-start | bytes 786440 | tf_op jit(solution)/shard_map/ppermute | solution.py:31
  140.7 52.8 %collective-permute-start.12 = (f32[4,4,16,256]{3,2,1,0:T(8,128)}, f32[4,4,16,256]{3,2,1,0:T(8,128)}, u32[]{:S(2)}, u32[]{:S(2)}) collective-permute-start(f32[4,4,16,256]{3,2,1,0:T(8,128)} %get-tuple-element.143), channel_id=1, source_target_pairs={{0,4},{1,5},{2,6},{3,7},{4,0},{5,1},{6,2},{7,3},{8,12},{9,13},{10,... | collective-permute-start | bytes 786440 | tf_op jit(solution)/shard_map/ppermute | solution.py:31
  193.6 28.8 %collective-permute-start.9 = (f32[4,4,16,256]{3,2,1,0:T(8,128)}, f32[4,4,16,256]{3,2,1,0:T(8,128)S(1)}, u32[]{:S(2)}, u32[]{:S(2)}) collective-permute-start(f32[4,4,16,256]{3,2,1,0:T(8,128)} %get-tuple-element.146), channel_id=1, source_target_pairs={{0,1},{1,2},{2,3},{3,4},{4,5},{5,6},{6,7},{7,0},{8,9},{9,10},{10,1... | collective-permute-start | bytes 786440 | tf_op jit(solution)/shard_map/ppermute | solution.py:31
  194.0 31.1 %collective-permute-start.15 = (f32[4,4,16,256]{3,2,1,0:T(8,128)}, f32[4,4,16,256]{3,2,1,0:T(8,128)S(1)}, u32[]{:S(2)}, u32[]{:S(2)}) collective-permute-start(f32[4,4,16,256]{3,2,1,0:T(8,128)} %get-tuple-element.140), channel_id=1, source_target_pairs={{0,7},{1,0},{2,1},{3,2},{4,3},{5,4},{6,5},{7,6},{8,15},{9,8},{10,9... | collective-permute-start | bytes 786440 | tf_op jit(solution)/shard_map/ppermute | solution.py:31
  197.1 30.2 %collective-permute-start.14 = (f32[4,4,16,256]{3,2,1,0:T(8,128)}, f32[4,4,16,256]{3,2,1,0:T(8,128)S(1)}, u32[]{:S(2)}, u32[]{:S(2)}) collective-permute-start(f32[4,4,16,256]{3,2,1,0:T(8,128)} %get-tuple-element.141), channel_id=1, source_target_pairs={{0,6},{1,7},{2,0},{3,1},{4,2},{5,3},{6,4},{7,5},{8,14},{9,15},{10,... | collective-permute-start | bytes 786440 | tf_op jit(solution)/shard_map/ppermute | solution.py:31
  227.3 27.5 %collective-permute-start.66 = (f32[16,3072]{1,0:T(8,128)}, f32[16,3072]{1,0:T(8,128)}, u32[]{:S(2)}, u32[]{:S(2)}) collective-permute-start(f32[16,3072]{1,0:T(8,128)} %get-tuple-element.116), channel_id=1, source_target_pairs={{0,4},{1,5},{2,6},{3,7},{4,0},{5,1},{6,2},{7,3},{8,12},{9,13},{10,... | collective-permute-start | bytes 589832 | tf_op jit(solution)/shard_map/ppermute | solution.py:31
  249.4 72.7 %collective-permute-start.35 = (f32[32,1,16,256]{3,2,1,0:T(8,128)}, f32[32,1,16,256]{3,2,1,0:T(8,128)}, u32[]{:S(2)}, u32[]{:S(2)}) collective-permute-start(f32[32,1,16,256]{3,2,1,0:T(8,128)} %get-tuple-element.74), channel_id=1, source_target_pairs={{1,0},{2,1},{3,2},{4,3},{5,4},{6,5},{7,6},{9,8},{10,9},{11,10},{12... | collective-permute-start | bytes 1572872 | tf_op jit(solution)/shard_map/ppermute | solution.py:26
  274.4 27.5 %collective-permute-start.61 = (f32[16,3072]{1,0:T(8,128)}, f32[16,3072]{1,0:T(8,128)}, u32[]{:S(2)}, u32[]{:S(2)}) collective-permute-start(f32[16,3072]{1,0:T(8,128)} %get-tuple-element.110), channel_id=1, source_target_pairs={{0,2},{1,3},{2,4},{3,5},{4,6},{5,7},{6,0},{7,1},{8,10},{9,11},{10,... | collective-permute-start | bytes 589832 | tf_op jit(solution)/shard_map/ppermute | solution.py:31
  279.2 68.4 %collective-permute-start.16 = (f32[32,1,16,256]{3,2,1,0:T(8,128)}, f32[32,1,16,256]{3,2,1,0:T(8,128)}, u32[]{:S(2)}, u32[]{:S(2)}) collective-permute-start(f32[32,1,16,256]{3,2,1,0:T(8,128)} %get-tuple-element.71), channel_id=1, source_target_pairs={{0,1},{1,2},{2,3},{3,4},{4,5},{5,6},{6,7},{8,9},{9,10},{10,11},{11... | collective-permute-start | bytes 1572872 | tf_op jit(solution)/shard_map/ppermute | solution.py:26
  310.4 34.4 %collective-permute-start.24 = (f32[128,256]{1,0:T(8,128)S(1)}, f32[128,256]{1,0:T(8,128)S(1)}, u32[]{:S(2)}, u32[]{:S(2)}) collective-permute-start(f32[128,256]{1,0:T(8,128)S(1)} %copy-done.50), channel_id=1, source_target_pairs={{0,24},{8,0},{16,8},{24,16},{1,25},{9,1},{17,9},{25,17},{2,26},{10... | collective-permute-start | bytes 393224 | tf_op jit(solution)/shard_map/ppermute | solution.py:31
  344.9 27.7 %collective-permute-start.52 = (f32[16,3072]{1,0:T(8,128)}, f32[16,3072]{1,0:T(8,128)S(1)}, u32[]{:S(2)}, u32[]{:S(2)}) collective-permute-start(f32[16,3072]{1,0:T(8,128)} %get-tuple-element.100), channel_id=1, source_target_pairs={{0,4},{1,5},{2,6},{3,7},{4,0},{5,1},{6,2},{7,3},{8,12},{9,13},{10,... | collective-permute-start | bytes 589832 | tf_op jit(solution)/shard_map/ppermute | solution.py:31
  347.6 28.5 %collective-permute-start.53 = (f32[16,3072]{1,0:T(8,128)}, f32[16,3072]{1,0:T(8,128)S(1)}, u32[]{:S(2)}, u32[]{:S(2)}) collective-permute-start(f32[16,3072]{1,0:T(8,128)} %get-tuple-element.101), channel_id=1, source_target_pairs={{0,3},{1,4},{2,5},{3,6},{4,7},{5,0},{6,1},{7,2},{8,11},{9,12},{10,... | collective-permute-start | bytes 589832 | tf_op jit(solution)/shard_map/ppermute | solution.py:31
  376.7 30.4 %collective-permute-start.44 = (f32[16,3328]{1,0:T(8,128)}, f32[16,3328]{1,0:T(8,128)S(1)}, u32[]{:S(2)}, u32[]{:S(2)}) collective-permute-start(f32[16,3328]{1,0:T(8,128)} %get-tuple-element.86), channel_id=1, source_target_pairs={{0,5},{1,6},{2,7},{3,0},{4,1},{5,2},{6,3},{7,4},{8,13},{9,14},{10,... | collective-permute-start | bytes 638984 | tf_op jit(solution)/shard_map/ppermute | solution.py:31
  380.1 36.4 %collective-permute-start.45 = (f32[16,3328]{1,0:T(8,128)}, f32[16,3328]{1,0:T(8,128)S(1)}, u32[]{:S(2)}, u32[]{:S(2)}) collective-permute-start(f32[16,3328]{1,0:T(8,128)} %get-tuple-element.87), channel_id=1, source_target_pairs={{0,4},{1,5},{2,6},{3,7},{4,0},{5,1},{6,2},{7,3},{8,12},{9,13},{10,... | collective-permute-start | bytes 638984 | tf_op jit(solution)/shard_map/ppermute | solution.py:31
  (94 other events, 2414.8 us)

commit v2 on v1

--- a/solution.py
+++ b/solution.py
@@ -18,6 +18,7 @@
 CHLOROPHYLL_WARM = 10.0
 LANES = 128
 ROWS = 8
+GAP = 8
 
 
 def shifted(block, axis, distance):
@@ -87,6 +88,7 @@
     held, _, across, lat = cur[0].shape
     tracers = n * held
     halves = across // ROWS
+    pitch = across + GAP
 
     row_at = lax.broadcasted_iota(jnp.int32, (across, lat), 0)
     lane_at = lax.broadcasted_iota(jnp.int32, (across, lat), 1)
@@ -150,7 +152,7 @@
         l = j // halves
         h = j % halves
         for t in range(tracers):
-            at = pl.multiple_of((t * nl + l) * across + h * ROWS, ROWS)
+            at = pl.multiple_of((t * nl + l) * pitch + h * ROWS, ROWS)
             for s in range(lat // LANES):
                 done[s, pl.ds(at, ROWS), :] = current[
                     t * ROWS : (t + 1) * ROWS, s * LANES : (s + 1) * LANES
@@ -164,7 +166,7 @@
         lanes = slice(s * LANES, (s + 1) * LANES)
         column = before[:, lanes]
         for l in range(nl):
-            at = pl.multiple_of((me * (held * nl) + l) * across, ROWS)
+            at = pl.multiple_of((me * (held * nl) + l) * pitch, ROWS)
             pigment = done[s, pl.ds(at, across), :]
             square = pigment * pigment
             absorb = WATER_ABSORB + PIGMENT_ABSORB * square / (1.0 + square)
@@ -183,7 +185,7 @@
             keep = lane < shift_ref[segment]
             index = jnp.broadcast_to(pick[pl.ds(segment, 1), :], (ROWS, LANES))
             for g in range(tracers * nl // ROWS):
-                value = done[s, pl.ds(g * ROWS * across + x, ROWS, stride=across), :]
+                value = done[s, pl.ds(g * ROWS * pitch + x, ROWS, stride=pitch), :]
                 value = jnp.take_along_axis(value, index, axis=1, mode="promise_in_bounds")
                 here = (slice(g * ROWS, (g + 1) * ROWS), pl.ds(tile, LANES))
                 packed[here] = jnp.where(keep, packed[here], value)
@@ -252,7 +254,7 @@
             ],
             scratch_shapes=[
                 pltpu.VMEM((nl * (across // ROWS), rows, lat), jnp.float32),
-                pltpu.VMEM((lat // LANES, n * held * nl * across, LANES), jnp.float32),
+                pltpu.VMEM((lat // LANES, n * held * nl * (across + GAP), LANES), jnp.float32),
                 pltpu.VMEM((n * held * nl, lanes), jnp.float32),
             ],
         ),
@@ -264,16 +266,26 @@
     )(me, tiles, shifts, *ins)
 
 
-def unpack_kernel(n, cap, has_base, *refs):
-    _, tile_ref = refs[:2]
-    received = refs[2 : 2 + n]
-    solute, water, pick, second = refs[2 + n : 6 + n]
-    out, slots, spread = refs[6 + n + has_base :]
+def unpack_kernel(n, taken, cap, has_base, closing, *refs):
+    me_ref, tile_ref = refs[:2]
+    received = refs[2 : 2 + len(taken)]
+    solute, water, pick, second = refs[2 + len(taken) : 6 + len(taken)]
+    rest = refs[6 + len(taken) :]
+    if closing:
+        totals = rest[: n - 1]
+        absorb, sun, carried = rest[n - 1 : n + 2]
+        rest = rest[n + 2 :]
+    rest = rest[has_base:]
+    out, *rest = rest
+    if closing:
+        warmed, *rest = rest
+    slots, spread = rest
     held, nl, across, lat = solute.shape
-    d = pl.program_id(0)
-    for k in range(n):
-
-        @pl.when(d == k)
+    pitch = across + GAP
+    step = pl.program_id(0)
+    for k in range(len(taken)):
+
+        @pl.when(step == k)
         def _():
             slots[:, :cap] = received[k][:, :cap]
 
@@ -293,51 +305,90 @@
                 b = jnp.take_along_axis(
                     slots[group, pl.ds(tail, LANES)], index, axis=1, mode="promise_in_bounds"
                 )
-                spread[s, pl.ds(g * ROWS * across + x, ROWS, stride=across), :] = jnp.where(
+                spread[s, pl.ds(g * ROWS * pitch + x, ROWS, stride=pitch), :] = jnp.where(
                     later, b, a
                 )
     wet = water[...] > 0.5
     for i in range(held):
         for l in range(nl):
-            at = (i * nl + l) * across
+            at = (i * nl + l) * pitch
             for s in range(parts):
                 lanes = slice(s * LANES, (s + 1) * LANES)
                 out[i, l, :, lanes] = jnp.where(
                     wet[:, lanes], spread[s, at : at + across, :], solute[i, l, :, lanes]
                 )
-
-
-def unpack_chunk(q, parts, me, tiles, received, solute, water, pick, second, base, cap):
-    n = len(received)
+    if closing:
+
+        @pl.when(step == 0)
+        def _():
+            size = held * nl
+            here = me_ref[0]
+            for k in range(across // size):
+                lane = slice(k * lat, (k + 1) * lat)
+                row = slice(k * size, (k + 1) * size)
+                over = jnp.zeros((size, lat), jnp.float32)
+                for d in range(1, n):
+                    above = lax.rem(here + d, n) < here
+                    over = over + jnp.where(above, totals[d - 1][:, lane], 0.0)
+                light = sun[...] * (CHLOROPHYLL_WARM * water[row, :])
+                coming = jnp.exp(-over)
+                for l in range(absorb.shape[0]):
+                    over = over + absorb[l, row, :]
+                    left = jnp.exp(-over)
+                    warmed[l, row, :] = carried[l, row, :] + light * (coming - left)
+                    coming = left
+
+
+def unpack_chunk(
+    q, parts, me, tiles, returned, taken, solute, water, pick, second, base, cap, heat=None
+):
+    n = len(returned)
     held, depth, across, lat = solute.shape
     nl = depth // n // parts
+    received = [returned[d] for d in taken]
 
     def all_of(x):
-        return pl.BlockSpec(x.shape, lambda d, *_: (0,) * x.ndim)
-
-    place = pl.BlockSpec(
-        (held, nl, across, lat), lambda d, me, *_: (0, lax.rem(me[0] + d, n) * parts + q, 0, 0)
-    )
+        return pl.BlockSpec(x.shape, lambda i, *_: (0,) * x.ndim)
+
+    def place_at(i, me, *_):
+        d = sum(jnp.where(i == k, d, 0) for k, d in enumerate(taken))
+        return 0, lax.rem(me[0] + d, n) * parts + q, 0, 0
+
+    place = pl.BlockSpec((held, nl, across, lat), place_at)
+    ins = [*received, solute, water, pick, second]
     specs = [all_of(x) for x in received] + [place, all_of(water), all_of(pick), all_of(second)]
-    ins = [*received, solute, water, pick, second]
+    shapes = [jax.ShapeDtypeStruct(solute.shape, jnp.float32)]
+    outs = [place]
+    if heat is not None:
+        width = across * lat // (held * nl)
+        for d in range(1, n):
+            ins.append(returned[d])
+            specs.append(pl.BlockSpec((held * nl, width), lambda i, *_: (0, cap // width)))
+        for x in heat:
+            ins.append(x)
+            specs.append(all_of(x))
+        shapes.append(jax.ShapeDtypeStruct(heat[-1].shape, jnp.float32))
+        outs.append(all_of(heat[-1]))
     aliases = {}
     if base is not None:
         aliases = {2 + len(ins): 0}
         ins.append(base)
         specs.append(pl.BlockSpec(memory_space=pl.ANY))
     return pl.pallas_call(
-        functools.partial(unpack_kernel, n, cap, base is not None),
+        functools.partial(
+            unpack_kernel, n, taken, cap, base is not None, heat is not None
+        ),
         grid_spec=pltpu.PrefetchScalarGridSpec(
             num_scalar_prefetch=2,
-            grid=(n,),
+            grid=(len(taken),),
             in_specs=specs,
-            out_specs=place,
+            out_specs=outs,
             scratch_shapes=[
                 pltpu.VMEM((held * nl, (cap // LANES + 2) * LANES), jnp.float32),
-                pltpu.VMEM((lat // LANES, held * nl * across, LANES), jnp.float32),
+                pltpu.VMEM((lat // LANES, held * nl * (across + GAP), LANES), jnp.float32),
             ],
         ),
-        out_shape=jax.ShapeDtypeStruct(solute.shape, jnp.float32),
+        out_shape=shapes,
         input_output_aliases=aliases,
         cost_estimate=pl.CostEstimate(
             flops=100 * solute.size, bytes_accessed=12 * solute.size // parts, transcendentals=0
@@ -362,6 +413,10 @@
     parts = levels // nl
     inner = list(range(1, parts - 1))
     return nl, parts, inner + [q for q in (parts - 1, 0) if q not in inner][: parts - len(inner)]
+
+
+def reach(n):
+    return sorted(range(1, n), key=lambda d: (-min(d, n - d), d))
 
 
 def on_device(
@@ -385,13 +440,13 @@
     blocks = {}
     raw = solute_fields
     for q in range(parts):
-        sends = []
-        for d in range(n):
+        sends = {}
+        for d in reach(n):
             to = lax.rem(me + d, n)
-            sends.append(lax.dynamic_slice_in_dim(raw, to * levels + q * nl, nl, 1))
+            sends[d] = lax.dynamic_slice_in_dim(raw, to * levels + q * nl, nl, 1)
         if q == 0:
-            raw, *sends = lax.optimization_barrier((raw, *sends))
-        blocks[q] = sends[:1]
+            raw, sends = lax.optimization_barrier((raw, sends))
+        blocks[q] = [lax.dynamic_slice_in_dim(raw, me * levels + q * nl, nl, 1)]
         for d in range(1, n):
             blocks[q].append(around(sends[d], "sec", d))
 
@@ -495,22 +550,19 @@
             returned[q].append(around(x, "sec", -d) if d else x)
 
     absorb = jnp.concatenate([absorbs[q] for q in range(parts)], axis=0)
-    over = 0.0
-    for d in range(1, n):
-        sums = returned[order[-1]][d][:, cap:]
-        sums = [sums[:, k : k + lat] for k in range(0, sums.shape[1], lat)]
-        over = over + jnp.where(lax.rem(me + d, n) < me, jnp.concatenate(sums, axis=0), 0.0)
-    depth_to = over[None] + jnp.cumsum(absorb, axis=0)
-    warming = shortwave * (jnp.exp(-(depth_to - absorb)) - jnp.exp(-depth_to))
-    thermal_revised = thermal_carried + CHLOROPHYLL_WARM * water * warming
-
+    sun = shortwave[None, :]
+
+    calls = [(q, tuple(range(n))) for q in order[:-1]]
+    far = [0, *reach(n)]
+    calls += [(order[-1], tuple(far[: n // 2])), (order[-1], tuple(far[n // 2 :]))]
     solute_revised = None
-    for q in order:
-        solute_revised = unpack_chunk(
-            q, parts, me_at, tiles, returned[q], solute_fields, water, spread_at, spread_later,
-            solute_revised, cap,
+    for k, (q, taken) in enumerate(calls):
+        heat = (absorb, sun, thermal_carried) if k == len(calls) - 1 else None
+        solute_revised, *thermal_revised = unpack_chunk(
+            q, parts, me_at, tiles, returned[q], taken, solute_fields, water, spread_at,
+            spread_later, solute_revised, cap, heat,
         )
-    return thermal_revised, jnp.stack([east, north]), spreading, solute_revised
+    return thermal_revised[0], jnp.stack([east, north]), spreading, solute_revised
 
 
 def solution(mesh):

time: 430 us -> 439 us (1.021)
  waiting for transfers between devices: 93.5 us -> 101 us
    ppermute x4, starting transfers between devices: 22.8 us -> 32.2 us  [shifted(): return lax.ppermute(block, axis, route)]
    ppermute x66, waiting for transfers between devices: 93.5 us -> 101 us  [around(): lax.ppermute(block, axis, [(i, (i + distance) % count) for i in range(cou...]
    ppermute x66, starting transfers between devices: 151 us -> 144 us  [around(): lax.ppermute(block, axis, [(i, (i + distance) % count) for i in range(cou...]
    pallas_call x4 -> x5, Pallas kernels: 33.4 us -> 35.6 us  [unpack_chunk(): pl.pallas_call(functools.partial(unpack_kernel, n, taken, cap, base is no...]
  transfers between devices with their start and end apart: 70 -> 70, of which waited for: 9 -> 17; matrix products, arithmetic and copies ran while one was open for 8% -> 7% of each run, Pallas kernels for 28% -> 26%
where the time goes in v2:
time: 439 us; the launch traced here: 438 us
  starting transfers between devices  177 us (40%)
  Pallas kernels  121 us (28%)
  waiting for transfers between devices  101 us (23%)
  local copies, waits for them, and re-layouts  21.8 us (5%)
  other arithmetic  13 us (3%)
    ppermute x66, starting transfers between devices, around(): lax.ppermute(block, axis, [(i, (i + distance) % count) for i in range(cou...  144 us
    ppermute x66, waiting for transfers between devices, around(): lax.ppermute(block, axis, [(i, (i + distance) % count) for i in range(cou...  101 us
    pallas_call x4, Pallas kernels, react_chunk(): pl.pallas_call(functools.partial(react_kernel, n, nl, q, closing), grid_s...  75.9 us
    pallas_call x5, Pallas kernels, unpack_chunk(): pl.pallas_call(functools.partial(unpack_kernel, n, taken, cap, base is no...  35.6 us
    ppermute x4, starting transfers between devices, shifted(): return lax.ppermute(block, axis, route)  32.2 us
    pallas_call x4, Pallas kernels, chunk_edges(): pl.pallas_call(functools.partial(edges_kernel, n, level, turn), in_specs=...  9.73 us
    dynamic_slice x3, local copies, waits for them, and re-layouts, on_device(): sends[d] = lax.dynamic_slice_in_dim(raw, to * levels + q * nl, nl, 1)  9.61 us
  transfers between devices with their start and end apart: 70, of which 17 were waited for; matrix products, arithmetic and copies ran while one was open for 7% of the time, Pallas kernels for 26%

profile of v2, /device:TPU:0, one launch (start us, length us, event | category | flops | bytes accessed | tf_op | source)
XLA Modules:
  0.0 437.8 jit_solution(13395618651908027670)
XLA Ops:
  12.3 4.1 collective-permute-start.24
  29.5 4.2 constant_dynamic-slice_fusion
  46.1 19.2 %collective-permute-done.2.refs_3_.refs_14_.refs_6_ = f32[4,4,16,256]{3,2,1,0:T(8,128)S(1)} collective-permute-done((f32[4,4,16,256]{3,2,1,0:T(8,128)}, f32[4,4,16,256]{3,2,1,0:T(8,128)S(1)}, u32[]{:S(2)}, u32[]{:S(2)}) %collective-permute-start.2) | collective-permute-done | bytes 262176 | tf_op jit(solution)/shard_map/ppermute | solution.py:32
  65.5 6.7 %collective-permute-start.15 = (f32[4,4,16,256]{3,2,1,0:T(8,128)S(1)}, f32[4,4,16,256]{3,2,1,0:T(8,128)S(1)}, u32[]{:S(2)}, u32[]{:S(2)}) collective-permute-start(f32[4,4,16,256]{3,2,1,0:T(8,128)S(1)} %get-tuple-element.143), channel_id=1, source_target_pairs={{0,1},{1,2},{2,3},{3,4},{4,5},{5,6},{6,7},{7,0},{8,9},{9,10},{10,1... | collective-permute-start | bytes 786440 | tf_op jit(solution)/shard_map/ppermute | solution.py:32
  72.3 11.2 %collective-permute-start.16 = (f32[4,4,16,256]{3,2,1,0:T(8,128)S(1)}, f32[4,4,16,256]{3,2,1,0:T(8,128)S(1)}, u32[]{:S(2)}, u32[]{:S(2)}) collective-permute-start(f32[4,4,16,256]{3,2,1,0:T(8,128)S(1)} %get-tuple-element.142), channel_id=1, source_target_pairs={{0,2},{1,3},{2,4},{3,5},{4,6},{5,7},{6,0},{7,1},{8,10},{9,11},{10,... | collective-permute-start | bytes 786440 | tf_op jit(solution)/shard_map/ppermute | solution.py:32
  83.6 15.4 %collective-permute-start.17 = (f32[4,4,16,256]{3,2,1,0:T(8,128)}, f32[4,4,16,256]{3,2,1,0:T(8,128)}, u32[]{:S(2)}, u32[]{:S(2)}) collective-permute-start(f32[4,4,16,256]{3,2,1,0:T(8,128)} %get-tuple-element.141), channel_id=1, source_target_pairs={{0,3},{1,4},{2,5},{3,6},{4,7},{5,0},{6,1},{7,2},{8,11},{9,12},{10,... | collective-permute-start | bytes 786440 | tf_op jit(solution)/shard_map/ppermute | solution.py:32
  106.1 10.9 %collective-permute-done.18.refs_4_.refs_7_.refs_15_.refs_23_ = f32[4,4,16,256]{3,2,1,0:T(8,128)} collective-permute-done((f32[4,4,16,256]{3,2,1,0:T(8,128)}, f32[4,4,16,256]{3,2,1,0:T(8,128)}, u32[]{:S(2)}, u32[]{:S(2)}) %collective-permute-start.18) | collective-permute-done | bytes 262176 | tf_op jit(solution)/shard_map/ppermute | solution.py:32
  117.0 14.4 %collective-permute-start.27 = (f32[4,4,16,256]{3,2,1,0:T(8,128)}, f32[4,4,16,256]{3,2,1,0:T(8,128)S(1)}, u32[]{:S(2)}, u32[]{:S(2)}) collective-permute-start(f32[4,4,16,256]{3,2,1,0:T(8,128)} %get-tuple-element.134), channel_id=1, source_target_pairs={{0,2},{1,3},{2,4},{3,5},{4,6},{5,7},{6,0},{7,1},{8,10},{9,11},{10,... | collective-permute-start | bytes 786440 | tf_op jit(solution)/shard_map/ppermute | solution.py:32
  131.3 8.4 %collective-permute-start.29 = (f32[4,4,16,256]{3,2,1,0:T(8,128)}, f32[4,4,16,256]{3,2,1,0:T(8,128)S(1)}, u32[]{:S(2)}, u32[]{:S(2)}) collective-permute-start(f32[4,4,16,256]{3,2,1,0:T(8,128)} %get-tuple-element.132), channel_id=1, source_target_pairs={{0,4},{1,5},{2,6},{3,7},{4,0},{5,1},{6,2},{7,3},{8,12},{9,13},{10,... | collective-permute-start | bytes 786440 | tf_op jit(solution)/shard_map/ppermute | solution.py:32
  142.7 12.1 %collective-permute-start.9 = (f32[4,4,16,256]{3,2,1,0:T(8,128)}, f32[4,4,16,256]{3,2,1,0:T(8,128)S(1)}, u32[]{:S(2)}, u32[]{:S(2)}) collective-permute-start(f32[4,4,16,256]{3,2,1,0:T(8,128)} %get-tuple-element.149), channel_id=1, source_target_pairs={{0,3},{1,4},{2,5},{3,6},{4,7},{5,0},{6,1},{7,2},{8,11},{9,12},{10,... | collective-permute-start | bytes 786440 | tf_op jit(solution)/shard_map/ppermute | solution.py:32
  154.8 22.1 %collective-permute-done.28.refs_3_.refs_22_.refs_6_.refs_14_ = f32[4,4,16,256]{3,2,1,0:T(8,128)S(1)} collective-permute-done((f32[4,4,16,256]{3,2,1,0:T(8,128)}, f32[4,4,16,256]{3,2,1,0:T(8,128)S(1)}, u32[]{:S(2)}, u32[]{:S(2)}) %collective-permute-start.28) | collective-permute-done | bytes 262176 | tf_op jit(solution)/shard_map/ppermute | solution.py:32
  177.1 6.0 %collective-permute-start.32 = (f32[4,4,16,256]{3,2,1,0:T(8,128)S(1)}, f32[4,4,16,256]{3,2,1,0:T(8,128)}, u32[]{:S(2)}, u32[]{:S(2)}) collective-permute-start(f32[4,4,16,256]{3,2,1,0:T(8,128)S(1)} %get-tuple-element.129), channel_id=1, source_target_pairs={{0,7},{1,0},{2,1},{3,2},{4,3},{5,4},{6,5},{7,6},{8,15},{9,8},{10,9... | collective-permute-start | bytes 786440 | tf_op jit(solution)/shard_map/ppermute | solution.py:32
  186.3 5.1 %collective-permute-done.31.refs_6_.refs_25_.refs_9_.refs_17_ = f32[4,4,16,256]{3,2,1,0:T(8,128)} collective-permute-done((f32[4,4,16,256]{3,2,1,0:T(8,128)S(1)}, f32[4,4,16,256]{3,2,1,0:T(8,128)}, u32[]{:S(2)}, u32[]{:S(2)}) %collective-permute-start.31) | collective-permute-done | bytes 262176 | tf_op jit(solution)/shard_map/ppermute | solution.py:32
  199.1 9.6 %collective-permute-start.11 = (f32[4,4,16,256]{3,2,1,0:T(8,128)S(1)}, f32[4,4,16,256]{3,2,1,0:T(8,128)S(1)}, u32[]{:S(2)}, u32[]{:S(2)}) collective-permute-start(f32[4,4,16,256]{3,2,1,0:T(8,128)S(1)} %copy-done.23), channel_id=1, source_target_pairs={{0,5},{1,6},{2,7},{3,0},{4,1},{5,2},{6,3},{7,4},{8,13},{9,14},{10,... | collective-permute-start | bytes 786440 | tf_op jit(solution)/shard_map/ppermute | solution.py:32
  208.7 3.2 collective-permute-start.12
  215.3 19.0 %react.4 = (f32[16,3072]{1,0:T(8,128)}, f32[16,3072]{1,0:T(8,128)}, f32[16,3072]{1,0:T(8,128)}, f32[16,3072]{1,0:T(8,128)}, f32[16,3072]{1,0:T(8,128)}, /*index=...) custom-call(s32[1]{0:T(128)} %bitcast.refs_0_, ...), custom_call_target="tpu_custom_call" | custom-call | flops 3221225472 | bytes 6291456 | tf_op jit(solution)/shard_map/react/pallas_call | solution.py:246
  234.3 2.9 collective-permute-start.22
  238.1 19.0 %react.5 = (f32[16,3072]{1,0:T(8,128)}, f32[16,3072]{1,0:T(8,128)}, f32[16,3072]{1,0:T(8,128)}, f32[16,3072]{1,0:T(8,128)}, f32[16,3072]{1,0:T(8,128)}, /*index=...) custom-call(s32[1]{0:T(128)} %bitcast.refs_0_, ...), custom_call_target="tpu_custom_call" | custom-call | flops 3221225472 | bytes 6291456 | tf_op jit(solution)/shard_map/react/pallas_call | solution.py:246
  274.4 25.5 %collective-permute-start.14 = (f32[32,1,16,256]{3,2,1,0:T(8,128)}, f32[32,1,16,256]{3,2,1,0:T(8,128)}, u32[]{:S(2)}, u32[]{:S(2)}) collective-permute-start(f32[32,1,16,256]{3,2,1,0:T(8,128)} %get-tuple-element.71), channel_id=1, source_target_pairs={{0,1},{1,2},{2,3},{3,4},{4,5},{5,6},{6,7},{8,9},{9,10},{10,11},{11... | collective-permute-start | bytes 1572872 | tf_op jit(solution)/shard_map/ppermute | solution.py:27
  300.1 3.6 collective-permute-start.63
  303.7 5.2 %collective-permute-done.62.refs_9_ = f32[16,3072]{1,0:T(8,128)S(1)} collective-permute-done((f32[16,3072]{1,0:T(8,128)}, f32[16,3072]{1,0:T(8,128)S(1)}, u32[]{:S(2)}, u32[]{:S(2)}) %collective-permute-start.62) | collective-permute-done | bytes 196640 | tf_op jit(solution)/shard_map/ppermute | solution.py:32
  309.0 4.0 collective-permute-start.66
  315.3 19.0 %react.6 = (f32[16,3072]{1,0:T(8,128)}, f32[16,3072]{1,0:T(8,128)}, f32[16,3072]{1,0:T(8,128)}, f32[16,3072]{1,0:T(8,128)}, f32[16,3072]{1,0:T(8,128)}, /*index=...) custom-call(s32[1]{0:T(128)} %bitcast.refs_0_, ...), custom_call_target="tpu_custom_call" | custom-call | flops 3221225472 | bytes 6291456 | tf_op jit(solution)/shard_map/react/pallas_call | solution.py:246
  334.3 3.4 collective-permute-start.69
  340.6 3.0 collective-permute-start.52
  343.6 19.0 %react.7 = (f32[16,3328]{1,0:T(8,128)}, f32[16,3328]{1,0:T(8,128)}, f32[16,3328]{1,0:T(8,128)}, f32[16,3328]{1,0:T(8,128)}, f32[16,3328]{1,0:T(8,128)}, /*index=...) custom-call(s32[1]{0:T(128)} %bitcast.refs_0_, ...), custom_call_target="tpu_custom_call" | custom-call | flops 3221225472 | bytes 6291456 | tf_op jit(solution)/shard_map/react/pallas_call | solution.py:246
  368.9 25.4 %collective-permute-done.53.refs_7_ = f32[16,3072]{1,0:T(8,128)S(1)} collective-permute-done((f32[16,3072]{1,0:T(8,128)}, f32[16,3072]{1,0:T(8,128)S(1)}, u32[]{:S(2)}, u32[]{:S(2)}) %collective-permute-start.53) | collective-permute-done | bytes 196640 | tf_op jit(solution)/shard_map/ppermute | solution.py:32
  399.6 8.3 %unpack.5.refs_14_ = f32[4,128,16,256]{3,2,1,0:T(8,128)} custom-call(s32[1]{0:T(128)} %bitcast.refs_0_, s32[32]{0:T(128)} %and_select_fusion.3.refs_1_, f32[16,3072]{1,0:T(8,128)} %get-tuple-element.112.refs_2_, f32[16,3072]{1,0:T(8,128)} %copy-done.41, f32[16,3072]{1,0:T(8,128)} %copy-done.42, f32[16,3072]{1,0:T(8,128)} %copy-done.43, ...), custom_call_target="tpu_custom_call" | custom-call | flops 209715200 | bytes 6291456 | tf_op jit(solution)/shard_map/unpack/pallas_call | solution.py:377
  408.0 8.4 %unpack.6.refs_14_ = f32[4,128,16,256]{3,2,1,0:T(8,128)} custom-call(s32[1]{0:T(128)} %bitcast.refs_0_, s32[32]{0:T(128)} %and_select_fusion.3.refs_1_, f32[16,3072]{1,0:T(8,128)} %get-tuple-element.104.refs_2_, f32[16,3072]{1,0:T(8,128)} %copy-done.34, f32[16,3072]{1,0:T(8,128)} %copy-done.35, ...), custom_call_target="tpu_custom_call", output_to_operand_aliasing={{}: (14, {})} | custom-call | flops 209715200 | bytes 6291456 | tf_op jit(solution)/shard_map/unpack/pallas_call | solution.py:377
  417.1 8.3 %unpack.7.refs_10_ = f32[4,128,16,256]{3,2,1,0:T(8,128)} custom-call(s32[1]{0:T(128)} %bitcast.refs_0_, s32[32]{0:T(128)} %and_select_fusion.3.refs_1_, f32[16,3072]{1,0:T(8,128)} %get-tuple-element.96.refs_2_, f32[16,3072]{1,0:T(8,128)} %copy-done.47, f32[16,3072]{1,0:T(8,128)} %collective-permute-done.50.refs_4_, ...), custom_call_target="tpu_custom_call", output_to_operand_aliasing={{}: (14, {})} | custom-call | flops 209715200 | bytes 6291456 | tf_op jit(solution)/shard_map/unpack/pallas_call | solution.py:377
  426.1 5.1 %unpack.8.refs_20_ = f32[4,128,16,256]{3,2,1,0:T(8,128)} custom-call(s32[1]{0:T(128)} %bitcast.refs_0_, s32[32]{0:T(128)} %and_select_fusion.3.refs_1_, f32[16,3328]{1,0:T(8,128)} %get-tuple-element.95.refs_2_, f32[16,3328]{1,0:T(8,128)} %copy-done.9, f32[16,3328]{1,0:T(8,128)} %copy-done.8, f32[16,3328]{1,0:T(8,128)} %copy-done.10, ...), custom_call_target="tpu_custom_call", output_to_operand_aliasing={{}: (10, {})} | custom-call | flops 209715200 | bytes 6291456 | tf_op jit(solution)/shard_map/unpack/pallas_call | solution.py:377
  432.1 5.6 %unpack.9 = (f32[4,128,16,256]{3,2,1,0:T(8,128)}, f32[16,16,256]{2,1,0:T(8,128)}) custom-call(s32[1]{0:T(128)} %bitcast.refs_0_, s32[32]{0:T(128)} %and_select_fusion.3.refs_1_, f32[16,3328]{1,0:T(8,128)} %copy-done.4, f32[16,3328]{1,0:T(8,128)} %copy-done.5, f32[16,3328]{1,0:T(8,128)} %copy-done.6, ...), custom_call_target="tpu_custom_call", output_to_operand_aliasing={{0}: (20, {})} | custom-call | flops 209715200 | bytes 6291456 | tf_op jit(solution)/shard_map/unpack/pallas_call | solution.py:377
  (324 shorter events, 98.7 us)
Async XLA Ops:
  3.4 38.6 %collective-permute-start = (f32[4,4,16,256]{3,2,1,0:T(8,128)}, f32[4,4,16,256]{3,2,1,0:T(8,128)S(1)}, u32[]{:S(2)}, u32[]{:S(2)}) collective-permute-start(f32[4,4,16,256]{3,2,1,0:T(8,128)} %get-tuple-element.64), channel_id=1, source_target_pairs={{0,1},{1,2},{2,3},{3,4},{4,5},{5,6},{6,7},{7,0},{8,9},{9,10},{10,1... | collective-permute-start | bytes 786440 | tf_op jit(solution)/shard_map/ppermute | solution.py:32
  5.5 29.0 %collective-permute-start.48 = (f32[16,1,256]{2,1,0:T(1,128)}, f32[16,1,256]{2,1,0:T(1,128)S(1)}, u32[]{:S(2)}, u32[]{:S(2)}) collective-permute-start(f32[16,1,256]{2,1,0:T(1,128)} %get-tuple-element.172), channel_id=1, source_target_pairs={{0,8},{8,16},{16,24},{24,0},{1,9},{9,17},{17,25},{25,1},{2,10},{10... | collective-permute-start | bytes 49160 | tf_op jit(solution)/shard_map/ppermute | solution.py:32
  36.2 29.2 %collective-permute-start.2 = (f32[4,4,16,256]{3,2,1,0:T(8,128)}, f32[4,4,16,256]{3,2,1,0:T(8,128)S(1)}, u32[]{:S(2)}, u32[]{:S(2)}) collective-permute-start(f32[4,4,16,256]{3,2,1,0:T(8,128)} %get-tuple-element.66), channel_id=1, source_target_pairs={{0,3},{1,4},{2,5},{3,6},{4,7},{5,0},{6,1},{7,2},{8,11},{9,12},{10,... | collective-permute-start | bytes 786440 | tf_op jit(solution)/shard_map/ppermute | solution.py:32
  40.0 32.3 %collective-permute-start.4 = (f32[4,4,16,256]{3,2,1,0:T(8,128)}, f32[4,4,16,256]{3,2,1,0:T(8,128)S(1)}, u32[]{:S(2)}, u32[]{:S(2)}) collective-permute-start(f32[4,4,16,256]{3,2,1,0:T(8,128)} %get-tuple-element.68), channel_id=1, source_target_pairs={{0,5},{1,6},{2,7},{3,0},{4,1},{5,2},{6,3},{7,4},{8,13},{9,14},{10,... | collective-permute-start | bytes 786440 | tf_op jit(solution)/shard_map/ppermute | solution.py:32
  42.0 41.6 %collective-permute-start.5 = (f32[4,4,16,256]{3,2,1,0:T(8,128)}, f32[4,4,16,256]{3,2,1,0:T(8,128)S(1)}, u32[]{:S(2)}, u32[]{:S(2)}) collective-permute-start(f32[4,4,16,256]{3,2,1,0:T(8,128)} %get-tuple-element.69), channel_id=1, source_target_pairs={{0,6},{1,7},{2,0},{3,1},{4,2},{5,3},{6,4},{7,5},{8,14},{9,15},{10,... | collective-permute-start | bytes 786440 | tf_op jit(solution)/shard_map/ppermute | solution.py:32
  45.2 53.9 %collective-permute-start.6 = (f32[4,4,16,256]{3,2,1,0:T(8,128)}, f32[4,4,16,256]{3,2,1,0:T(8,128)S(1)}, u32[]{:S(2)}, u32[]{:S(2)}) collective-permute-start(f32[4,4,16,256]{3,2,1,0:T(8,128)} %get-tuple-element.70), channel_id=1, source_target_pairs={{0,7},{1,0},{2,1},{3,2},{4,3},{5,4},{6,5},{7,6},{8,15},{9,8},{10,9... | collective-permute-start | bytes 786440 | tf_op jit(solution)/shard_map/ppermute | solution.py:32
  65.3 33.7 %collective-permute-start.7 = (f32[4,4,16,256]{3,2,1,0:T(8,128)S(1)}, f32[4,4,16,256]{3,2,1,0:T(8,128)S(1)}, u32[]{:S(2)}, u32[]{:S(2)}) collective-permute-start(f32[4,4,16,256]{3,2,1,0:T(8,128)S(1)} %get-tuple-element.151), channel_id=1, source_target_pairs={{0,1},{1,2},{2,3},{3,4},{4,5},{5,6},{6,7},{7,0},{8,9},{9,10},{10,1... | collective-permute-start | bytes 786440 | tf_op jit(solution)/shard_map/ppermute | solution.py:32
  65.5 33.6 %collective-permute-start.15 = (f32[4,4,16,256]{3,2,1,0:T(8,128)S(1)}, f32[4,4,16,256]{3,2,1,0:T(8,128)S(1)}, u32[]{:S(2)}, u32[]{:S(2)}) collective-permute-start(f32[4,4,16,256]{3,2,1,0:T(8,128)S(1)} %get-tuple-element.143), channel_id=1, source_target_pairs={{0,1},{1,2},{2,3},{3,4},{4,5},{5,6},{6,7},{7,0},{8,9},{9,10},{10,1... | collective-permute-start | bytes 786440 | tf_op jit(solution)/shard_map/ppermute | solution.py:32
  72.3 29.3 %collective-permute-start.16 = (f32[4,4,16,256]{3,2,1,0:T(8,128)S(1)}, f32[4,4,16,256]{3,2,1,0:T(8,128)S(1)}, u32[]{:S(2)}, u32[]{:S(2)}) collective-permute-start(f32[4,4,16,256]{3,2,1,0:T(8,128)S(1)} %get-tuple-element.142), channel_id=1, source_target_pairs={{0,2},{1,3},{2,4},{3,5},{4,6},{5,7},{6,0},{7,1},{8,10},{9,11},{10,... | collective-permute-start | bytes 786440 | tf_op jit(solution)/shard_map/ppermute | solution.py:32
  99.1 32.3 %collective-permute-start.19 = (f32[4,4,16,256]{3,2,1,0:T(8,128)}, f32[4,4,16,256]{3,2,1,0:T(8,128)}, u32[]{:S(2)}, u32[]{:S(2)}) collective-permute-start(f32[4,4,16,256]{3,2,1,0:T(8,128)} %get-tuple-element.139), channel_id=1, source_target_pairs={{0,5},{1,6},{2,7},{3,0},{4,1},{5,2},{6,3},{7,4},{8,13},{9,14},{10,... | collective-permute-start | bytes 786440 | tf_op jit(solution)/shard_map/ppermute | solution.py:32
  99.2 32.2 %collective-permute-start.20 = (f32[4,4,16,256]{3,2,1,0:T(8,128)S(1)}, f32[4,4,16,256]{3,2,1,0:T(8,128)}, u32[]{:S(2)}, u32[]{:S(2)}) collective-permute-start(f32[4,4,16,256]{3,2,1,0:T(8,128)S(1)} %get-tuple-element.138), channel_id=1, source_target_pairs={{0,6},{1,7},{2,0},{3,1},{4,2},{5,3},{6,4},{7,5},{8,14},{9,15},{10,... | collective-permute-start | bytes 786440 | tf_op jit(solution)/shard_map/ppermute | solution.py:32
  101.6 38.2 %collective-permute-start.21 = (f32[4,4,16,256]{3,2,1,0:T(8,128)S(1)}, f32[4,4,16,256]{3,2,1,0:T(8,128)}, u32[]{:S(2)}, u32[]{:S(2)}) collective-permute-start(f32[4,4,16,256]{3,2,1,0:T(8,128)S(1)} %get-tuple-element.137), channel_id=1, source_target_pairs={{0,7},{1,0},{2,1},{3,2},{4,3},{5,4},{6,5},{7,6},{8,15},{9,8},{10,9... | collective-permute-start | bytes 786440 | tf_op jit(solution)/shard_map/ppermute | solution.py:32
  106.1 36.5 %collective-permute-start.26 = (f32[4,4,16,256]{3,2,1,0:T(8,128)}, f32[4,4,16,256]{3,2,1,0:T(8,128)S(1)}, u32[]{:S(2)}, u32[]{:S(2)}) collective-permute-start(f32[4,4,16,256]{3,2,1,0:T(8,128)} %get-tuple-element.135), channel_id=1, source_target_pairs={{0,1},{1,2},{2,3},{3,4},{4,5},{5,6},{6,7},{7,0},{8,9},{9,10},{10,1... | collective-permute-start | bytes 786440 | tf_op jit(solution)/shard_map/ppermute | solution.py:32
  131.3 45.5 %collective-permute-start.28 = (f32[4,4,16,256]{3,2,1,0:T(8,128)}, f32[4,4,16,256]{3,2,1,0:T(8,128)S(1)}, u32[]{:S(2)}, u32[]{:S(2)}) collective-permute-start(f32[4,4,16,256]{3,2,1,0:T(8,128)} %get-tuple-element.133), channel_id=1, source_target_pairs={{0,3},{1,4},{2,5},{3,6},{4,7},{5,0},{6,1},{7,2},{8,11},{9,12},{10,... | collective-permute-start | bytes 786440 | tf_op jit(solution)/shard_map/ppermute | solution.py:32
  131.3 45.7 %collective-permute-start.29 = (f32[4,4,16,256]{3,2,1,0:T(8,128)}, f32[4,4,16,256]{3,2,1,0:T(8,128)S(1)}, u32[]{:S(2)}, u32[]{:S(2)}) collective-permute-start(f32[4,4,16,256]{3,2,1,0:T(8,128)} %get-tuple-element.132), channel_id=1, source_target_pairs={{0,4},{1,5},{2,6},{3,7},{4,0},{5,1},{6,2},{7,3},{8,12},{9,13},{10,... | collective-permute-start | bytes 786440 | tf_op jit(solution)/shard_map/ppermute | solution.py:32
  139.8 37.3 %collective-permute-start.30 = (f32[4,4,16,256]{3,2,1,0:T(8,128)}, f32[4,4,16,256]{3,2,1,0:T(8,128)S(1)}, u32[]{:S(2)}, u32[]{:S(2)}) collective-permute-start(f32[4,4,16,256]{3,2,1,0:T(8,128)} %get-tuple-element.131), channel_id=1, source_target_pairs={{0,5},{1,6},{2,7},{3,0},{4,1},{5,2},{6,3},{7,4},{8,13},{9,14},{10,... | collective-permute-start | bytes 786440 | tf_op jit(solution)/shard_map/ppermute | solution.py:32
  142.5 56.5 %collective-permute-start.8 = (f32[4,4,16,256]{3,2,1,0:T(8,128)}, f32[4,4,16,256]{3,2,1,0:T(8,128)S(1)}, u32[]{:S(2)}, u32[]{:S(2)}) collective-permute-start(f32[4,4,16,256]{3,2,1,0:T(8,128)} %get-tuple-element.150), channel_id=1, source_target_pairs={{0,2},{1,3},{2,4},{3,5},{4,6},{5,7},{6,0},{7,1},{8,10},{9,11},{10,... | collective-permute-start | bytes 786440 | tf_op jit(solution)/shard_map/ppermute | solution.py:32
  142.7 66.0 %collective-permute-start.9 = (f32[4,4,16,256]{3,2,1,0:T(8,128)}, f32[4,4,16,256]{3,2,1,0:T(8,128)S(1)}, u32[]{:S(2)}, u32[]{:S(2)}) collective-permute-start(f32[4,4,16,256]{3,2,1,0:T(8,128)} %get-tuple-element.149), channel_id=1, source_target_pairs={{0,3},{1,4},{2,5},{3,6},{4,7},{5,0},{6,1},{7,2},{8,11},{9,12},{10,... | collective-permute-start | bytes 786440 | tf_op jit(solution)/shard_map/ppermute | solution.py:32
  176.9 35.0 %collective-permute-start.10 = (f32[4,4,16,256]{3,2,1,0:T(8,128)}, f32[4,4,16,256]{3,2,1,0:T(8,128)}, u32[]{:S(2)}, u32[]{:S(2)}) collective-permute-start(f32[4,4,16,256]{3,2,1,0:T(8,128)} %get-tuple-element.148), channel_id=1, source_target_pairs={{0,4},{1,5},{2,6},{3,7},{4,0},{5,1},{6,2},{7,3},{8,12},{9,13},{10,... | collective-permute-start | bytes 786440 | tf_op jit(solution)/shard_map/ppermute | solution.py:32
  199.1 35.2 %collective-permute-start.11 = (f32[4,4,16,256]{3,2,1,0:T(8,128)S(1)}, f32[4,4,16,256]{3,2,1,0:T(8,128)S(1)}, u32[]{:S(2)}, u32[]{:S(2)}) collective-permute-start(f32[4,4,16,256]{3,2,1,0:T(8,128)S(1)} %copy-done.23), channel_id=1, source_target_pairs={{0,5},{1,6},{2,7},{3,0},{4,1},{5,2},{6,3},{7,4},{8,13},{9,14},{10,... | collective-permute-start | bytes 786440 | tf_op jit(solution)/shard_map/ppermute | solution.py:32
  262.8 50.3 %collective-permute-start.33 = (f32[32,1,16,256]{3,2,1,0:T(8,128)}, f32[32,1,16,256]{3,2,1,0:T(8,128)S(1)}, u32[]{:S(2)}, u32[]{:S(2)}) collective-permute-start(f32[32,1,16,256]{3,2,1,0:T(8,128)} %get-tuple-element.74), channel_id=1, source_target_pairs={{1,0},{2,1},{3,2},{4,3},{5,4},{6,5},{7,6},{9,8},{10,9},{11,10},{12... | collective-permute-start | bytes 1572872 | tf_op jit(solution)/shard_map/ppermute | solution.py:27
  269.7 30.4 %collective-permute-start.59 = (f32[16,3072]{1,0:T(8,128)}, f32[16,3072]{1,0:T(8,128)S(1)}, u32[]{:S(2)}, u32[]{:S(2)}) collective-permute-start(f32[16,3072]{1,0:T(8,128)} %get-tuple-element.108), channel_id=1, source_target_pairs={{0,4},{1,5},{2,6},{3,7},{4,0},{5,1},{6,2},{7,3},{8,12},{9,13},{10,... | collective-permute-start | bytes 589832 | tf_op jit(solution)/shard_map/ppermute | solution.py:32
  271.0 29.1 %collective-permute-start.60 = (f32[16,3072]{1,0:T(8,128)}, f32[16,3072]{1,0:T(8,128)S(1)}, u32[]{:S(2)}, u32[]{:S(2)}) collective-permute-start(f32[16,3072]{1,0:T(8,128)} %get-tuple-element.109), channel_id=1, source_target_pairs={{0,3},{1,4},{2,5},{3,6},{4,7},{5,0},{6,1},{7,2},{8,11},{9,12},{10,... | collective-permute-start | bytes 589832 | tf_op jit(solution)/shard_map/ppermute | solution.py:32
  271.0 32.7 %collective-permute-start.61 = (f32[16,3072]{1,0:T(8,128)}, f32[16,3072]{1,0:T(8,128)S(1)}, u32[]{:S(2)}, u32[]{:S(2)}) collective-permute-start(f32[16,3072]{1,0:T(8,128)} %get-tuple-element.110), channel_id=1, source_target_pairs={{0,2},{1,3},{2,4},{3,5},{4,6},{5,7},{6,0},{7,1},{8,10},{9,11},{10,... | collective-permute-start | bytes 589832 | tf_op jit(solution)/shard_map/ppermute | solution.py:32
  274.4 66.2 %collective-permute-start.14 = (f32[32,1,16,256]{3,2,1,0:T(8,128)}, f32[32,1,16,256]{3,2,1,0:T(8,128)}, u32[]{:S(2)}, u32[]{:S(2)}) collective-permute-start(f32[32,1,16,256]{3,2,1,0:T(8,128)} %get-tuple-element.71), channel_id=1, source_target_pairs={{0,1},{1,2},{2,3},{3,4},{4,5},{5,6},{6,7},{8,9},{9,10},{10,11},{11... | collective-permute-start | bytes 1572872 | tf_op jit(solution)/shard_map/ppermute | solution.py:27
  362.8 33.7 %collective-permute-start.44 = (f32[16,3328]{1,0:T(8,128)}, f32[16,3328]{1,0:T(8,128)S(1)}, u32[]{:S(2)}, u32[]{:S(2)}) collective-permute-start(f32[16,3328]{1,0:T(8,128)} %get-tuple-element.88), channel_id=1, source_target_pairs={{0,5},{1,6},{2,7},{3,0},{4,1},{5,2},{6,3},{7,4},{8,13},{9,14},{10,... | collective-permute-start | bytes 638984 | tf_op jit(solution)/shard_map/ppermute | solution.py:32
  364.2 32.8 %collective-permute-start.45 = (f32[16,3328]{1,0:T(8,128)}, f32[16,3328]{1,0:T(8,128)S(1)}, u32[]{:S(2)}, u32[]{:S(2)}) collective-permute-start(f32[16,3328]{1,0:T(8,128)} %get-tuple-element.89), channel_id=1, source_target_pairs={{0,4},{1,5},{2,6},{3,7},{4,0},{5,1},{6,2},{7,3},{8,12},{9,13},{10,... | collective-permute-start | bytes 638984 | tf_op jit(solution)/shard_map/ppermute | solution.py:32
  365.1 29.2 %collective-permute-start.53 = (f32[16,3072]{1,0:T(8,128)}, f32[16,3072]{1,0:T(8,128)S(1)}, u32[]{:S(2)}, u32[]{:S(2)}) collective-permute-start(f32[16,3072]{1,0:T(8,128)} %get-tuple-element.101), channel_id=1, source_target_pairs={{0,3},{1,4},{2,5},{3,6},{4,7},{5,0},{6,1},{7,2},{8,11},{9,12},{10,... | collective-permute-start | bytes 589832 | tf_op jit(solution)/shard_map/ppermute | solution.py:32
  394.2 37.0 %collective-permute-start.40 = (f32[16,3328]{1,0:T(8,128)}, f32[16,3328]{1,0:T(8,128)S(1)}, u32[]{:S(2)}, u32[]{:S(2)}) collective-permute-start(f32[16,3328]{1,0:T(8,128)} %get-tuple-element.84), channel_id=1, source_target_pairs={{0,6},{1,7},{2,0},{3,1},{4,2},{5,3},{6,4},{7,5},{8,14},{9,15},{10,... | collective-permute-start | bytes 638984 | tf_op jit(solution)/shard_map/ppermute | solution.py:32
  394.2 37.0 %collective-permute-start.41 = (f32[16,3328]{1,0:T(8,128)}, f32[16,3328]{1,0:T(8,128)S(1)}, u32[]{:S(2)}, u32[]{:S(2)}) collective-permute-start(f32[16,3328]{1,0:T(8,128)} %get-tuple-element.85), channel_id=1, source_target_pairs={{0,2},{1,3},{2,4},{3,5},{4,6},{5,7},{6,0},{7,1},{8,10},{9,11},{10,... | collective-permute-start | bytes 638984 | tf_op jit(solution)/shard_map/ppermute | solution.py:32
  396.5 34.7 %collective-permute-start.42 = (f32[16,3328]{1,0:T(8,128)}, f32[16,3328]{1,0:T(8,128)S(1)}, u32[]{:S(2)}, u32[]{:S(2)}) collective-permute-start(f32[16,3328]{1,0:T(8,128)} %get-tuple-element.86), channel_id=1, source_target_pairs={{0,7},{1,0},{2,1},{3,2},{4,3},{5,4},{6,5},{7,6},{8,15},{9,8},{10,9... | collective-permute-start | bytes 638984 | tf_op jit(solution)/shard_map/ppermute | solution.py:32
  396.5 34.7 %collective-permute-start.43 = (f32[16,3328]{1,0:T(8,128)}, f32[16,3328]{1,0:T(8,128)S(1)}, u32[]{:S(2)}, u32[]{:S(2)}) collective-permute-start(f32[16,3328]{1,0:T(8,128)} %get-tuple-element.87), channel_id=1, source_target_pairs={{0,1},{1,2},{2,3},{3,4},{4,5},{5,6},{6,7},{7,0},{8,9},{9,10},{10,1... | collective-permute-start | bytes 638984 | tf_op jit(solution)/shard_map/ppermute | solution.py:32
  (105 other events, 3095.5 us)

commit v3 on v2

--- a/solution.py
+++ b/solution.py
@@ -266,7 +266,7 @@
     )(me, tiles, shifts, *ins)
 
 
-def unpack_kernel(n, taken, cap, has_base, closing, *refs):
+def unpack_kernel(n, taken, nl, cap, at_level, has_base, closing, *refs):
     me_ref, tile_ref = refs[:2]
     received = refs[2 : 2 + len(taken)]
     solute, water, pick, second = refs[2 + len(taken) : 6 + len(taken)]
@@ -279,16 +279,71 @@
     out, *rest = rest
     if closing:
         warmed, *rest = rest
-    slots, spread = rest
-    held, nl, across, lat = solute.shape
+    slots, water_in, spread, sems = rest
+    held, depth, across, lat = solute.shape
+    levels = depth // n
     pitch = across + GAP
-    step = pl.program_id(0)
-    for k in range(len(taken)):
-
-        @pl.when(step == k)
-        def _():
-            slots[:, :cap] = received[k][:, :cap]
-
+    here = me_ref[0]
+    count = len(taken)
+
+    def place(k):
+        d = sum(jnp.where(k == j, d, 0) for j, d in enumerate(taken))
+        return pl.ds(lax.rem(here + d, n) * levels + at_level, nl)
+
+    def packed_in(k, source):
+        return pltpu.make_async_copy(
+            source.at[:, pl.ds(0, cap)], slots.at[k, :, pl.ds(0, cap)], sems.at[0, k]
+        )
+
+    def block_in(k):
+        return pltpu.make_async_copy(solute.at[:, place(k)], water_in.at[k], sems.at[1, k])
+
+    def block_out(k):
+        return pltpu.make_async_copy(water_in.at[k], out.at[:, place(k)], sems.at[2, k])
+
+    for k in range(count):
+        packed_in(k, received[k]).start()
+        block_in(k).start()
+    wet = water[...] > 0.5
+
+    def unpack(k, carry):
+        packed_in(k, received[0]).wait()
+        block_in(k).wait()
+        spread_block(k, tile_ref, pick, second, slots, spread, held * nl, across, lat)
+        for i in range(held):
+            for l in range(nl):
+                at = (i * nl + l) * pitch
+                for s in range(lat // LANES):
+                    lanes = slice(s * LANES, (s + 1) * LANES)
+                    water_in[k, i, l, :, lanes] = jnp.where(
+                        wet[:, lanes], spread[s, at : at + across, :], water_in[k, i, l, :, lanes]
+                    )
+        block_out(k).start()
+        return carry
+
+    lax.fori_loop(0, count, unpack, 0)
+    if closing:
+        size = held * nl
+        for k in range(across // size):
+            lane = slice(k * lat, (k + 1) * lat)
+            row = slice(k * size, (k + 1) * size)
+            over = jnp.zeros((size, lat), jnp.float32)
+            for d in range(1, n):
+                above = lax.rem(here + d, n) < here
+                over = over + jnp.where(above, totals[d - 1][:, lane], 0.0)
+            light = sun[...] * (CHLOROPHYLL_WARM * water[row, :])
+            coming = jnp.exp(-over)
+            for l in range(absorb.shape[0]):
+                over = over + absorb[l, row, :]
+                left = jnp.exp(-over)
+                warmed[l, row, :] = carried[l, row, :] + light * (coming - left)
+                coming = left
+    for k in range(count):
+        block_out(k).wait()
+
+
+def spread_block(k, tile_ref, pick, second, slots, spread, rows, across, lat):
+    pitch = across + GAP
     parts = lat // LANES
     for x in range(across):
         for s in range(parts):
@@ -297,46 +352,17 @@
             tail = pl.multiple_of(tile_ref[segment] * LANES + LANES, LANES)
             index = jnp.broadcast_to(pick[segment : segment + 1, :], (ROWS, LANES))
             later = jnp.broadcast_to(second[segment : segment + 1, :], (ROWS, LANES)) > 0
-            for g in range(held * nl // ROWS):
+            for g in range(rows // ROWS):
                 group = slice(g * ROWS, (g + 1) * ROWS)
                 a = jnp.take_along_axis(
-                    slots[group, pl.ds(tile, LANES)], index, axis=1, mode="promise_in_bounds"
+                    slots[k, group, pl.ds(tile, LANES)], index, axis=1, mode="promise_in_bounds"
                 )
                 b = jnp.take_along_axis(
-                    slots[group, pl.ds(tail, LANES)], index, axis=1, mode="promise_in_bounds"
+                    slots[k, group, pl.ds(tail, LANES)], index, axis=1, mode="promise_in_bounds"
                 )
                 spread[s, pl.ds(g * ROWS * pitch + x, ROWS, stride=pitch), :] = jnp.where(
                     later, b, a
                 )
-    wet = water[...] > 0.5
-    for i in range(held):
-        for l in range(nl):
-            at = (i * nl + l) * pitch
-            for s in range(parts):
-                lanes = slice(s * LANES, (s + 1) * LANES)
-                out[i, l, :, lanes] = jnp.where(
-                    wet[:, lanes], spread[s, at : at + across, :], solute[i, l, :, lanes]
-                )
-    if closing:
-
-        @pl.when(step == 0)
-        def _():
-            size = held * nl
-            here = me_ref[0]
-            for k in range(across // size):
-                lane = slice(k * lat, (k + 1) * lat)
-                row = slice(k * size, (k + 1) * size)
-                over = jnp.zeros((size, lat), jnp.float32)
-                for d in range(1, n):
-                    above = lax.rem(here + d, n) < here
-                    over = over + jnp.where(above, totals[d - 1][:, lane], 0.0)
-                light = sun[...] * (CHLOROPHYLL_WARM * water[row, :])
-                coming = jnp.exp(-over)
-                for l in range(absorb.shape[0]):
-                    over = over + absorb[l, row, :]
-                    left = jnp.exp(-over)
-                    warmed[l, row, :] = carried[l, row, :] + light * (coming - left)
-                    coming = left
 
 
 def unpack_chunk(
@@ -350,15 +376,11 @@
     def all_of(x):
         return pl.BlockSpec(x.shape, lambda i, *_: (0,) * x.ndim)
 
-    def place_at(i, me, *_):
-        d = sum(jnp.where(i == k, d, 0) for k, d in enumerate(taken))
-        return 0, lax.rem(me[0] + d, n) * parts + q, 0, 0
-
-    place = pl.BlockSpec((held, nl, across, lat), place_at)
+    apart = pl.BlockSpec(memory_space=pl.ANY)
     ins = [*received, solute, water, pick, second]
-    specs = [all_of(x) for x in received] + [place, all_of(water), all_of(pick), all_of(second)]
+    specs = [apart] * (len(taken) + 1) + [all_of(water), all_of(pick), all_of(second)]
     shapes = [jax.ShapeDtypeStruct(solute.shape, jnp.float32)]
-    outs = [place]
+    outs = [apart]
     if heat is not None:
         width = across * lat // (held * nl)
         for d in range(1, n):
@@ -376,16 +398,18 @@
         specs.append(pl.BlockSpec(memory_space=pl.ANY))
     return pl.pallas_call(
         functools.partial(
-            unpack_kernel, n, taken, cap, base is not None, heat is not None
+            unpack_kernel, n, taken, nl, cap, q * nl, base is not None, heat is not None
         ),
         grid_spec=pltpu.PrefetchScalarGridSpec(
             num_scalar_prefetch=2,
-            grid=(len(taken),),
+            grid=(1,),
             in_specs=specs,
             out_specs=outs,
             scratch_shapes=[
-                pltpu.VMEM((held * nl, (cap // LANES + 2) * LANES), jnp.float32),
+                pltpu.VMEM((len(taken), held * nl, (cap // LANES + 2) * LANES), jnp.float32),
+                pltpu.VMEM((len(taken), held, nl, across, lat), jnp.float32),
                 pltpu.VMEM((lat // LANES, held * nl * (across + GAP), LANES), jnp.float32),
+                pltpu.SemaphoreType.DMA((3, len(taken))),
             ],
         ),
         out_shape=shapes,
@@ -444,8 +468,8 @@
         for d in reach(n):
             to = lax.rem(me + d, n)
             sends[d] = lax.dynamic_slice_in_dim(raw, to * levels + q * nl, nl, 1)
-        if q == 0:
-            raw, sends = lax.optimization_barrier((raw, sends))
+            if q == 0 and d in reach(n)[:: n - 2]:
+                raw, sends = lax.optimization_barrier((raw, sends))
         blocks[q] = [lax.dynamic_slice_in_dim(raw, me * levels + q * nl, nl, 1)]
         for d in range(1, n):
             blocks[q].append(around(sends[d], "sec", d))
@@ -554,7 +578,7 @@
 
     calls = [(q, tuple(range(n))) for q in order[:-1]]
     far = [0, *reach(n)]
-    calls += [(order[-1], tuple(far[: n // 2])), (order[-1], tuple(far[n // 2 :]))]
+    calls += [(order[-1], tuple(far[a:b])) for a, b in ((0, n // 2), (n // 2, n - 2), (n - 2, n))]
     solute_revised = None
     for k, (q, taken) in enumerate(calls):
         heat = (absorb, sun, thermal_carried) if k == len(calls) - 1 else None

time: 439 us -> 446 us (1.016)
  starting transfers between devices: 177 us -> 240 us
  waiting for transfers between devices: 101 us -> 42.9 us
    ppermute x66, starting transfers between devices: 144 us -> 231 us  [around(): lax.ppermute(block, axis, [(i, (i + distance) % count) for i in range(cou...]
    ppermute x66, waiting for transfers between devices: 101 us -> 42.9 us  [around(): lax.ppermute(block, axis, [(i, (i + distance) % count) for i in range(cou...]
    ppermute x4, starting transfers between devices: 32.2 us -> 8.69 us  [shifted(): return lax.ppermute(block, axis, route)]
    pallas_call x5 -> x6, Pallas kernels: 35.6 us -> 31.9 us  [unpack_chunk(): pl.pallas_call(functools.partial(unpack_kernel, n, taken, nl, cap, q * nl...]
    dynamic_slice x3 -> x4, local copies, waits for them, and re-layouts: 9.61 us -> 9.89 us  [on_device(): sends[d] = lax.dynamic_slice_in_dim(raw, to * levels + q * nl, nl, 1)]
  transfers between devices with their start and end apart: 70 -> 70, of which waited for: 17 -> 13; matrix products, arithmetic and copies ran while one was open for 7% -> 8% of each run, Pallas kernels for 26% -> 25%
where the time goes in v3:
time: 446 us; the launch traced here: 444 us
  starting transfers between devices  240 us (54%)
  Pallas kernels  118 us (26%)
  waiting for transfers between devices  42.9 us (10%)
  local copies, waits for them, and re-layouts  24 us (5%)
  other arithmetic  14.5 us (3%)
    ppermute x66, starting transfers between devices, around(): lax.ppermute(block, axis, [(i, (i + distance) % count) for i in range(cou...  231 us
    pallas_call x4, Pallas kernels, react_chunk(): pl.pallas_call(functools.partial(react_kernel, n, nl, q, closing), grid_s...  75.9 us
    ppermute x66, waiting for transfers between devices, around(): lax.ppermute(block, axis, [(i, (i + distance) % count) for i in range(cou...  42.9 us
    pallas_call x6, Pallas kernels, unpack_chunk(): pl.pallas_call(functools.partial(unpack_kernel, n, taken, nl, cap, q * nl...  31.9 us
    dynamic_slice x4, local copies, waits for them, and re-layouts, on_device(): sends[d] = lax.dynamic_slice_in_dim(raw, to * levels + q * nl, nl, 1)  9.89 us
    pallas_call x4, Pallas kernels, chunk_edges(): pl.pallas_call(functools.partial(edges_kernel, n, level, turn), in_specs=...  9.75 us
  transfers between devices with their start and end apart: 70, of which 13 were waited for; matrix products, arithmetic and copies ran while one was open for 8% of the time, Pallas kernels for 25%

profile of v3, /device:TPU:0, one launch (start us, length us, event | category | flops | bytes accessed | tf_op | source)
XLA Modules:
  0.0 444.2 jit_solution(8172626528187628665)
XLA Ops:
  28.4 4.3 constant_dynamic-slice_fusion
  47.9 11.9 %collective-permute-done.3.refs_4_.refs_15_.refs_7_ = f32[4,4,16,256]{3,2,1,0:T(8,128)S(1)} collective-permute-done((f32[4,4,16,256]{3,2,1,0:T(8,128)}, f32[4,4,16,256]{3,2,1,0:T(8,128)S(1)}, u32[]{:S(2)}, u32[]{:S(2)}) %collective-permute-start.3) | collective-permute-done | bytes 262176 | tf_op jit(solution)/shard_map/ppermute | solution.py:32
  59.8 10.8 %collective-permute-start.8 = (f32[4,4,16,256]{3,2,1,0:T(8,128)S(1)}, f32[4,4,16,256]{3,2,1,0:T(8,128)S(1)}, u32[]{:S(2)}, u32[]{:S(2)}) collective-permute-start(f32[4,4,16,256]{3,2,1,0:T(8,128)S(1)} %get-tuple-element.154), channel_id=1, source_target_pairs={{0,2},{1,3},{2,4},{3,5},{4,6},{5,7},{6,0},{7,1},{8,10},{9,11},{10,... | collective-permute-start | bytes 786440 | tf_op jit(solution)/shard_map/ppermute | solution.py:32
  70.6 14.0 %collective-permute-start.10 = (f32[4,4,16,256]{3,2,1,0:T(8,128)S(1)}, f32[4,4,16,256]{3,2,1,0:T(8,128)S(1)}, u32[]{:S(2)}, u32[]{:S(2)}) collective-permute-start(f32[4,4,16,256]{3,2,1,0:T(8,128)S(1)} %get-tuple-element.152), channel_id=1, source_target_pairs={{0,4},{1,5},{2,6},{3,7},{4,0},{5,1},{6,2},{7,3},{8,12},{9,13},{10,... | collective-permute-start | bytes 786440 | tf_op jit(solution)/shard_map/ppermute | solution.py:32
  84.6 14.0 %collective-permute-start.12 = (f32[4,4,16,256]{3,2,1,0:T(8,128)S(1)}, f32[4,4,16,256]{3,2,1,0:T(8,128)S(1)}, u32[]{:S(2)}, u32[]{:S(2)}) collective-permute-start(f32[4,4,16,256]{3,2,1,0:T(8,128)S(1)} %get-tuple-element.150), channel_id=1, source_target_pairs={{0,6},{1,7},{2,0},{3,1},{4,2},{5,3},{6,4},{7,5},{8,14},{9,15},{10,... | collective-permute-start | bytes 786440 | tf_op jit(solution)/shard_map/ppermute | solution.py:32
  99.4 4.3 collective-permute-done.10.refs_4_.refs_23_.refs_7_
  103.7 11.7 %collective-permute-start.16 = (f32[4,4,16,256]{3,2,1,0:T(8,128)}, f32[4,4,16,256]{3,2,1,0:T(8,128)}, u32[]{:S(2)}, u32[]{:S(2)}) collective-permute-start(f32[4,4,16,256]{3,2,1,0:T(8,128)} %get-tuple-element.146), channel_id=1, source_target_pairs={{0,2},{1,3},{2,4},{3,5},{4,6},{5,7},{6,0},{7,1},{8,10},{9,11},{10,... | collective-permute-start | bytes 786440 | tf_op jit(solution)/shard_map/ppermute | solution.py:32
  115.5 14.1 %collective-permute-start.18 = (f32[4,4,16,256]{3,2,1,0:T(8,128)}, f32[4,4,16,256]{3,2,1,0:T(8,128)}, u32[]{:S(2)}, u32[]{:S(2)}) collective-permute-start(f32[4,4,16,256]{3,2,1,0:T(8,128)} %get-tuple-element.144), channel_id=1, source_target_pairs={{0,4},{1,5},{2,6},{3,7},{4,0},{5,1},{6,2},{7,3},{8,12},{9,13},{10,... | collective-permute-start | bytes 786440 | tf_op jit(solution)/shard_map/ppermute | solution.py:32
  131.3 12.4 %collective-permute-start.20 = (f32[4,4,16,256]{3,2,1,0:T(8,128)}, f32[4,4,16,256]{3,2,1,0:T(8,128)S(1)}, u32[]{:S(2)}, u32[]{:S(2)}) collective-permute-start(f32[4,4,16,256]{3,2,1,0:T(8,128)} %get-tuple-element.142), channel_id=1, source_target_pairs={{0,6},{1,7},{2,0},{3,1},{4,2},{5,3},{6,4},{7,5},{8,14},{9,15},{10,... | collective-permute-start | bytes 786440 | tf_op jit(solution)/shard_map/ppermute | solution.py:32
  144.3 4.2 collective-permute-done.18.refs_4_.refs_7_.refs_15_.refs_23_
  148.5 12.0 %collective-permute-start.27 = (f32[4,4,16,256]{3,2,1,0:T(8,128)}, f32[4,4,16,256]{3,2,1,0:T(8,128)S(1)}, u32[]{:S(2)}, u32[]{:S(2)}) collective-permute-start(f32[4,4,16,256]{3,2,1,0:T(8,128)} %get-tuple-element.138), channel_id=1, source_target_pairs={{0,2},{1,3},{2,4},{3,5},{4,6},{5,7},{6,0},{7,1},{8,10},{9,11},{10,... | collective-permute-start | bytes 786440 | tf_op jit(solution)/shard_map/ppermute | solution.py:32
  163.4 11.3 %collective-permute-start.29 = (f32[4,4,16,256]{3,2,1,0:T(8,128)}, f32[4,4,16,256]{3,2,1,0:T(8,128)S(1)}, u32[]{:S(2)}, u32[]{:S(2)}) collective-permute-start(f32[4,4,16,256]{3,2,1,0:T(8,128)} %get-tuple-element.136), channel_id=1, source_target_pairs={{0,4},{1,5},{2,6},{3,7},{4,0},{5,1},{6,2},{7,3},{8,12},{9,13},{10,... | collective-permute-start | bytes 786440 | tf_op jit(solution)/shard_map/ppermute | solution.py:32
  174.7 13.9 %collective-permute-start.31 = (f32[4,4,16,256]{3,2,1,0:T(8,128)S(1)}, f32[4,4,16,256]{3,2,1,0:T(8,128)}, u32[]{:S(2)}, u32[]{:S(2)}) collective-permute-start(f32[4,4,16,256]{3,2,1,0:T(8,128)S(1)} %get-tuple-element.134), channel_id=1, source_target_pairs={{0,6},{1,7},{2,0},{3,1},{4,2},{5,3},{6,4},{7,5},{8,14},{9,15},{10,... | collective-permute-start | bytes 786440 | tf_op jit(solution)/shard_map/ppermute | solution.py:32
  210.0 19.0 %react.4 = (f32[16,3072]{1,0:T(8,128)}, f32[16,3072]{1,0:T(8,128)}, f32[16,3072]{1,0:T(8,128)}, f32[16,3072]{1,0:T(8,128)}, f32[16,3072]{1,0:T(8,128)}, /*index=...) custom-call(s32[1]{0:T(128)} %bitcast.refs_0_, ...), custom_call_target="tpu_custom_call" | custom-call | flops 3221225472 | bytes 6291456 | tf_op jit(solution)/shard_map/react/pallas_call | solution.py:246
  232.4 19.0 %react.5 = (f32[16,3072]{1,0:T(8,128)}, f32[16,3072]{1,0:T(8,128)}, f32[16,3072]{1,0:T(8,128)}, f32[16,3072]{1,0:T(8,128)}, f32[16,3072]{1,0:T(8,128)}, /*index=...) custom-call(s32[1]{0:T(128)} %bitcast.refs_0_, ...), custom_call_target="tpu_custom_call" | custom-call | flops 3221225472 | bytes 6291456 | tf_op jit(solution)/shard_map/react/pallas_call | solution.py:246
  251.4 14.2 %collective-permute-start.56 = (f32[16,3072]{1,0:T(8,128)}, f32[16,3072]{1,0:T(8,128)S(1)}, u32[]{:S(2)}, u32[]{:S(2)}) collective-permute-start(f32[16,3072]{1,0:T(8,128)} %get-tuple-element.109), channel_id=1, source_target_pairs={{0,7},{1,0},{2,1},{3,2},{4,3},{5,4},{6,5},{7,6},{8,15},{9,8},{10,9... | collective-permute-start | bytes 589832 | tf_op jit(solution)/shard_map/ppermute | solution.py:32
  271.3 4.2 collective-permute-done.57.refs_4_
  275.5 4.2 collective-permute-done.58.refs_5_
  279.7 12.1 %collective-permute-start.62 = (f32[16,3072]{1,0:T(8,128)}, f32[16,3072]{1,0:T(8,128)S(1)}, u32[]{:S(2)}, u32[]{:S(2)}) collective-permute-start(f32[16,3072]{1,0:T(8,128)} %get-tuple-element.115), channel_id=1, source_target_pairs={{0,1},{1,2},{2,3},{3,4},{4,5},{5,6},{6,7},{7,0},{8,9},{9,10},{10,1... | collective-permute-start | bytes 589832 | tf_op jit(solution)/shard_map/ppermute | solution.py:32
  291.8 6.5 %collective-permute-done.59.refs_6_ = f32[16,3072]{1,0:T(8,128)S(1)} collective-permute-done((f32[16,3072]{1,0:T(8,128)}, f32[16,3072]{1,0:T(8,128)S(1)}, u32[]{:S(2)}, u32[]{:S(2)}) %collective-permute-start.59) | collective-permute-done | bytes 196640 | tf_op jit(solution)/shard_map/ppermute | solution.py:32
  307.2 18.9 %react.6 = (f32[16,3072]{1,0:T(8,128)}, f32[16,3072]{1,0:T(8,128)}, f32[16,3072]{1,0:T(8,128)}, f32[16,3072]{1,0:T(8,128)}, f32[16,3072]{1,0:T(8,128)}, /*index=...) custom-call(s32[1]{0:T(128)} %bitcast.refs_0_, ...), custom_call_target="tpu_custom_call" | custom-call | flops 3221225472 | bytes 6291456 | tf_op jit(solution)/shard_map/react/pallas_call | solution.py:246
  329.4 5.9 %collective-permute-start.49 = (f32[16,3072]{1,0:T(8,128)}, f32[16,3072]{1,0:T(8,128)S(1)}, u32[]{:S(2)}, u32[]{:S(2)}) collective-permute-start(f32[16,3072]{1,0:T(8,128)} %get-tuple-element.101), channel_id=1, source_target_pairs={{0,7},{1,0},{2,1},{3,2},{4,3},{5,4},{6,5},{7,6},{8,15},{9,8},{10,9... | collective-permute-start | bytes 589832 | tf_op jit(solution)/shard_map/ppermute | solution.py:32
  336.0 4.3 collective-permute-start.50
  340.4 6.8 %collective-permute-start.51 = (f32[16,3072]{1,0:T(8,128)}, f32[16,3072]{1,0:T(8,128)S(1)}, u32[]{:S(2)}, u32[]{:S(2)}) collective-permute-start(f32[16,3072]{1,0:T(8,128)} %get-tuple-element.103), channel_id=1, source_target_pairs={{0,5},{1,6},{2,7},{3,0},{4,1},{5,2},{6,3},{7,4},{8,13},{9,14},{10,... | collective-permute-start | bytes 589832 | tf_op jit(solution)/shard_map/ppermute | solution.py:32
  347.2 11.1 %collective-permute-start.52 = (f32[16,3072]{1,0:T(8,128)}, f32[16,3072]{1,0:T(8,128)}, u32[]{:S(2)}, u32[]{:S(2)}) collective-permute-start(f32[16,3072]{1,0:T(8,128)} %get-tuple-element.104), channel_id=1, source_target_pairs={{0,4},{1,5},{2,6},{3,7},{4,0},{5,1},{6,2},{7,3},{8,12},{9,13},{10,... | collective-permute-start | bytes 589832 | tf_op jit(solution)/shard_map/ppermute | solution.py:32
  358.8 19.0 %react.7 = (f32[16,3328]{1,0:T(8,128)}, f32[16,3328]{1,0:T(8,128)}, f32[16,3328]{1,0:T(8,128)}, f32[16,3328]{1,0:T(8,128)}, f32[16,3328]{1,0:T(8,128)}, /*index=...) custom-call(s32[1]{0:T(128)} %bitcast.refs_0_, ...), custom_call_target="tpu_custom_call" | custom-call | flops 3221225472 | bytes 6291456 | tf_op jit(solution)/shard_map/react/pallas_call | solution.py:246
  387.6 18.2 %collective-permute-start.40 = (f32[16,3328]{1,0:T(8,128)}, f32[16,3328]{1,0:T(8,128)S(1)}, u32[]{:S(2)}, u32[]{:S(2)}) collective-permute-start(f32[16,3328]{1,0:T(8,128)} %get-tuple-element.88), channel_id=1, source_target_pairs={{0,7},{1,0},{2,1},{3,2},{4,3},{5,4},{6,5},{7,6},{8,15},{9,8},{10,9... | collective-permute-start | bytes 638984 | tf_op jit(solution)/shard_map/ppermute | solution.py:32
  408.4 6.1 %unpack.6.refs_14_ = f32[4,128,16,256]{3,2,1,0:T(8,128)} custom-call(s32[1]{0:T(128)} %bitcast.refs_0_, s32[32]{0:T(128)} %and_select_fusion.3.refs_1_, f32[16,3072]{1,0:T(8,128)} %get-tuple-element.116.refs_2_, f32[16,3072]{1,0:T(8,128)} %copy-done.37, f32[16,3072]{1,0:T(8,128)} %copy-done.38, f32[16,3072]{1,0:T(8,128)} %copy-done.39, ...), custom_call_target="tpu_custom_call" | custom-call | flops 209715200 | bytes 6291456 | tf_op jit(solution)/shard_map/unpack/pallas_call | solution.py:399
  414.6 6.2 %unpack.7.refs_14_ = f32[4,128,16,256]{3,2,1,0:T(8,128)} custom-call(s32[1]{0:T(128)} %bitcast.refs_0_, s32[32]{0:T(128)} %and_select_fusion.3.refs_1_, f32[16,3072]{1,0:T(8,128)} %get-tuple-element.108.refs_2_, f32[16,3072]{1,0:T(8,128)} %copy-done.30, f32[16,3072]{1,0:T(8,128)} %copy-done.31, ...), custom_call_target="tpu_custom_call", output_to_operand_aliasing={{}: (14, {})} | custom-call | flops 209715200 | bytes 6291456 | tf_op jit(solution)/shard_map/unpack/pallas_call | solution.py:399
  421.6 6.1 %unpack.8.refs_10_ = f32[4,128,16,256]{3,2,1,0:T(8,128)} custom-call(s32[1]{0:T(128)} %bitcast.refs_0_, s32[32]{0:T(128)} %and_select_fusion.3.refs_1_, f32[16,3072]{1,0:T(8,128)} %get-tuple-element.100.refs_2_, f32[16,3072]{1,0:T(8,128)} %copy-done.42, f32[16,3072]{1,0:T(8,128)} %collective-permute-done.50.refs_4_, ...), custom_call_target="tpu_custom_call", output_to_operand_aliasing={{}: (14, {})} | custom-call | flops 209715200 | bytes 6291456 | tf_op jit(solution)/shard_map/unpack/pallas_call | solution.py:399
  428.4 4.6 %unpack.9.refs_8_ = f32[4,128,16,256]{3,2,1,0:T(8,128)} custom-call(s32[1]{0:T(128)} %bitcast.refs_0_, s32[32]{0:T(128)} %and_select_fusion.3.refs_1_, f32[16,3328]{1,0:T(8,128)} %get-tuple-element.99.refs_2_, f32[16,3328]{1,0:T(8,128)} %copy-done.8, f32[16,3328]{1,0:T(8,128)} %copy-done.7, f32[16,3328]{1,0:T(8,128)} %copy-done.10, ...), custom_call_target="tpu_custom_call", output_to_operand_aliasing={{}: (10, {})} | custom-call | flops 209715200 | bytes 6291456 | tf_op jit(solution)/shard_map/unpack/pallas_call | solution.py:399
  439.0 5.0 %unpack.11 = (f32[4,128,16,256]{3,2,1,0:T(8,128)}, f32[16,16,256]{2,1,0:T(8,128)}) custom-call(s32[1]{0:T(128)} %bitcast.refs_0_, s32[32]{0:T(128)} %and_select_fusion.3.refs_1_, f32[16,3328]{1,0:T(8,128)} %copy-done.5, f32[16,3328]{1,0:T(8,128)} %copy-done.6, f32[4,128,16,256]{3,2,1,0:T(8,128)} %refs_4_.3, ...), custom_call_target="tpu_custom_call", output_to_operand_aliasing={{0}: (18, {})} | custom-call | flops 209715200 | bytes 6291456 | tf_op jit(solution)/shard_map/unpack/pallas_call | solution.py:399
  (328 shorter events, 111.8 us)
Async XLA Ops:
  3.9 40.3 %collective-permute-start = (f32[4,4,16,256]{3,2,1,0:T(8,128)S(1)}, f32[4,4,16,256]{3,2,1,0:T(8,128)}, u32[]{:S(2)}, u32[]{:S(2)}) collective-permute-start(f32[4,4,16,256]{3,2,1,0:T(8,128)S(1)} %get-tuple-element.68), channel_id=1, source_target_pairs={{0,1},{1,2},{2,3},{3,4},{4,5},{5,6},{6,7},{7,0},{8,9},{9,10},{10,1... | collective-permute-start | bytes 786440 | tf_op jit(solution)/shard_map/ppermute | solution.py:32
  4.4 41.2 %collective-permute-start.1 = (f32[4,4,16,256]{3,2,1,0:T(8,128)S(1)}, f32[4,4,16,256]{3,2,1,0:T(8,128)}, u32[]{:S(2)}, u32[]{:S(2)}) collective-permute-start(f32[4,4,16,256]{3,2,1,0:T(8,128)S(1)} %get-tuple-element.69), channel_id=1, source_target_pairs={{0,2},{1,3},{2,4},{3,5},{4,6},{5,7},{6,0},{7,1},{8,10},{9,11},{10,... | collective-permute-start | bytes 786440 | tf_op jit(solution)/shard_map/ppermute | solution.py:32
  7.0 39.9 %collective-permute-start.2 = (f32[4,4,16,256]{3,2,1,0:T(8,128)S(1)}, f32[4,4,16,256]{3,2,1,0:T(8,128)}, u32[]{:S(2)}, u32[]{:S(2)}) collective-permute-start(f32[4,4,16,256]{3,2,1,0:T(8,128)S(1)} %get-tuple-element.70), channel_id=1, source_target_pairs={{0,3},{1,4},{2,5},{3,6},{4,7},{5,0},{6,1},{7,2},{8,11},{9,12},{10,... | collective-permute-start | bytes 786440 | tf_op jit(solution)/shard_map/ppermute | solution.py:32
  45.6 39.0 %collective-permute-start.6 = (f32[4,4,16,256]{3,2,1,0:T(8,128)S(1)}, f32[4,4,16,256]{3,2,1,0:T(8,128)S(1)}, u32[]{:S(2)}, u32[]{:S(2)}) collective-permute-start(f32[4,4,16,256]{3,2,1,0:T(8,128)S(1)} %get-tuple-element.74), channel_id=1, source_target_pairs={{0,7},{1,0},{2,1},{3,2},{4,3},{5,4},{6,5},{7,6},{8,15},{9,8},{10,9... | collective-permute-start | bytes 786440 | tf_op jit(solution)/shard_map/ppermute | solution.py:32
  47.0 37.6 %collective-permute-start.7 = (f32[4,4,16,256]{3,2,1,0:T(8,128)S(1)}, f32[4,4,16,256]{3,2,1,0:T(8,128)S(1)}, u32[]{:S(2)}, u32[]{:S(2)}) collective-permute-start(f32[4,4,16,256]{3,2,1,0:T(8,128)S(1)} %get-tuple-element.155), channel_id=1, source_target_pairs={{0,1},{1,2},{2,3},{3,4},{4,5},{5,6},{6,7},{7,0},{8,9},{9,10},{10,1... | collective-permute-start | bytes 786440 | tf_op jit(solution)/shard_map/ppermute | solution.py:32
  59.8 39.1 %collective-permute-start.8 = (f32[4,4,16,256]{3,2,1,0:T(8,128)S(1)}, f32[4,4,16,256]{3,2,1,0:T(8,128)S(1)}, u32[]{:S(2)}, u32[]{:S(2)}) collective-permute-start(f32[4,4,16,256]{3,2,1,0:T(8,128)S(1)} %get-tuple-element.154), channel_id=1, source_target_pairs={{0,2},{1,3},{2,4},{3,5},{4,6},{5,7},{6,0},{7,1},{8,10},{9,11},{10,... | collective-permute-start | bytes 786440 | tf_op jit(solution)/shard_map/ppermute | solution.py:32
  70.6 33.1 %collective-permute-start.10 = (f32[4,4,16,256]{3,2,1,0:T(8,128)S(1)}, f32[4,4,16,256]{3,2,1,0:T(8,128)S(1)}, u32[]{:S(2)}, u32[]{:S(2)}) collective-permute-start(f32[4,4,16,256]{3,2,1,0:T(8,128)S(1)} %get-tuple-element.152), channel_id=1, source_target_pairs={{0,4},{1,5},{2,6},{3,7},{4,0},{5,1},{6,2},{7,3},{8,12},{9,13},{10,... | collective-permute-start | bytes 786440 | tf_op jit(solution)/shard_map/ppermute | solution.py:32
  84.6 30.8 %collective-permute-start.11 = (f32[4,4,16,256]{3,2,1,0:T(8,128)S(1)}, f32[4,4,16,256]{3,2,1,0:T(8,128)S(1)}, u32[]{:S(2)}, u32[]{:S(2)}) collective-permute-start(f32[4,4,16,256]{3,2,1,0:T(8,128)S(1)} %get-tuple-element.151), channel_id=1, source_target_pairs={{0,5},{1,6},{2,7},{3,0},{4,1},{5,2},{6,3},{7,4},{8,13},{9,14},{10,... | collective-permute-start | bytes 786440 | tf_op jit(solution)/shard_map/ppermute | solution.py:32
  84.6 30.8 %collective-permute-start.12 = (f32[4,4,16,256]{3,2,1,0:T(8,128)S(1)}, f32[4,4,16,256]{3,2,1,0:T(8,128)S(1)}, u32[]{:S(2)}, u32[]{:S(2)}) collective-permute-start(f32[4,4,16,256]{3,2,1,0:T(8,128)S(1)} %get-tuple-element.150), channel_id=1, source_target_pairs={{0,6},{1,7},{2,0},{3,1},{4,2},{5,3},{6,4},{7,5},{8,14},{9,15},{10,... | collective-permute-start | bytes 786440 | tf_op jit(solution)/shard_map/ppermute | solution.py:32
  98.9 32.2 %collective-permute-start.13 = (f32[4,4,16,256]{3,2,1,0:T(8,128)}, f32[4,4,16,256]{3,2,1,0:T(8,128)}, u32[]{:S(2)}, u32[]{:S(2)}) collective-permute-start(f32[4,4,16,256]{3,2,1,0:T(8,128)} %get-tuple-element.149), channel_id=1, source_target_pairs={{0,7},{1,0},{2,1},{3,2},{4,3},{5,4},{6,5},{7,6},{8,15},{9,8},{10,9... | collective-permute-start | bytes 786440 | tf_op jit(solution)/shard_map/ppermute | solution.py:32
  99.0 32.4 %collective-permute-start.15 = (f32[4,4,16,256]{3,2,1,0:T(8,128)}, f32[4,4,16,256]{3,2,1,0:T(8,128)}, u32[]{:S(2)}, u32[]{:S(2)}) collective-permute-start(f32[4,4,16,256]{3,2,1,0:T(8,128)} %get-tuple-element.147), channel_id=1, source_target_pairs={{0,1},{1,2},{2,3},{3,4},{4,5},{5,6},{6,7},{7,0},{8,9},{9,10},{10,1... | collective-permute-start | bytes 786440 | tf_op jit(solution)/shard_map/ppermute | solution.py:32
  103.7 40.0 %collective-permute-start.16 = (f32[4,4,16,256]{3,2,1,0:T(8,128)}, f32[4,4,16,256]{3,2,1,0:T(8,128)}, u32[]{:S(2)}, u32[]{:S(2)}) collective-permute-start(f32[4,4,16,256]{3,2,1,0:T(8,128)} %get-tuple-element.146), channel_id=1, source_target_pairs={{0,2},{1,3},{2,4},{3,5},{4,6},{5,7},{6,0},{7,1},{8,10},{9,11},{10,... | collective-permute-start | bytes 786440 | tf_op jit(solution)/shard_map/ppermute | solution.py:32
  115.5 33.0 %collective-permute-start.18 = (f32[4,4,16,256]{3,2,1,0:T(8,128)}, f32[4,4,16,256]{3,2,1,0:T(8,128)}, u32[]{:S(2)}, u32[]{:S(2)}) collective-permute-start(f32[4,4,16,256]{3,2,1,0:T(8,128)} %get-tuple-element.144), channel_id=1, source_target_pairs={{0,4},{1,5},{2,6},{3,7},{4,0},{5,1},{6,2},{7,3},{8,12},{9,13},{10,... | collective-permute-start | bytes 786440 | tf_op jit(solution)/shard_map/ppermute | solution.py:32
  131.0 32.3 %collective-permute-start.19 = (f32[4,4,16,256]{3,2,1,0:T(8,128)}, f32[4,4,16,256]{3,2,1,0:T(8,128)S(1)}, u32[]{:S(2)}, u32[]{:S(2)}) collective-permute-start(f32[4,4,16,256]{3,2,1,0:T(8,128)} %get-tuple-element.143), channel_id=1, source_target_pairs={{0,5},{1,6},{2,7},{3,0},{4,1},{5,2},{6,3},{7,4},{8,13},{9,14},{10,... | collective-permute-start | bytes 786440 | tf_op jit(solution)/shard_map/ppermute | solution.py:32
  131.3 32.0 %collective-permute-start.20 = (f32[4,4,16,256]{3,2,1,0:T(8,128)}, f32[4,4,16,256]{3,2,1,0:T(8,128)S(1)}, u32[]{:S(2)}, u32[]{:S(2)}) collective-permute-start(f32[4,4,16,256]{3,2,1,0:T(8,128)} %get-tuple-element.142), channel_id=1, source_target_pairs={{0,6},{1,7},{2,0},{3,1},{4,2},{5,3},{6,4},{7,5},{8,14},{9,15},{10,... | collective-permute-start | bytes 786440 | tf_op jit(solution)/shard_map/ppermute | solution.py:32
  143.7 30.9 %collective-permute-start.21 = (f32[4,4,16,256]{3,2,1,0:T(8,128)}, f32[4,4,16,256]{3,2,1,0:T(8,128)S(1)}, u32[]{:S(2)}, u32[]{:S(2)}) collective-permute-start(f32[4,4,16,256]{3,2,1,0:T(8,128)} %get-tuple-element.141), channel_id=1, source_target_pairs={{0,7},{1,0},{2,1},{3,2},{4,3},{5,4},{6,5},{7,6},{8,15},{9,8},{10,9... | collective-permute-start | bytes 786440 | tf_op jit(solution)/shard_map/ppermute | solution.py:32
  143.8 30.9 %collective-permute-start.26 = (f32[4,4,16,256]{3,2,1,0:T(8,128)}, f32[4,4,16,256]{3,2,1,0:T(8,128)S(1)}, u32[]{:S(2)}, u32[]{:S(2)}) collective-permute-start(f32[4,4,16,256]{3,2,1,0:T(8,128)} %get-tuple-element.139), channel_id=1, source_target_pairs={{0,1},{1,2},{2,3},{3,4},{4,5},{5,6},{6,7},{7,0},{8,9},{9,10},{10,1... | collective-permute-start | bytes 786440 | tf_op jit(solution)/shard_map/ppermute | solution.py:32
  148.5 40.1 %collective-permute-start.27 = (f32[4,4,16,256]{3,2,1,0:T(8,128)}, f32[4,4,16,256]{3,2,1,0:T(8,128)S(1)}, u32[]{:S(2)}, u32[]{:S(2)}) collective-permute-start(f32[4,4,16,256]{3,2,1,0:T(8,128)} %get-tuple-element.138), channel_id=1, source_target_pairs={{0,2},{1,3},{2,4},{3,5},{4,6},{5,7},{6,0},{7,1},{8,10},{9,11},{10,... | collective-permute-start | bytes 786440 | tf_op jit(solution)/shard_map/ppermute | solution.py:32
  200.1 51.3 %collective-permute-start.22 = (f32[128,256]{1,0:T(8,128)}, f32[128,256]{1,0:T(8,128)S(1)}, u32[]{:S(2)}, u32[]{:S(2)}) collective-permute-start(f32[128,256]{1,0:T(8,128)} %get-tuple-element.76), channel_id=1, source_target_pairs={{0,24},{8,0},{16,8},{24,16},{1,25},{9,1},{17,9},{25,17},{2,26},{10... | collective-permute-start | bytes 393224 | tf_op jit(solution)/shard_map/ppermute | solution.py:32
  202.4 63.2 %collective-permute-start.23 = (f32[128,256]{1,0:T(8,128)}, f32[128,256]{1,0:T(8,128)S(1)}, u32[]{:S(2)}, u32[]{:S(2)}) collective-permute-start(f32[128,256]{1,0:T(8,128)} %get-tuple-element.77), channel_id=1, source_target_pairs={{0,8},{8,16},{16,24},{24,0},{1,9},{9,17},{17,25},{25,1},{2,10},{10... | collective-permute-start | bytes 393224 | tf_op jit(solution)/shard_map/ppermute | solution.py:32
  202.6 103.3 %collective-permute-start.33 = (f32[32,1,16,256]{3,2,1,0:T(8,128)}, f32[32,1,16,256]{3,2,1,0:T(8,128)}, u32[]{:S(2)}, u32[]{:S(2)}) collective-permute-start(f32[32,1,16,256]{3,2,1,0:T(8,128)} %get-tuple-element.78), channel_id=1, source_target_pairs={{1,0},{2,1},{3,2},{4,3},{5,4},{6,5},{7,6},{9,8},{10,9},{11,10},{12... | collective-permute-start | bytes 1572872 | tf_op jit(solution)/shard_map/ppermute | solution.py:27
  229.1 36.6 %collective-permute-start.34 = (f32[128,256]{1,0:T(8,128)S(1)}, f32[128,256]{1,0:T(8,128)S(1)}, u32[]{:S(2)}, u32[]{:S(2)}) collective-permute-start(f32[128,256]{1,0:T(8,128)S(1)} %copy-done.63), channel_id=1, source_target_pairs={{0,24},{8,0},{16,8},{24,16},{1,25},{9,1},{17,9},{25,17},{2,26},{10... | collective-permute-start | bytes 393224 | tf_op jit(solution)/shard_map/ppermute | solution.py:32
  231.8 34.0 %collective-permute-start.35 = (f32[128,256]{1,0:T(8,128)S(1)}, f32[128,256]{1,0:T(8,128)S(1)}, u32[]{:S(2)}, u32[]{:S(2)}) collective-permute-start(f32[128,256]{1,0:T(8,128)S(1)} %copy-done.62), channel_id=1, source_target_pairs={{0,8},{8,16},{16,24},{24,0},{1,9},{9,17},{17,25},{25,1},{2,10},{10... | collective-permute-start | bytes 393224 | tf_op jit(solution)/shard_map/ppermute | solution.py:32
  266.9 31.4 %collective-permute-start.59 = (f32[16,3072]{1,0:T(8,128)}, f32[16,3072]{1,0:T(8,128)S(1)}, u32[]{:S(2)}, u32[]{:S(2)}) collective-permute-start(f32[16,3072]{1,0:T(8,128)} %get-tuple-element.112), channel_id=1, source_target_pairs={{0,4},{1,5},{2,6},{3,7},{4,0},{5,1},{6,2},{7,3},{8,12},{9,13},{10,... | collective-permute-start | bytes 589832 | tf_op jit(solution)/shard_map/ppermute | solution.py:32
  299.1 59.2 %collective-permute-start.14 = (f32[32,1,16,256]{3,2,1,0:T(8,128)}, f32[32,1,16,256]{3,2,1,0:T(8,128)}, u32[]{:S(2)}, u32[]{:S(2)}) collective-permute-start(f32[32,1,16,256]{3,2,1,0:T(8,128)} %get-tuple-element.75), channel_id=1, source_target_pairs={{0,1},{1,2},{2,3},{3,4},{4,5},{5,6},{6,7},{8,9},{9,10},{10,11},{11... | collective-permute-start | bytes 1572872 | tf_op jit(solution)/shard_map/ppermute | solution.py:27
  340.4 37.5 %collective-permute-start.51 = (f32[16,3072]{1,0:T(8,128)}, f32[16,3072]{1,0:T(8,128)S(1)}, u32[]{:S(2)}, u32[]{:S(2)}) collective-permute-start(f32[16,3072]{1,0:T(8,128)} %get-tuple-element.103), channel_id=1, source_target_pairs={{0,5},{1,6},{2,7},{3,0},{4,1},{5,2},{6,3},{7,4},{8,13},{9,14},{10,... | collective-permute-start | bytes 589832 | tf_op jit(solution)/shard_map/ppermute | solution.py:32
  347.2 34.5 %collective-permute-start.52 = (f32[16,3072]{1,0:T(8,128)}, f32[16,3072]{1,0:T(8,128)}, u32[]{:S(2)}, u32[]{:S(2)}) collective-permute-start(f32[16,3072]{1,0:T(8,128)} %get-tuple-element.104), channel_id=1, source_target_pairs={{0,4},{1,5},{2,6},{3,7},{4,0},{5,1},{6,2},{7,3},{8,12},{9,13},{10,... | collective-permute-start | bytes 589832 | tf_op jit(solution)/shard_map/ppermute | solution.py:32
  382.6 50.4 %collective-permute-start.42 = (f32[16,3328]{1,0:T(8,128)}, f32[16,3328]{1,0:T(8,128)S(1)}, u32[]{:S(2)}, u32[]{:S(2)}) collective-permute-start(f32[16,3328]{1,0:T(8,128)} %get-tuple-element.90), channel_id=1, source_target_pairs={{0,6},{1,7},{2,0},{3,1},{4,2},{5,3},{6,4},{7,5},{8,14},{9,15},{10,... | collective-permute-start | bytes 638984 | tf_op jit(solution)/shard_map/ppermute | solution.py:32
  385.2 42.5 %collective-permute-start.45 = (f32[16,3328]{1,0:T(8,128)}, f32[16,3328]{1,0:T(8,128)S(1)}, u32[]{:S(2)}, u32[]{:S(2)}) collective-permute-start(f32[16,3328]{1,0:T(8,128)} %get-tuple-element.93), channel_id=1, source_target_pairs={{0,3},{1,4},{2,5},{3,6},{4,7},{5,0},{6,1},{7,2},{8,11},{9,12},{10,... | collective-permute-start | bytes 638984 | tf_op jit(solution)/shard_map/ppermute | solution.py:32
  385.2 47.8 %collective-permute-start.46 = (f32[16,3328]{1,0:T(8,128)}, f32[16,3328]{1,0:T(8,128)S(1)}, u32[]{:S(2)}, u32[]{:S(2)}) collective-permute-start(f32[16,3328]{1,0:T(8,128)} %get-tuple-element.94), channel_id=1, source_target_pairs={{0,2},{1,3},{2,4},{3,5},{4,6},{5,7},{6,0},{7,1},{8,10},{9,11},{10,... | collective-permute-start | bytes 638984 | tf_op jit(solution)/shard_map/ppermute | solution.py:32
  387.6 50.6 %collective-permute-start.40 = (f32[16,3328]{1,0:T(8,128)}, f32[16,3328]{1,0:T(8,128)S(1)}, u32[]{:S(2)}, u32[]{:S(2)}) collective-permute-start(f32[16,3328]{1,0:T(8,128)} %get-tuple-element.88), channel_id=1, source_target_pairs={{0,7},{1,0},{2,1},{3,2},{4,3},{5,4},{6,5},{7,6},{8,15},{9,8},{10,9... | collective-permute-start | bytes 638984 | tf_op jit(solution)/shard_map/ppermute | solution.py:32
  407.9 30.4 %collective-permute-start.41 = (f32[16,3328]{1,0:T(8,128)}, f32[16,3328]{1,0:T(8,128)S(1)}, u32[]{:S(2)}, u32[]{:S(2)}) collective-permute-start(f32[16,3328]{1,0:T(8,128)} %get-tuple-element.89), channel_id=1, source_target_pairs={{0,1},{1,2},{2,3},{3,4},{4,5},{5,6},{6,7},{7,0},{8,9},{9,10},{10,1... | collective-permute-start | bytes 638984 | tf_op jit(solution)/shard_map/ppermute | solution.py:32
  (106 other events, 3345.8 us)

commit v4 on v3

--- a/solution.py
+++ b/solution.py
@@ -266,71 +266,79 @@
     )(me, tiles, shifts, *ins)
 
 
-def unpack_kernel(n, taken, nl, cap, at_level, has_base, closing, *refs):
+def unpack_kernel(n, nl, cap, at_level, has_base, closing, *refs):
     me_ref, tile_ref = refs[:2]
-    received = refs[2 : 2 + len(taken)]
-    solute, water, pick, second = refs[2 + len(taken) : 6 + len(taken)]
-    rest = refs[6 + len(taken) :]
-    if closing:
-        totals = rest[: n - 1]
-        absorb, sun, carried = rest[n - 1 : n + 2]
-        rest = rest[n + 2 :]
-    rest = rest[has_base:]
+    received = refs[2 : 2 + n]
+    solute, *small = refs[2 + n : 6 + n + 3 * closing]
+    rest = refs[6 + n + 3 * closing + has_base :]
     out, *rest = rest
     if closing:
-        warmed, *rest = rest
-    slots, water_in, spread, sems = rest
+        warmed_out, *rest = rest
+    slots, cells, spread, sems, *rest = rest
     held, depth, across, lat = solute.shape
     levels = depth // n
     pitch = across + GAP
     here = me_ref[0]
-    count = len(taken)
-
-    def place(k):
-        d = sum(jnp.where(k == j, d, 0) for j, d in enumerate(taken))
+    lanes_in = received[0].shape[1]
+    copies = [
+        pltpu.make_async_copy(source, target, sems.at[0, n + k])
+        for k, (source, target) in enumerate(zip(small, rest))
+    ]
+
+    def place(d):
         return pl.ds(lax.rem(here + d, n) * levels + at_level, nl)
 
-    def packed_in(k, source):
+    def packed_in(d, source):
         return pltpu.make_async_copy(
-            source.at[:, pl.ds(0, cap)], slots.at[k, :, pl.ds(0, cap)], sems.at[0, k]
+            source, slots.at[d, :, pl.ds(0, lanes_in)], sems.at[0, d]
         )
 
-    def block_in(k):
-        return pltpu.make_async_copy(solute.at[:, place(k)], water_in.at[k], sems.at[1, k])
-
-    def block_out(k):
-        return pltpu.make_async_copy(water_in.at[k], out.at[:, place(k)], sems.at[2, k])
-
-    for k in range(count):
-        packed_in(k, received[k]).start()
-        block_in(k).start()
+    def block_in(d):
+        return pltpu.make_async_copy(solute.at[:, place(d)], cells.at[d], sems.at[1, d])
+
+    def block_out(d):
+        return pltpu.make_async_copy(cells.at[d], out.at[:, place(d)], sems.at[2, d])
+
+    for copy in copies[:3]:
+        copy.start()
+    for d in range(n):
+        packed_in(d, received[d]).start()
+        block_in(d).start()
+    for copy in copies[3:]:
+        copy.start()
+    for copy in copies[:3]:
+        copy.wait()
+    water, pick, second = rest[:3]
     wet = water[...] > 0.5
 
-    def unpack(k, carry):
-        packed_in(k, received[0]).wait()
-        block_in(k).wait()
-        spread_block(k, tile_ref, pick, second, slots, spread, held * nl, across, lat)
+    def unpack(d, carry):
+        packed_in(d, received[0]).wait()
+        block_in(d).wait()
+        spread_block(d, tile_ref, pick, second, slots, spread, held * nl, across, lat)
         for i in range(held):
             for l in range(nl):
                 at = (i * nl + l) * pitch
                 for s in range(lat // LANES):
                     lanes = slice(s * LANES, (s + 1) * LANES)
-                    water_in[k, i, l, :, lanes] = jnp.where(
-                        wet[:, lanes], spread[s, at : at + across, :], water_in[k, i, l, :, lanes]
+                    cells[d, i, l, :, lanes] = jnp.where(
+                        wet[:, lanes], spread[s, at : at + across, :], cells[d, i, l, :, lanes]
                     )
-        block_out(k).start()
+        block_out(d).start()
         return carry
 
-    lax.fori_loop(0, count, unpack, 0)
+    lax.fori_loop(0, n, unpack, 0)
     if closing:
+        for copy in copies[3:]:
+            copy.wait()
+        absorb, sun, carried, warmed = rest[3:]
         size = held * nl
         for k in range(across // size):
-            lane = slice(k * lat, (k + 1) * lat)
+            lane = slice(cap + k * lat, cap + (k + 1) * lat)
             row = slice(k * size, (k + 1) * size)
             over = jnp.zeros((size, lat), jnp.float32)
             for d in range(1, n):
                 above = lax.rem(here + d, n) < here
-                over = over + jnp.where(above, totals[d - 1][:, lane], 0.0)
+                over = over + jnp.where(above, slots[d, :, lane], 0.0)
             light = sun[...] * (CHLOROPHYLL_WARM * water[row, :])
             coming = jnp.exp(-over)
             for l in range(absorb.shape[0]):
@@ -338,8 +346,11 @@
                 left = jnp.exp(-over)
                 warmed[l, row, :] = carried[l, row, :] + light * (coming - left)
                 coming = left
-    for k in range(count):
-        block_out(k).wait()
+        warm = pltpu.make_async_copy(warmed, warmed_out, sems.at[1, n])
+        warm.start()
+        warm.wait()
+    for d in range(n):
+        block_out(d).wait()
 
 
 def spread_block(k, tile_ref, pick, second, slots, spread, rows, across, lat):
@@ -365,51 +376,37 @@
                 )
 
 
-def unpack_chunk(
-    q, parts, me, tiles, returned, taken, solute, water, pick, second, base, cap, heat=None
-):
+def unpack_chunk(q, parts, me, tiles, returned, solute, small, base, cap, heat=()):
     n = len(returned)
     held, depth, across, lat = solute.shape
     nl = depth // n // parts
-    received = [returned[d] for d in taken]
-
-    def all_of(x):
-        return pl.BlockSpec(x.shape, lambda i, *_: (0,) * x.ndim)
-
-    apart = pl.BlockSpec(memory_space=pl.ANY)
-    ins = [*received, solute, water, pick, second]
-    specs = [apart] * (len(taken) + 1) + [all_of(water), all_of(pick), all_of(second)]
+    ins = [*returned, solute, *small, *heat]
     shapes = [jax.ShapeDtypeStruct(solute.shape, jnp.float32)]
-    outs = [apart]
-    if heat is not None:
-        width = across * lat // (held * nl)
-        for d in range(1, n):
-            ins.append(returned[d])
-            specs.append(pl.BlockSpec((held * nl, width), lambda i, *_: (0, cap // width)))
-        for x in heat:
-            ins.append(x)
-            specs.append(all_of(x))
+    scratch = [pltpu.VMEM(x.shape, x.dtype) for x in (*small, *heat)]
+    if heat:
         shapes.append(jax.ShapeDtypeStruct(heat[-1].shape, jnp.float32))
-        outs.append(all_of(heat[-1]))
+        scratch.append(scratch[-1])
     aliases = {}
     if base is not None:
         aliases = {2 + len(ins): 0}
         ins.append(base)
-        specs.append(pl.BlockSpec(memory_space=pl.ANY))
+    apart = pl.BlockSpec(memory_space=pltpu.HBM)
+    slot_lanes = max(cap + 2 * LANES, returned[0].shape[1])
     return pl.pallas_call(
         functools.partial(
-            unpack_kernel, n, taken, nl, cap, q * nl, base is not None, heat is not None
+            unpack_kernel, n, nl, cap, q * nl, base is not None, len(heat) > 0
         ),
         grid_spec=pltpu.PrefetchScalarGridSpec(
             num_scalar_prefetch=2,
             grid=(1,),
-            in_specs=specs,
-            out_specs=outs,
+            in_specs=[apart] * len(ins),
+            out_specs=[apart] * len(shapes),
             scratch_shapes=[
-                pltpu.VMEM((len(taken), held * nl, (cap // LANES + 2) * LANES), jnp.float32),
-                pltpu.VMEM((len(taken), held, nl, across, lat), jnp.float32),
+                pltpu.VMEM((n, held * nl, slot_lanes), jnp.float32),
+                pltpu.VMEM((n, held, nl, across, lat), jnp.float32),
                 pltpu.VMEM((lat // LANES, held * nl * (across + GAP), LANES), jnp.float32),
-                pltpu.SemaphoreType.DMA((3, len(taken))),
+                pltpu.SemaphoreType.DMA((3, n + len(small) + len(heat))),
+                *scratch,
             ],
         ),
         out_shape=shapes,
@@ -468,8 +465,8 @@
         for d in reach(n):
             to = lax.rem(me + d, n)
             sends[d] = lax.dynamic_slice_in_dim(raw, to * levels + q * nl, nl, 1)
-            if q == 0 and d in reach(n)[:: n - 2]:
-                raw, sends = lax.optimization_barrier((raw, sends))
+        if q == 0:
+            raw, sends = lax.optimization_barrier((raw, sends))
         blocks[q] = [lax.dynamic_slice_in_dim(raw, me * levels + q * nl, nl, 1)]
         for d in range(1, n):
             blocks[q].append(around(sends[d], "sec", d))
@@ -576,15 +573,12 @@
     absorb = jnp.concatenate([absorbs[q] for q in range(parts)], axis=0)
     sun = shortwave[None, :]
 
-    calls = [(q, tuple(range(n))) for q in order[:-1]]
-    far = [0, *reach(n)]
-    calls += [(order[-1], tuple(far[a:b])) for a, b in ((0, n // 2), (n // 2, n - 2), (n - 2, n))]
+    small = (water, spread_at, spread_later)
     solute_revised = None
-    for k, (q, taken) in enumerate(calls):
-        heat = (absorb, sun, thermal_carried) if k == len(calls) - 1 else None
+    for q in order:
+        heat = (absorb, sun, thermal_carried) if q == order[-1] else ()
         solute_revised, *thermal_revised = unpack_chunk(
-            q, parts, me_at, tiles, returned[q], taken, solute_fields, water, spread_at,
-            spread_later, solute_revised, cap, heat,
+            q, parts, me_at, tiles, returned[q], solute_fields, small, solute_revised, cap, heat
         )
     return thermal_revised[0], jnp.stack([east, north]), spreading, solute_revised
 

time: 446 us -> 425 us (0.953)
  starting transfers between devices: 240 us -> 185 us
  waiting for transfers between devices: 42.9 us -> 93.7 us
  Pallas kernels: 118 us -> 108 us
    ppermute x66, starting transfers between devices: 231 us -> 152 us  [around(): lax.ppermute(block, axis, [(i, (i + distance) % count) for i in range(cou...]
    ppermute x66, waiting for transfers between devices: 42.9 us -> 93.7 us  [around(): lax.ppermute(block, axis, [(i, (i + distance) % count) for i in range(cou...]
    ppermute x4, starting transfers between devices: 8.69 us -> 32.2 us  [shifted(): return lax.ppermute(block, axis, route)]
    pallas_call x6 -> x4, Pallas kernels: 31.9 us -> 22 us  [unpack_chunk(): pl.pallas_call(functools.partial(unpack_kernel, n, nl, cap, q * nl, base...]
    dynamic_slice x4 -> x3, local copies, waits for them, and re-layouts: 9.89 us -> 9.61 us  [on_device(): sends[d] = lax.dynamic_slice_in_dim(raw, to * levels + q * nl, nl, 1)]
  transfers between devices with their start and end apart: 70 -> 70, of which waited for: 13 -> 17; matrix products, arithmetic and copies ran while one was open for 8% -> 7% of each run, Pallas kernels for 25% -> 24%
where the time goes in v4:
time: 425 us; the launch traced here: 424 us
  starting transfers between devices  185 us (44%)
  Pallas kernels  108 us (25%)
  waiting for transfers between devices  93.7 us (22%)
  local copies, waits for them, and re-layouts  20.5 us (5%)
  other arithmetic  13 us (3%)
    ppermute x66, starting transfers between devices, around(): lax.ppermute(block, axis, [(i, (i + distance) % count) for i in range(cou...  152 us
    ppermute x66, waiting for transfers between devices, around(): lax.ppermute(block, axis, [(i, (i + distance) % count) for i in range(cou...  93.7 us
    pallas_call x4, Pallas kernels, react_chunk(): pl.pallas_call(functools.partial(react_kernel, n, nl, q, closing), grid_s...  75.9 us
    ppermute x4, starting transfers between devices, shifted(): return lax.ppermute(block, axis, route)  32.2 us
    pallas_call x4, Pallas kernels, unpack_chunk(): pl.pallas_call(functools.partial(unpack_kernel, n, nl, cap, q * nl, base...  22 us
    pallas_call x4, Pallas kernels, chunk_edges(): pl.pallas_call(functools.partial(edges_kernel, n, level, turn), in_specs=...  9.73 us
    dynamic_slice x3, local copies, waits for them, and re-layouts, on_device(): sends[d] = lax.dynamic_slice_in_dim(raw, to * levels + q * nl, nl, 1)  9.61 us
  transfers between devices with their start and end apart: 70, of which 17 were waited for; matrix products, arithmetic and copies ran while one was open for 7% of the time, Pallas kernels for 24%

profile of v4, /device:TPU:0, one launch (start us, length us, event | category | flops | bytes accessed | tf_op | source)
XLA Modules:
  0.0 423.9 jit_solution(9707017165519750957)
XLA Ops:
  12.3 4.1 collective-permute-start.24
  29.5 4.2 %constant_dynamic-slice_fusion = (f32[4,4,16,256]{3,2,1,0:T(8,128)S(1)}, f32[4,4,16,256]{3,2,1,0:T(8,128)S(1)}, f32[4,4,16,256]{3,2,1,0:T(8,128)}, f32[4,4,16,25...) fusion(f32[4,128,16,256]{3,2,1,0:T(8,128)} %refs_10_.7, ...), kind=kLoop, calls=%fused_computation.78 | loop fusion | bytes 9437256 | tf_op jit(solution)/shard_map/dynamic_slice | solution.py:467
  46.1 19.2 %collective-permute-done.2.refs_3_.refs_14_.refs_6_ = f32[4,4,16,256]{3,2,1,0:T(8,128)S(1)} collective-permute-done((f32[4,4,16,256]{3,2,1,0:T(8,128)}, f32[4,4,16,256]{3,2,1,0:T(8,128)S(1)}, u32[]{:S(2)}, u32[]{:S(2)}) %collective-permute-start.2) | collective-permute-done | bytes 262176 | tf_op jit(solution)/shard_map/ppermute | solution.py:32
  65.5 6.7 %collective-permute-start.15 = (f32[4,4,16,256]{3,2,1,0:T(8,128)S(1)}, f32[4,4,16,256]{3,2,1,0:T(8,128)S(1)}, u32[]{:S(2)}, u32[]{:S(2)}) collective-permute-start(f32[4,4,16,256]{3,2,1,0:T(8,128)S(1)} %get-tuple-element.143), channel_id=1, source_target_pairs={{0,1},{1,2},{2,3},{3,4},{4,5},{5,6},{6,7},{7,0},{8,9},{9,10},{10,1... | collective-permute-start | bytes 786440 | tf_op jit(solution)/shard_map/ppermute | solution.py:32
  72.3 11.2 %collective-permute-start.16 = (f32[4,4,16,256]{3,2,1,0:T(8,128)S(1)}, f32[4,4,16,256]{3,2,1,0:T(8,128)S(1)}, u32[]{:S(2)}, u32[]{:S(2)}) collective-permute-start(f32[4,4,16,256]{3,2,1,0:T(8,128)S(1)} %get-tuple-element.142), channel_id=1, source_target_pairs={{0,2},{1,3},{2,4},{3,5},{4,6},{5,7},{6,0},{7,1},{8,10},{9,11},{10,... | collective-permute-start | bytes 786440 | tf_op jit(solution)/shard_map/ppermute | solution.py:32
  83.6 15.4 %collective-permute-start.17 = (f32[4,4,16,256]{3,2,1,0:T(8,128)}, f32[4,4,16,256]{3,2,1,0:T(8,128)}, u32[]{:S(2)}, u32[]{:S(2)}) collective-permute-start(f32[4,4,16,256]{3,2,1,0:T(8,128)} %get-tuple-element.141), channel_id=1, source_target_pairs={{0,3},{1,4},{2,5},{3,6},{4,7},{5,0},{6,1},{7,2},{8,11},{9,12},{10,... | collective-permute-start | bytes 786440 | tf_op jit(solution)/shard_map/ppermute | solution.py:32
  106.1 10.9 %collective-permute-done.18.refs_4_.refs_7_.refs_15_.refs_23_ = f32[4,4,16,256]{3,2,1,0:T(8,128)} collective-permute-done((f32[4,4,16,256]{3,2,1,0:T(8,128)}, f32[4,4,16,256]{3,2,1,0:T(8,128)}, u32[]{:S(2)}, u32[]{:S(2)}) %collective-permute-start.18) | collective-permute-done | bytes 262176 | tf_op jit(solution)/shard_map/ppermute | solution.py:32
  117.0 14.4 %collective-permute-start.27 = (f32[4,4,16,256]{3,2,1,0:T(8,128)}, f32[4,4,16,256]{3,2,1,0:T(8,128)S(1)}, u32[]{:S(2)}, u32[]{:S(2)}) collective-permute-start(f32[4,4,16,256]{3,2,1,0:T(8,128)} %get-tuple-element.134), channel_id=1, source_target_pairs={{0,2},{1,3},{2,4},{3,5},{4,6},{5,7},{6,0},{7,1},{8,10},{9,11},{10,... | collective-permute-start | bytes 786440 | tf_op jit(solution)/shard_map/ppermute | solution.py:32
  131.3 8.4 %collective-permute-start.29 = (f32[4,4,16,256]{3,2,1,0:T(8,128)}, f32[4,4,16,256]{3,2,1,0:T(8,128)S(1)}, u32[]{:S(2)}, u32[]{:S(2)}) collective-permute-start(f32[4,4,16,256]{3,2,1,0:T(8,128)} %get-tuple-element.132), channel_id=1, source_target_pairs={{0,4},{1,5},{2,6},{3,7},{4,0},{5,1},{6,2},{7,3},{8,12},{9,13},{10,... | collective-permute-start | bytes 786440 | tf_op jit(solution)/shard_map/ppermute | solution.py:32
  142.7 12.1 %collective-permute-start.9 = (f32[4,4,16,256]{3,2,1,0:T(8,128)}, f32[4,4,16,256]{3,2,1,0:T(8,128)S(1)}, u32[]{:S(2)}, u32[]{:S(2)}) collective-permute-start(f32[4,4,16,256]{3,2,1,0:T(8,128)} %get-tuple-element.149), channel_id=1, source_target_pairs={{0,3},{1,4},{2,5},{3,6},{4,7},{5,0},{6,1},{7,2},{8,11},{9,12},{10,... | collective-permute-start | bytes 786440 | tf_op jit(solution)/shard_map/ppermute | solution.py:32
  154.8 22.1 %collective-permute-done.28.refs_3_.refs_22_.refs_6_.refs_14_ = f32[4,4,16,256]{3,2,1,0:T(8,128)S(1)} collective-permute-done((f32[4,4,16,256]{3,2,1,0:T(8,128)}, f32[4,4,16,256]{3,2,1,0:T(8,128)S(1)}, u32[]{:S(2)}, u32[]{:S(2)}) %collective-permute-start.28) | collective-permute-done | bytes 262176 | tf_op jit(solution)/shard_map/ppermute | solution.py:32
  177.1 6.0 %collective-permute-start.32 = (f32[4,4,16,256]{3,2,1,0:T(8,128)S(1)}, f32[4,4,16,256]{3,2,1,0:T(8,128)}, u32[]{:S(2)}, u32[]{:S(2)}) collective-permute-start(f32[4,4,16,256]{3,2,1,0:T(8,128)S(1)} %get-tuple-element.129), channel_id=1, source_target_pairs={{0,7},{1,0},{2,1},{3,2},{4,3},{5,4},{6,5},{7,6},{8,15},{9,8},{10,9... | collective-permute-start | bytes 786440 | tf_op jit(solution)/shard_map/ppermute | solution.py:32
  186.3 5.1 %collective-permute-done.31.refs_6_.refs_25_.refs_9_.refs_17_ = f32[4,4,16,256]{3,2,1,0:T(8,128)} collective-permute-done((f32[4,4,16,256]{3,2,1,0:T(8,128)S(1)}, f32[4,4,16,256]{3,2,1,0:T(8,128)}, u32[]{:S(2)}, u32[]{:S(2)}) %collective-permute-start.31) | collective-permute-done | bytes 262176 | tf_op jit(solution)/shard_map/ppermute | solution.py:32
  199.1 9.6 %collective-permute-start.11 = (f32[4,4,16,256]{3,2,1,0:T(8,128)S(1)}, f32[4,4,16,256]{3,2,1,0:T(8,128)S(1)}, u32[]{:S(2)}, u32[]{:S(2)}) collective-permute-start(f32[4,4,16,256]{3,2,1,0:T(8,128)S(1)} %copy-done.16), channel_id=1, source_target_pairs={{0,5},{1,6},{2,7},{3,0},{4,1},{5,2},{6,3},{7,4},{8,13},{9,14},{10,... | collective-permute-start | bytes 786440 | tf_op jit(solution)/shard_map/ppermute | solution.py:32
  208.7 3.2 collective-permute-start.12
  215.3 19.0 %react.4 = (f32[16,3072]{1,0:T(8,128)}, f32[16,3072]{1,0:T(8,128)}, f32[16,3072]{1,0:T(8,128)}, f32[16,3072]{1,0:T(8,128)}, f32[16,3072]{1,0:T(8,128)}, /*index=...) custom-call(s32[1]{0:T(128)} %bitcast.refs_0_, ...), custom_call_target="tpu_custom_call" | custom-call | flops 3221225472 | bytes 6291456 | tf_op jit(solution)/shard_map/react/pallas_call | solution.py:246
  234.3 2.9 collective-permute-start.22
  238.1 19.0 %react.5 = (f32[16,3072]{1,0:T(8,128)}, f32[16,3072]{1,0:T(8,128)}, f32[16,3072]{1,0:T(8,128)}, f32[16,3072]{1,0:T(8,128)}, f32[16,3072]{1,0:T(8,128)}, /*index=...) custom-call(s32[1]{0:T(128)} %bitcast.refs_0_, ...), custom_call_target="tpu_custom_call" | custom-call | flops 3221225472 | bytes 6291456 | tf_op jit(solution)/shard_map/react/pallas_call | solution.py:246
  274.4 25.5 %collective-permute-start.14 = (f32[32,1,16,256]{3,2,1,0:T(8,128)}, f32[32,1,16,256]{3,2,1,0:T(8,128)}, u32[]{:S(2)}, u32[]{:S(2)}) collective-permute-start(f32[32,1,16,256]{3,2,1,0:T(8,128)} %get-tuple-element.71), channel_id=1, source_target_pairs={{0,1},{1,2},{2,3},{3,4},{4,5},{5,6},{6,7},{8,9},{9,10},{10,11},{11... | collective-permute-start | bytes 1572872 | tf_op jit(solution)/shard_map/ppermute | solution.py:27
  300.1 3.6 collective-permute-start.63
  303.8 5.2 %collective-permute-done.62.refs_9_ = f32[16,3072]{1,0:T(8,128)S(1)} collective-permute-done((f32[16,3072]{1,0:T(8,128)}, f32[16,3072]{1,0:T(8,128)S(1)}, u32[]{:S(2)}, u32[]{:S(2)}) %collective-permute-start.62) | collective-permute-done | bytes 196640 | tf_op jit(solution)/shard_map/ppermute | solution.py:32
  309.0 4.0 collective-permute-start.66
  315.3 19.0 %react.6 = (f32[16,3072]{1,0:T(8,128)}, f32[16,3072]{1,0:T(8,128)}, f32[16,3072]{1,0:T(8,128)}, f32[16,3072]{1,0:T(8,128)}, f32[16,3072]{1,0:T(8,128)}, /*index=...) custom-call(s32[1]{0:T(128)} %bitcast.refs_0_, ...), custom_call_target="tpu_custom_call" | custom-call | flops 3221225472 | bytes 6291456 | tf_op jit(solution)/shard_map/react/pallas_call | solution.py:246
  334.3 3.5 collective-permute-start.69
  340.6 3.1 collective-permute-start.52
  343.7 19.0 %react.7 = (f32[16,3328]{1,0:T(8,128)}, f32[16,3328]{1,0:T(8,128)}, f32[16,3328]{1,0:T(8,128)}, f32[16,3328]{1,0:T(8,128)}, f32[16,3328]{1,0:T(8,128)}, /*index=...) custom-call(s32[1]{0:T(128)} %bitcast.refs_0_, ...), custom_call_target="tpu_custom_call" | custom-call | flops 3221225472 | bytes 6291456 | tf_op jit(solution)/shard_map/react/pallas_call | solution.py:246
  368.5 18.1 %collective-permute-done.53.refs_7_ = f32[16,3072]{1,0:T(8,128)S(1)} collective-permute-done((f32[16,3072]{1,0:T(8,128)}, f32[16,3072]{1,0:T(8,128)S(1)}, u32[]{:S(2)}, u32[]{:S(2)}) %collective-permute-start.53) | collective-permute-done | bytes 196640 | tf_op jit(solution)/shard_map/ppermute | solution.py:32
  386.8 10.1 %collective-permute-start.44 = (f32[16,3328]{1,0:T(8,128)}, f32[16,3328]{1,0:T(8,128)S(1)}, u32[]{:S(2)}, u32[]{:S(2)}) collective-permute-start(f32[16,3328]{1,0:T(8,128)} %get-tuple-element.89), channel_id=1, source_target_pairs={{0,3},{1,4},{2,5},{3,6},{4,7},{5,0},{6,1},{7,2},{8,11},{9,12},{10,... | collective-permute-start | bytes 638984 | tf_op jit(solution)/shard_map/ppermute | solution.py:32
  399.8 5.4 %unpack.4.refs_14_ = f32[4,128,16,256]{3,2,1,0:T(8,128)} custom-call(s32[1]{0:T(128)} %bitcast.refs_0_, s32[32]{0:T(128)} %and_select_fusion.3.refs_1_, f32[16,3072]{1,0:T(8,128)} %get-tuple-element.112.refs_2_, f32[16,3072]{1,0:T(8,128)} %copy-done.41, f32[16,3072]{1,0:T(8,128)} %copy-done.42, f32[16,3072]{1,0:T(8,128)} %copy-done.43, ...), custom_call_target="tpu_custom_call" | custom-call | flops 209715200 | bytes 6291456 | tf_op jit(solution)/shard_map/unpack/pallas_call | solution.py:395
  405.3 5.6 %unpack.5.refs_14_ = f32[4,128,16,256]{3,2,1,0:T(8,128)} custom-call(s32[1]{0:T(128)} %bitcast.refs_0_, s32[32]{0:T(128)} %and_select_fusion.3.refs_1_, f32[16,3072]{1,0:T(8,128)} %get-tuple-element.104.refs_2_, f32[16,3072]{1,0:T(8,128)} %copy-done.34, f32[16,3072]{1,0:T(8,128)} %copy-done.35, ...), custom_call_target="tpu_custom_call", output_to_operand_aliasing={{}: (14, {})} | custom-call | flops 209715200 | bytes 6291456 | tf_op jit(solution)/shard_map/unpack/pallas_call | solution.py:395
  411.7 5.4 %unpack.6.refs_17_ = f32[4,128,16,256]{3,2,1,0:T(8,128)} custom-call(s32[1]{0:T(128)} %bitcast.refs_0_, s32[32]{0:T(128)} %and_select_fusion.3.refs_1_, f32[16,3072]{1,0:T(8,128)} %get-tuple-element.96.refs_2_, f32[16,3072]{1,0:T(8,128)} %copy-done.47, f32[16,3072]{1,0:T(8,128)} %collective-permute-done.50.refs_4_, ...), custom_call_target="tpu_custom_call", output_to_operand_aliasing={{}: (14, {})} | custom-call | flops 209715200 | bytes 6291456 | tf_op jit(solution)/shard_map/unpack/pallas_call | solution.py:395
  418.1 5.6 %unpack.7 = (f32[4,128,16,256]{3,2,1,0:T(8,128)}, f32[16,16,256]{2,1,0:T(8,128)}) custom-call(s32[1]{0:T(128)} %bitcast.refs_0_, s32[32]{0:T(128)} %and_select_fusion.3.refs_1_, f32[16,3328]{1,0:T(8,128)} %get-tuple-element.84.refs_2_, f32[16,3328]{1,0:T(8,128)} %copy-done.27, f32[16,3328]{1,0:T(8,128)} %copy-done.28, ...), custom_call_target="tpu_custom_call", output_to_operand_aliasing={{0}: (17, {})} | custom-call | flops 209715200 | bytes 6291456 | tf_op jit(solution)/shard_map/unpack/pallas_call | solution.py:395
  (323 shorter events, 95.3 us)
Async XLA Ops:
  3.4 38.6 %collective-permute-start = (f32[4,4,16,256]{3,2,1,0:T(8,128)}, f32[4,4,16,256]{3,2,1,0:T(8,128)S(1)}, u32[]{:S(2)}, u32[]{:S(2)}) collective-permute-start(f32[4,4,16,256]{3,2,1,0:T(8,128)} %get-tuple-element.64), channel_id=1, source_target_pairs={{0,1},{1,2},{2,3},{3,4},{4,5},{5,6},{6,7},{7,0},{8,9},{9,10},{10,1... | collective-permute-start | bytes 786440 | tf_op jit(solution)/shard_map/ppermute | solution.py:32
  5.5 29.0 %collective-permute-start.48 = (f32[16,1,256]{2,1,0:T(1,128)}, f32[16,1,256]{2,1,0:T(1,128)S(1)}, u32[]{:S(2)}, u32[]{:S(2)}) collective-permute-start(f32[16,1,256]{2,1,0:T(1,128)} %get-tuple-element.172), channel_id=1, source_target_pairs={{0,8},{8,16},{16,24},{24,0},{1,9},{9,17},{17,25},{25,1},{2,10},{10... | collective-permute-start | bytes 49160 | tf_op jit(solution)/shard_map/ppermute | solution.py:32
  36.2 29.2 %collective-permute-start.2 = (f32[4,4,16,256]{3,2,1,0:T(8,128)}, f32[4,4,16,256]{3,2,1,0:T(8,128)S(1)}, u32[]{:S(2)}, u32[]{:S(2)}) collective-permute-start(f32[4,4,16,256]{3,2,1,0:T(8,128)} %get-tuple-element.66), channel_id=1, source_target_pairs={{0,3},{1,4},{2,5},{3,6},{4,7},{5,0},{6,1},{7,2},{8,11},{9,12},{10,... | collective-permute-start | bytes 786440 | tf_op jit(solution)/shard_map/ppermute | solution.py:32
  40.0 32.3 %collective-permute-start.4 = (f32[4,4,16,256]{3,2,1,0:T(8,128)}, f32[4,4,16,256]{3,2,1,0:T(8,128)S(1)}, u32[]{:S(2)}, u32[]{:S(2)}) collective-permute-start(f32[4,4,16,256]{3,2,1,0:T(8,128)} %get-tuple-element.68), channel_id=1, source_target_pairs={{0,5},{1,6},{2,7},{3,0},{4,1},{5,2},{6,3},{7,4},{8,13},{9,14},{10,... | collective-permute-start | bytes 786440 | tf_op jit(solution)/shard_map/ppermute | solution.py:32
  42.0 41.6 %collective-permute-start.5 = (f32[4,4,16,256]{3,2,1,0:T(8,128)}, f32[4,4,16,256]{3,2,1,0:T(8,128)S(1)}, u32[]{:S(2)}, u32[]{:S(2)}) collective-permute-start(f32[4,4,16,256]{3,2,1,0:T(8,128)} %get-tuple-element.69), channel_id=1, source_target_pairs={{0,6},{1,7},{2,0},{3,1},{4,2},{5,3},{6,4},{7,5},{8,14},{9,15},{10,... | collective-permute-start | bytes 786440 | tf_op jit(solution)/shard_map/ppermute | solution.py:32
  45.2 53.9 %collective-permute-start.6 = (f32[4,4,16,256]{3,2,1,0:T(8,128)}, f32[4,4,16,256]{3,2,1,0:T(8,128)S(1)}, u32[]{:S(2)}, u32[]{:S(2)}) collective-permute-start(f32[4,4,16,256]{3,2,1,0:T(8,128)} %get-tuple-element.70), channel_id=1, source_target_pairs={{0,7},{1,0},{2,1},{3,2},{4,3},{5,4},{6,5},{7,6},{8,15},{9,8},{10,9... | collective-permute-start | bytes 786440 | tf_op jit(solution)/shard_map/ppermute | solution.py:32
  65.3 33.7 %collective-permute-start.7 = (f32[4,4,16,256]{3,2,1,0:T(8,128)S(1)}, f32[4,4,16,256]{3,2,1,0:T(8,128)S(1)}, u32[]{:S(2)}, u32[]{:S(2)}) collective-permute-start(f32[4,4,16,256]{3,2,1,0:T(8,128)S(1)} %get-tuple-element.151), channel_id=1, source_target_pairs={{0,1},{1,2},{2,3},{3,4},{4,5},{5,6},{6,7},{7,0},{8,9},{9,10},{10,1... | collective-permute-start | bytes 786440 | tf_op jit(solution)/shard_map/ppermute | solution.py:32
  65.5 33.6 %collective-permute-start.15 = (f32[4,4,16,256]{3,2,1,0:T(8,128)S(1)}, f32[4,4,16,256]{3,2,1,0:T(8,128)S(1)}, u32[]{:S(2)}, u32[]{:S(2)}) collective-permute-start(f32[4,4,16,256]{3,2,1,0:T(8,128)S(1)} %get-tuple-element.143), channel_id=1, source_target_pairs={{0,1},{1,2},{2,3},{3,4},{4,5},{5,6},{6,7},{7,0},{8,9},{9,10},{10,1... | collective-permute-start | bytes 786440 | tf_op jit(solution)/shard_map/ppermute | solution.py:32
  72.3 29.3 %collective-permute-start.16 = (f32[4,4,16,256]{3,2,1,0:T(8,128)S(1)}, f32[4,4,16,256]{3,2,1,0:T(8,128)S(1)}, u32[]{:S(2)}, u32[]{:S(2)}) collective-permute-start(f32[4,4,16,256]{3,2,1,0:T(8,128)S(1)} %get-tuple-element.142), channel_id=1, source_target_pairs={{0,2},{1,3},{2,4},{3,5},{4,6},{5,7},{6,0},{7,1},{8,10},{9,11},{10,... | collective-permute-start | bytes 786440 | tf_op jit(solution)/shard_map/ppermute | solution.py:32
  99.1 32.3 %collective-permute-start.19 = (f32[4,4,16,256]{3,2,1,0:T(8,128)}, f32[4,4,16,256]{3,2,1,0:T(8,128)}, u32[]{:S(2)}, u32[]{:S(2)}) collective-permute-start(f32[4,4,16,256]{3,2,1,0:T(8,128)} %get-tuple-element.139), channel_id=1, source_target_pairs={{0,5},{1,6},{2,7},{3,0},{4,1},{5,2},{6,3},{7,4},{8,13},{9,14},{10,... | collective-permute-start | bytes 786440 | tf_op jit(solution)/shard_map/ppermute | solution.py:32
  99.2 32.2 %collective-permute-start.20 = (f32[4,4,16,256]{3,2,1,0:T(8,128)S(1)}, f32[4,4,16,256]{3,2,1,0:T(8,128)}, u32[]{:S(2)}, u32[]{:S(2)}) collective-permute-start(f32[4,4,16,256]{3,2,1,0:T(8,128)S(1)} %get-tuple-element.138), channel_id=1, source_target_pairs={{0,6},{1,7},{2,0},{3,1},{4,2},{5,3},{6,4},{7,5},{8,14},{9,15},{10,... | collective-permute-start | bytes 786440 | tf_op jit(solution)/shard_map/ppermute | solution.py:32
  101.6 38.2 %collective-permute-start.21 = (f32[4,4,16,256]{3,2,1,0:T(8,128)S(1)}, f32[4,4,16,256]{3,2,1,0:T(8,128)}, u32[]{:S(2)}, u32[]{:S(2)}) collective-permute-start(f32[4,4,16,256]{3,2,1,0:T(8,128)S(1)} %get-tuple-element.137), channel_id=1, source_target_pairs={{0,7},{1,0},{2,1},{3,2},{4,3},{5,4},{6,5},{7,6},{8,15},{9,8},{10,9... | collective-permute-start | bytes 786440 | tf_op jit(solution)/shard_map/ppermute | solution.py:32
  106.1 36.5 %collective-permute-start.26 = (f32[4,4,16,256]{3,2,1,0:T(8,128)}, f32[4,4,16,256]{3,2,1,0:T(8,128)S(1)}, u32[]{:S(2)}, u32[]{:S(2)}) collective-permute-start(f32[4,4,16,256]{3,2,1,0:T(8,128)} %get-tuple-element.135), channel_id=1, source_target_pairs={{0,1},{1,2},{2,3},{3,4},{4,5},{5,6},{6,7},{7,0},{8,9},{9,10},{10,1... | collective-permute-start | bytes 786440 | tf_op jit(solution)/shard_map/ppermute | solution.py:32
  131.3 45.5 %collective-permute-start.28 = (f32[4,4,16,256]{3,2,1,0:T(8,128)}, f32[4,4,16,256]{3,2,1,0:T(8,128)S(1)}, u32[]{:S(2)}, u32[]{:S(2)}) collective-permute-start(f32[4,4,16,256]{3,2,1,0:T(8,128)} %get-tuple-element.133), channel_id=1, source_target_pairs={{0,3},{1,4},{2,5},{3,6},{4,7},{5,0},{6,1},{7,2},{8,11},{9,12},{10,... | collective-permute-start | bytes 786440 | tf_op jit(solution)/shard_map/ppermute | solution.py:32
  131.3 45.7 %collective-permute-start.29 = (f32[4,4,16,256]{3,2,1,0:T(8,128)}, f32[4,4,16,256]{3,2,1,0:T(8,128)S(1)}, u32[]{:S(2)}, u32[]{:S(2)}) collective-permute-start(f32[4,4,16,256]{3,2,1,0:T(8,128)} %get-tuple-element.132), channel_id=1, source_target_pairs={{0,4},{1,5},{2,6},{3,7},{4,0},{5,1},{6,2},{7,3},{8,12},{9,13},{10,... | collective-permute-start | bytes 786440 | tf_op jit(solution)/shard_map/ppermute | solution.py:32
  139.8 37.3 %collective-permute-start.30 = (f32[4,4,16,256]{3,2,1,0:T(8,128)}, f32[4,4,16,256]{3,2,1,0:T(8,128)S(1)}, u32[]{:S(2)}, u32[]{:S(2)}) collective-permute-start(f32[4,4,16,256]{3,2,1,0:T(8,128)} %get-tuple-element.131), channel_id=1, source_target_pairs={{0,5},{1,6},{2,7},{3,0},{4,1},{5,2},{6,3},{7,4},{8,13},{9,14},{10,... | collective-permute-start | bytes 786440 | tf_op jit(solution)/shard_map/ppermute | solution.py:32
  142.5 56.5 %collective-permute-start.8 = (f32[4,4,16,256]{3,2,1,0:T(8,128)}, f32[4,4,16,256]{3,2,1,0:T(8,128)S(1)}, u32[]{:S(2)}, u32[]{:S(2)}) collective-permute-start(f32[4,4,16,256]{3,2,1,0:T(8,128)} %get-tuple-element.150), channel_id=1, source_target_pairs={{0,2},{1,3},{2,4},{3,5},{4,6},{5,7},{6,0},{7,1},{8,10},{9,11},{10,... | collective-permute-start | bytes 786440 | tf_op jit(solution)/shard_map/ppermute | solution.py:32
  142.7 66.0 %collective-permute-start.9 = (f32[4,4,16,256]{3,2,1,0:T(8,128)}, f32[4,4,16,256]{3,2,1,0:T(8,128)S(1)}, u32[]{:S(2)}, u32[]{:S(2)}) collective-permute-start(f32[4,4,16,256]{3,2,1,0:T(8,128)} %get-tuple-element.149), channel_id=1, source_target_pairs={{0,3},{1,4},{2,5},{3,6},{4,7},{5,0},{6,1},{7,2},{8,11},{9,12},{10,... | collective-permute-start | bytes 786440 | tf_op jit(solution)/shard_map/ppermute | solution.py:32
  176.9 35.0 %collective-permute-start.10 = (f32[4,4,16,256]{3,2,1,0:T(8,128)}, f32[4,4,16,256]{3,2,1,0:T(8,128)}, u32[]{:S(2)}, u32[]{:S(2)}) collective-permute-start(f32[4,4,16,256]{3,2,1,0:T(8,128)} %get-tuple-element.148), channel_id=1, source_target_pairs={{0,4},{1,5},{2,6},{3,7},{4,0},{5,1},{6,2},{7,3},{8,12},{9,13},{10,... | collective-permute-start | bytes 786440 | tf_op jit(solution)/shard_map/ppermute | solution.py:32
  199.1 35.2 %collective-permute-start.11 = (f32[4,4,16,256]{3,2,1,0:T(8,128)S(1)}, f32[4,4,16,256]{3,2,1,0:T(8,128)S(1)}, u32[]{:S(2)}, u32[]{:S(2)}) collective-permute-start(f32[4,4,16,256]{3,2,1,0:T(8,128)S(1)} %copy-done.16), channel_id=1, source_target_pairs={{0,5},{1,6},{2,7},{3,0},{4,1},{5,2},{6,3},{7,4},{8,13},{9,14},{10,... | collective-permute-start | bytes 786440 | tf_op jit(solution)/shard_map/ppermute | solution.py:32
  208.7 28.5 %collective-permute-start.12 = (f32[4,4,16,256]{3,2,1,0:T(8,128)S(1)}, f32[4,4,16,256]{3,2,1,0:T(8,128)S(1)}, u32[]{:S(2)}, u32[]{:S(2)}) collective-permute-start(f32[4,4,16,256]{3,2,1,0:T(8,128)S(1)} %get-tuple-element.146), channel_id=1, source_target_pairs={{0,6},{1,7},{2,0},{3,1},{4,2},{5,3},{6,4},{7,5},{8,14},{9,15},{10,... | collective-permute-start | bytes 786440 | tf_op jit(solution)/shard_map/ppermute | solution.py:32
  262.8 50.3 %collective-permute-start.33 = (f32[32,1,16,256]{3,2,1,0:T(8,128)}, f32[32,1,16,256]{3,2,1,0:T(8,128)S(1)}, u32[]{:S(2)}, u32[]{:S(2)}) collective-permute-start(f32[32,1,16,256]{3,2,1,0:T(8,128)} %get-tuple-element.74), channel_id=1, source_target_pairs={{1,0},{2,1},{3,2},{4,3},{5,4},{6,5},{7,6},{9,8},{10,9},{11,10},{12... | collective-permute-start | bytes 1572872 | tf_op jit(solution)/shard_map/ppermute | solution.py:27
  269.7 30.4 %collective-permute-start.59 = (f32[16,3072]{1,0:T(8,128)}, f32[16,3072]{1,0:T(8,128)S(1)}, u32[]{:S(2)}, u32[]{:S(2)}) collective-permute-start(f32[16,3072]{1,0:T(8,128)} %get-tuple-element.108), channel_id=1, source_target_pairs={{0,4},{1,5},{2,6},{3,7},{4,0},{5,1},{6,2},{7,3},{8,12},{9,13},{10,... | collective-permute-start | bytes 589832 | tf_op jit(solution)/shard_map/ppermute | solution.py:32
  271.0 29.1 %collective-permute-start.60 = (f32[16,3072]{1,0:T(8,128)}, f32[16,3072]{1,0:T(8,128)S(1)}, u32[]{:S(2)}, u32[]{:S(2)}) collective-permute-start(f32[16,3072]{1,0:T(8,128)} %get-tuple-element.109), channel_id=1, source_target_pairs={{0,3},{1,4},{2,5},{3,6},{4,7},{5,0},{6,1},{7,2},{8,11},{9,12},{10,... | collective-permute-start | bytes 589832 | tf_op jit(solution)/shard_map/ppermute | solution.py:32
  271.0 32.7 %collective-permute-start.61 = (f32[16,3072]{1,0:T(8,128)}, f32[16,3072]{1,0:T(8,128)S(1)}, u32[]{:S(2)}, u32[]{:S(2)}) collective-permute-start(f32[16,3072]{1,0:T(8,128)} %get-tuple-element.110), channel_id=1, source_target_pairs={{0,2},{1,3},{2,4},{3,5},{4,6},{5,7},{6,0},{7,1},{8,10},{9,11},{10,... | collective-permute-start | bytes 589832 | tf_op jit(solution)/shard_map/ppermute | solution.py:32
  274.4 66.2 %collective-permute-start.14 = (f32[32,1,16,256]{3,2,1,0:T(8,128)}, f32[32,1,16,256]{3,2,1,0:T(8,128)}, u32[]{:S(2)}, u32[]{:S(2)}) collective-permute-start(f32[32,1,16,256]{3,2,1,0:T(8,128)} %get-tuple-element.71), channel_id=1, source_target_pairs={{0,1},{1,2},{2,3},{3,4},{4,5},{5,6},{6,7},{8,9},{9,10},{10,11},{11... | collective-permute-start | bytes 1572872 | tf_op jit(solution)/shard_map/ppermute | solution.py:27
  309.0 28.8 %collective-permute-start.66 = (f32[16,3072]{1,0:T(8,128)}, f32[16,3072]{1,0:T(8,128)S(1)}, u32[]{:S(2)}, u32[]{:S(2)}) collective-permute-start(f32[16,3072]{1,0:T(8,128)} %get-tuple-element.116), channel_id=1, source_target_pairs={{0,4},{1,5},{2,6},{3,7},{4,0},{5,1},{6,2},{7,3},{8,12},{9,13},{10,... | collective-permute-start | bytes 589832 | tf_op jit(solution)/shard_map/ppermute | solution.py:32
  362.8 34.1 %collective-permute-start.40 = (f32[16,3328]{1,0:T(8,128)}, f32[16,3328]{1,0:T(8,128)S(1)}, u32[]{:S(2)}, u32[]{:S(2)}) collective-permute-start(f32[16,3328]{1,0:T(8,128)} %get-tuple-element.85), channel_id=1, source_target_pairs={{0,7},{1,0},{2,1},{3,2},{4,3},{5,4},{6,5},{7,6},{8,15},{9,8},{10,9... | collective-permute-start | bytes 638984 | tf_op jit(solution)/shard_map/ppermute | solution.py:32
  364.0 33.0 %collective-permute-start.41 = (f32[16,3328]{1,0:T(8,128)}, f32[16,3328]{1,0:T(8,128)S(1)}, u32[]{:S(2)}, u32[]{:S(2)}) collective-permute-start(f32[16,3328]{1,0:T(8,128)} %get-tuple-element.86), channel_id=1, source_target_pairs={{0,6},{1,7},{2,0},{3,1},{4,2},{5,3},{6,4},{7,5},{8,14},{9,15},{10,... | collective-permute-start | bytes 638984 | tf_op jit(solution)/shard_map/ppermute | solution.py:32
  386.7 30.4 %collective-permute-start.42 = (f32[16,3328]{1,0:T(8,128)}, f32[16,3328]{1,0:T(8,128)S(1)}, u32[]{:S(2)}, u32[]{:S(2)}) collective-permute-start(f32[16,3328]{1,0:T(8,128)} %get-tuple-element.87), channel_id=1, source_target_pairs={{0,5},{1,6},{2,7},{3,0},{4,1},{5,2},{6,3},{7,4},{8,13},{9,14},{10,... | collective-permute-start | bytes 638984 | tf_op jit(solution)/shard_map/ppermute | solution.py:32
  386.7 30.4 %collective-permute-start.43 = (f32[16,3328]{1,0:T(8,128)}, f32[16,3328]{1,0:T(8,128)S(1)}, u32[]{:S(2)}, u32[]{:S(2)}) collective-permute-start(f32[16,3328]{1,0:T(8,128)} %get-tuple-element.88), channel_id=1, source_target_pairs={{0,4},{1,5},{2,6},{3,7},{4,0},{5,1},{6,2},{7,3},{8,12},{9,13},{10,... | collective-permute-start | bytes 638984 | tf_op jit(solution)/shard_map/ppermute | solution.py:32
  386.8 30.4 %collective-permute-start.44 = (f32[16,3328]{1,0:T(8,128)}, f32[16,3328]{1,0:T(8,128)S(1)}, u32[]{:S(2)}, u32[]{:S(2)}) collective-permute-start(f32[16,3328]{1,0:T(8,128)} %get-tuple-element.89), channel_id=1, source_target_pairs={{0,3},{1,4},{2,5},{3,6},{4,7},{5,0},{6,1},{7,2},{8,11},{9,12},{10,... | collective-permute-start | bytes 638984 | tf_op jit(solution)/shard_map/ppermute | solution.py:32
  (105 other events, 3036.8 us)

commit v5 on v4

--- a/solution.py
+++ b/solution.py
@@ -311,8 +311,9 @@
     water, pick, second = rest[:3]
     wet = water[...] > 0.5
 
-    def unpack(d, carry):
-        packed_in(d, received[0]).wait()
+    def unpack(d, carry, arrived=False):
+        if not arrived:
+            packed_in(d, received[0]).wait()
         block_in(d).wait()
         spread_block(d, tile_ref, pick, second, slots, spread, held * nl, across, lat)
         for i in range(held):
@@ -326,8 +327,11 @@
         block_out(d).start()
         return carry
 
-    lax.fori_loop(0, n, unpack, 0)
+    early = n - 3 if closing else n
+    lax.fori_loop(0, early, unpack, 0)
     if closing:
+        for d in range(early, n):
+            packed_in(d, received[0]).wait()
         for copy in copies[3:]:
             copy.wait()
         absorb, sun, carried, warmed = rest[3:]
@@ -348,6 +352,7 @@
                 coming = left
         warm = pltpu.make_async_copy(warmed, warmed_out, sems.at[1, n])
         warm.start()
+        lax.fori_loop(early, n, functools.partial(unpack, arrived=True), 0)
         warm.wait()
     for d in range(n):
         block_out(d).wait()

time: 425 us -> 425 us (level)
  no operation moved by 1% of the time
where the time goes in v5:
time: 425 us; the launch traced here: 424 us
  starting transfers between devices  185 us (44%)
  Pallas kernels  108 us (25%)
  waiting for transfers between devices  93.7 us (22%)
  local copies, waits for them, and re-layouts  20.5 us (5%)
  other arithmetic  13 us (3%)
    ppermute x66, starting transfers between devices, around(): lax.ppermute(block, axis, [(i, (i + distance) % count) for i in range(cou...  152 us
    ppermute x66, waiting for transfers between devices, around(): lax.ppermute(block, axis, [(i, (i + distance) % count) for i in range(cou...  93.7 us
    pallas_call x4, Pallas kernels, react_chunk(): pl.pallas_call(functools.partial(react_kernel, n, nl, q, closing), grid_s...  75.9 us
    ppermute x4, starting transfers between devices, shifted(): return lax.ppermute(block, axis, route)  32.2 us
    pallas_call x4, Pallas kernels, unpack_chunk(): pl.pallas_call(functools.partial(unpack_kernel, n, nl, cap, q * nl, base...  22 us
    pallas_call x4, Pallas kernels, chunk_edges(): pl.pallas_call(functools.partial(edges_kernel, n, level, turn), in_specs=...  9.73 us
    dynamic_slice x3, local copies, waits for them, and re-layouts, on_device(): sends[d] = lax.dynamic_slice_in_dim(raw, to * levels + q * nl, nl, 1)  9.61 us
  transfers between devices with their start and end apart: 70, of which 17 were waited for; matrix products, arithmetic and copies ran while one was open for 7% of the time, Pallas kernels for 24%

profile of v5, /device:TPU:0, one launch (start us, length us, event | category | flops | bytes accessed | tf_op | source)
XLA Modules:
  0.0 423.9 jit_solution(5415082577879800862)
XLA Ops:
  12.3 4.1 collective-permute-start.24
  29.5 4.2 %constant_dynamic-slice_fusion = (f32[4,4,16,256]{3,2,1,0:T(8,128)S(1)}, f32[4,4,16,256]{3,2,1,0:T(8,128)S(1)}, f32[4,4,16,256]{3,2,1,0:T(8,128)}, f32[4,4,16,25...) fusion(f32[4,128,16,256]{3,2,1,0:T(8,128)} %refs_10_.7, ...), kind=kLoop, calls=%fused_computation.78 | loop fusion | bytes 9437256 | tf_op jit(solution)/shard_map/dynamic_slice | solution.py:472
  46.1 19.2 %collective-permute-done.2.refs_3_.refs_14_.refs_6_ = f32[4,4,16,256]{3,2,1,0:T(8,128)S(1)} collective-permute-done((f32[4,4,16,256]{3,2,1,0:T(8,128)}, f32[4,4,16,256]{3,2,1,0:T(8,128)S(1)}, u32[]{:S(2)}, u32[]{:S(2)}) %collective-permute-start.2) | collective-permute-done | bytes 262176 | tf_op jit(solution)/shard_map/ppermute | solution.py:32
  65.5 6.7 %collective-permute-start.15 = (f32[4,4,16,256]{3,2,1,0:T(8,128)S(1)}, f32[4,4,16,256]{3,2,1,0:T(8,128)S(1)}, u32[]{:S(2)}, u32[]{:S(2)}) collective-permute-start(f32[4,4,16,256]{3,2,1,0:T(8,128)S(1)} %get-tuple-element.143), channel_id=1, source_target_pairs={{0,1},{1,2},{2,3},{3,4},{4,5},{5,6},{6,7},{7,0},{8,9},{9,10},{10,1... | collective-permute-start | bytes 786440 | tf_op jit(solution)/shard_map/ppermute | solution.py:32
  72.3 11.2 %collective-permute-start.16 = (f32[4,4,16,256]{3,2,1,0:T(8,128)S(1)}, f32[4,4,16,256]{3,2,1,0:T(8,128)S(1)}, u32[]{:S(2)}, u32[]{:S(2)}) collective-permute-start(f32[4,4,16,256]{3,2,1,0:T(8,128)S(1)} %get-tuple-element.142), channel_id=1, source_target_pairs={{0,2},{1,3},{2,4},{3,5},{4,6},{5,7},{6,0},{7,1},{8,10},{9,11},{10,... | collective-permute-start | bytes 786440 | tf_op jit(solution)/shard_map/ppermute | solution.py:32
  83.6 15.4 %collective-permute-start.17 = (f32[4,4,16,256]{3,2,1,0:T(8,128)}, f32[4,4,16,256]{3,2,1,0:T(8,128)}, u32[]{:S(2)}, u32[]{:S(2)}) collective-permute-start(f32[4,4,16,256]{3,2,1,0:T(8,128)} %get-tuple-element.141), channel_id=1, source_target_pairs={{0,3},{1,4},{2,5},{3,6},{4,7},{5,0},{6,1},{7,2},{8,11},{9,12},{10,... | collective-permute-start | bytes 786440 | tf_op jit(solution)/shard_map/ppermute | solution.py:32
  106.1 10.9 %collective-permute-done.18.refs_4_.refs_7_.refs_15_.refs_23_ = f32[4,4,16,256]{3,2,1,0:T(8,128)} collective-permute-done((f32[4,4,16,256]{3,2,1,0:T(8,128)}, f32[4,4,16,256]{3,2,1,0:T(8,128)}, u32[]{:S(2)}, u32[]{:S(2)}) %collective-permute-start.18) | collective-permute-done | bytes 262176 | tf_op jit(solution)/shard_map/ppermute | solution.py:32
  117.0 14.4 %collective-permute-start.27 = (f32[4,4,16,256]{3,2,1,0:T(8,128)}, f32[4,4,16,256]{3,2,1,0:T(8,128)S(1)}, u32[]{:S(2)}, u32[]{:S(2)}) collective-permute-start(f32[4,4,16,256]{3,2,1,0:T(8,128)} %get-tuple-element.134), channel_id=1, source_target_pairs={{0,2},{1,3},{2,4},{3,5},{4,6},{5,7},{6,0},{7,1},{8,10},{9,11},{10,... | collective-permute-start | bytes 786440 | tf_op jit(solution)/shard_map/ppermute | solution.py:32
  131.3 8.4 %collective-permute-start.29 = (f32[4,4,16,256]{3,2,1,0:T(8,128)}, f32[4,4,16,256]{3,2,1,0:T(8,128)S(1)}, u32[]{:S(2)}, u32[]{:S(2)}) collective-permute-start(f32[4,4,16,256]{3,2,1,0:T(8,128)} %get-tuple-element.132), channel_id=1, source_target_pairs={{0,4},{1,5},{2,6},{3,7},{4,0},{5,1},{6,2},{7,3},{8,12},{9,13},{10,... | collective-permute-start | bytes 786440 | tf_op jit(solution)/shard_map/ppermute | solution.py:32
  142.7 12.1 %collective-permute-start.9 = (f32[4,4,16,256]{3,2,1,0:T(8,128)}, f32[4,4,16,256]{3,2,1,0:T(8,128)S(1)}, u32[]{:S(2)}, u32[]{:S(2)}) collective-permute-start(f32[4,4,16,256]{3,2,1,0:T(8,128)} %get-tuple-element.149), channel_id=1, source_target_pairs={{0,3},{1,4},{2,5},{3,6},{4,7},{5,0},{6,1},{7,2},{8,11},{9,12},{10,... | collective-permute-start | bytes 786440 | tf_op jit(solution)/shard_map/ppermute | solution.py:32
  154.8 22.1 %collective-permute-done.28.refs_3_.refs_22_.refs_6_.refs_14_ = f32[4,4,16,256]{3,2,1,0:T(8,128)S(1)} collective-permute-done((f32[4,4,16,256]{3,2,1,0:T(8,128)}, f32[4,4,16,256]{3,2,1,0:T(8,128)S(1)}, u32[]{:S(2)}, u32[]{:S(2)}) %collective-permute-start.28) | collective-permute-done | bytes 262176 | tf_op jit(solution)/shard_map/ppermute | solution.py:32
  177.1 6.0 %collective-permute-start.32 = (f32[4,4,16,256]{3,2,1,0:T(8,128)S(1)}, f32[4,4,16,256]{3,2,1,0:T(8,128)}, u32[]{:S(2)}, u32[]{:S(2)}) collective-permute-start(f32[4,4,16,256]{3,2,1,0:T(8,128)S(1)} %get-tuple-element.129), channel_id=1, source_target_pairs={{0,7},{1,0},{2,1},{3,2},{4,3},{5,4},{6,5},{7,6},{8,15},{9,8},{10,9... | collective-permute-start | bytes 786440 | tf_op jit(solution)/shard_map/ppermute | solution.py:32
  186.3 5.1 %collective-permute-done.31.refs_6_.refs_25_.refs_9_.refs_17_ = f32[4,4,16,256]{3,2,1,0:T(8,128)} collective-permute-done((f32[4,4,16,256]{3,2,1,0:T(8,128)S(1)}, f32[4,4,16,256]{3,2,1,0:T(8,128)}, u32[]{:S(2)}, u32[]{:S(2)}) %collective-permute-start.31) | collective-permute-done | bytes 262176 | tf_op jit(solution)/shard_map/ppermute | solution.py:32
  199.1 9.6 %collective-permute-start.11 = (f32[4,4,16,256]{3,2,1,0:T(8,128)S(1)}, f32[4,4,16,256]{3,2,1,0:T(8,128)S(1)}, u32[]{:S(2)}, u32[]{:S(2)}) collective-permute-start(f32[4,4,16,256]{3,2,1,0:T(8,128)S(1)} %copy-done.16), channel_id=1, source_target_pairs={{0,5},{1,6},{2,7},{3,0},{4,1},{5,2},{6,3},{7,4},{8,13},{9,14},{10,... | collective-permute-start | bytes 786440 | tf_op jit(solution)/shard_map/ppermute | solution.py:32
  208.7 3.2 collective-permute-start.12
  215.3 19.0 %react.4 = (f32[16,3072]{1,0:T(8,128)}, f32[16,3072]{1,0:T(8,128)}, f32[16,3072]{1,0:T(8,128)}, f32[16,3072]{1,0:T(8,128)}, f32[16,3072]{1,0:T(8,128)}, /*index=...) custom-call(s32[1]{0:T(128)} %bitcast.refs_0_, ...), custom_call_target="tpu_custom_call" | custom-call | flops 3221225472 | bytes 6291456 | tf_op jit(solution)/shard_map/react/pallas_call | solution.py:246
  234.3 2.9 collective-permute-start.22
  238.1 19.0 %react.5 = (f32[16,3072]{1,0:T(8,128)}, f32[16,3072]{1,0:T(8,128)}, f32[16,3072]{1,0:T(8,128)}, f32[16,3072]{1,0:T(8,128)}, f32[16,3072]{1,0:T(8,128)}, /*index=...) custom-call(s32[1]{0:T(128)} %bitcast.refs_0_, ...), custom_call_target="tpu_custom_call" | custom-call | flops 3221225472 | bytes 6291456 | tf_op jit(solution)/shard_map/react/pallas_call | solution.py:246
  274.4 25.5 %collective-permute-start.14 = (f32[32,1,16,256]{3,2,1,0:T(8,128)}, f32[32,1,16,256]{3,2,1,0:T(8,128)}, u32[]{:S(2)}, u32[]{:S(2)}) collective-permute-start(f32[32,1,16,256]{3,2,1,0:T(8,128)} %get-tuple-element.71), channel_id=1, source_target_pairs={{0,1},{1,2},{2,3},{3,4},{4,5},{5,6},{6,7},{8,9},{9,10},{10,11},{11... | collective-permute-start | bytes 1572872 | tf_op jit(solution)/shard_map/ppermute | solution.py:27
  300.1 3.6 collective-permute-start.63
  303.8 5.2 %collective-permute-done.62.refs_9_ = f32[16,3072]{1,0:T(8,128)S(1)} collective-permute-done((f32[16,3072]{1,0:T(8,128)}, f32[16,3072]{1,0:T(8,128)S(1)}, u32[]{:S(2)}, u32[]{:S(2)}) %collective-permute-start.62) | collective-permute-done | bytes 196640 | tf_op jit(solution)/shard_map/ppermute | solution.py:32
  309.0 4.0 collective-permute-start.66
  315.3 19.0 %react.6 = (f32[16,3072]{1,0:T(8,128)}, f32[16,3072]{1,0:T(8,128)}, f32[16,3072]{1,0:T(8,128)}, f32[16,3072]{1,0:T(8,128)}, f32[16,3072]{1,0:T(8,128)}, /*index=...) custom-call(s32[1]{0:T(128)} %bitcast.refs_0_, ...), custom_call_target="tpu_custom_call" | custom-call | flops 3221225472 | bytes 6291456 | tf_op jit(solution)/shard_map/react/pallas_call | solution.py:246
  334.3 3.5 collective-permute-start.69
  340.6 3.1 collective-permute-start.52
  343.7 19.0 %react.7 = (f32[16,3328]{1,0:T(8,128)}, f32[16,3328]{1,0:T(8,128)}, f32[16,3328]{1,0:T(8,128)}, f32[16,3328]{1,0:T(8,128)}, f32[16,3328]{1,0:T(8,128)}, /*index=...) custom-call(s32[1]{0:T(128)} %bitcast.refs_0_, ...), custom_call_target="tpu_custom_call" | custom-call | flops 3221225472 | bytes 6291456 | tf_op jit(solution)/shard_map/react/pallas_call | solution.py:246
  368.5 18.1 %collective-permute-done.53.refs_7_ = f32[16,3072]{1,0:T(8,128)S(1)} collective-permute-done((f32[16,3072]{1,0:T(8,128)}, f32[16,3072]{1,0:T(8,128)S(1)}, u32[]{:S(2)}, u32[]{:S(2)}) %collective-permute-start.53) | collective-permute-done | bytes 196640 | tf_op jit(solution)/shard_map/ppermute | solution.py:32
  386.8 10.1 %collective-permute-start.44 = (f32[16,3328]{1,0:T(8,128)}, f32[16,3328]{1,0:T(8,128)S(1)}, u32[]{:S(2)}, u32[]{:S(2)}) collective-permute-start(f32[16,3328]{1,0:T(8,128)} %get-tuple-element.89), channel_id=1, source_target_pairs={{0,3},{1,4},{2,5},{3,6},{4,7},{5,0},{6,1},{7,2},{8,11},{9,12},{10,... | collective-permute-start | bytes 638984 | tf_op jit(solution)/shard_map/ppermute | solution.py:32
  399.8 5.4 %unpack.4.refs_14_ = f32[4,128,16,256]{3,2,1,0:T(8,128)} custom-call(s32[1]{0:T(128)} %bitcast.refs_0_, s32[32]{0:T(128)} %and_select_fusion.3.refs_1_, f32[16,3072]{1,0:T(8,128)} %get-tuple-element.112.refs_2_, f32[16,3072]{1,0:T(8,128)} %copy-done.41, f32[16,3072]{1,0:T(8,128)} %copy-done.42, f32[16,3072]{1,0:T(8,128)} %copy-done.43, ...), custom_call_target="tpu_custom_call" | custom-call | flops 209715200 | bytes 6291456 | tf_op jit(solution)/shard_map/unpack/pallas_call | solution.py:400
  405.3 5.6 %unpack.5.refs_14_ = f32[4,128,16,256]{3,2,1,0:T(8,128)} custom-call(s32[1]{0:T(128)} %bitcast.refs_0_, s32[32]{0:T(128)} %and_select_fusion.3.refs_1_, f32[16,3072]{1,0:T(8,128)} %get-tuple-element.104.refs_2_, f32[16,3072]{1,0:T(8,128)} %copy-done.34, f32[16,3072]{1,0:T(8,128)} %copy-done.35, ...), custom_call_target="tpu_custom_call", output_to_operand_aliasing={{}: (14, {})} | custom-call | flops 209715200 | bytes 6291456 | tf_op jit(solution)/shard_map/unpack/pallas_call | solution.py:400
  411.7 5.4 %unpack.6.refs_17_ = f32[4,128,16,256]{3,2,1,0:T(8,128)} custom-call(s32[1]{0:T(128)} %bitcast.refs_0_, s32[32]{0:T(128)} %and_select_fusion.3.refs_1_, f32[16,3072]{1,0:T(8,128)} %get-tuple-element.96.refs_2_, f32[16,3072]{1,0:T(8,128)} %copy-done.47, f32[16,3072]{1,0:T(8,128)} %collective-permute-done.50.refs_4_, ...), custom_call_target="tpu_custom_call", output_to_operand_aliasing={{}: (14, {})} | custom-call | flops 209715200 | bytes 6291456 | tf_op jit(solution)/shard_map/unpack/pallas_call | solution.py:400
  418.1 5.6 %unpack.7 = (f32[4,128,16,256]{3,2,1,0:T(8,128)}, f32[16,16,256]{2,1,0:T(8,128)}) custom-call(s32[1]{0:T(128)} %bitcast.refs_0_, s32[32]{0:T(128)} %and_select_fusion.3.refs_1_, f32[16,3328]{1,0:T(8,128)} %get-tuple-element.84.refs_2_, f32[16,3328]{1,0:T(8,128)} %copy-done.27, f32[16,3328]{1,0:T(8,128)} %copy-done.28, ...), custom_call_target="tpu_custom_call", output_to_operand_aliasing={{0}: (17, {})} | custom-call | flops 209715200 | bytes 6291456 | tf_op jit(solution)/shard_map/unpack/pallas_call | solution.py:400
  (323 shorter events, 95.3 us)
Async XLA Ops:
  3.4 38.6 %collective-permute-start = (f32[4,4,16,256]{3,2,1,0:T(8,128)}, f32[4,4,16,256]{3,2,1,0:T(8,128)S(1)}, u32[]{:S(2)}, u32[]{:S(2)}) collective-permute-start(f32[4,4,16,256]{3,2,1,0:T(8,128)} %get-tuple-element.64), channel_id=1, source_target_pairs={{0,1},{1,2},{2,3},{3,4},{4,5},{5,6},{6,7},{7,0},{8,9},{9,10},{10,1... | collective-permute-start | bytes 786440 | tf_op jit(solution)/shard_map/ppermute | solution.py:32
  5.5 29.0 %collective-permute-start.48 = (f32[16,1,256]{2,1,0:T(1,128)}, f32[16,1,256]{2,1,0:T(1,128)S(1)}, u32[]{:S(2)}, u32[]{:S(2)}) collective-permute-start(f32[16,1,256]{2,1,0:T(1,128)} %get-tuple-element.172), channel_id=1, source_target_pairs={{0,8},{8,16},{16,24},{24,0},{1,9},{9,17},{17,25},{25,1},{2,10},{10... | collective-permute-start | bytes 49160 | tf_op jit(solution)/shard_map/ppermute | solution.py:32
  36.2 29.2 %collective-permute-start.2 = (f32[4,4,16,256]{3,2,1,0:T(8,128)}, f32[4,4,16,256]{3,2,1,0:T(8,128)S(1)}, u32[]{:S(2)}, u32[]{:S(2)}) collective-permute-start(f32[4,4,16,256]{3,2,1,0:T(8,128)} %get-tuple-element.66), channel_id=1, source_target_pairs={{0,3},{1,4},{2,5},{3,6},{4,7},{5,0},{6,1},{7,2},{8,11},{9,12},{10,... | collective-permute-start | bytes 786440 | tf_op jit(solution)/shard_map/ppermute | solution.py:32
  40.0 32.3 %collective-permute-start.4 = (f32[4,4,16,256]{3,2,1,0:T(8,128)}, f32[4,4,16,256]{3,2,1,0:T(8,128)S(1)}, u32[]{:S(2)}, u32[]{:S(2)}) collective-permute-start(f32[4,4,16,256]{3,2,1,0:T(8,128)} %get-tuple-element.68), channel_id=1, source_target_pairs={{0,5},{1,6},{2,7},{3,0},{4,1},{5,2},{6,3},{7,4},{8,13},{9,14},{10,... | collective-permute-start | bytes 786440 | tf_op jit(solution)/shard_map/ppermute | solution.py:32
  42.0 41.6 %collective-permute-start.5 = (f32[4,4,16,256]{3,2,1,0:T(8,128)}, f32[4,4,16,256]{3,2,1,0:T(8,128)S(1)}, u32[]{:S(2)}, u32[]{:S(2)}) collective-permute-start(f32[4,4,16,256]{3,2,1,0:T(8,128)} %get-tuple-element.69), channel_id=1, source_target_pairs={{0,6},{1,7},{2,0},{3,1},{4,2},{5,3},{6,4},{7,5},{8,14},{9,15},{10,... | collective-permute-start | bytes 786440 | tf_op jit(solution)/shard_map/ppermute | solution.py:32
  45.2 53.9 %collective-permute-start.6 = (f32[4,4,16,256]{3,2,1,0:T(8,128)}, f32[4,4,16,256]{3,2,1,0:T(8,128)S(1)}, u32[]{:S(2)}, u32[]{:S(2)}) collective-permute-start(f32[4,4,16,256]{3,2,1,0:T(8,128)} %get-tuple-element.70), channel_id=1, source_target_pairs={{0,7},{1,0},{2,1},{3,2},{4,3},{5,4},{6,5},{7,6},{8,15},{9,8},{10,9... | collective-permute-start | bytes 786440 | tf_op jit(solution)/shard_map/ppermute | solution.py:32
  65.3 33.7 %collective-permute-start.7 = (f32[4,4,16,256]{3,2,1,0:T(8,128)S(1)}, f32[4,4,16,256]{3,2,1,0:T(8,128)S(1)}, u32[]{:S(2)}, u32[]{:S(2)}) collective-permute-start(f32[4,4,16,256]{3,2,1,0:T(8,128)S(1)} %get-tuple-element.151), channel_id=1, source_target_pairs={{0,1},{1,2},{2,3},{3,4},{4,5},{5,6},{6,7},{7,0},{8,9},{9,10},{10,1... | collective-permute-start | bytes 786440 | tf_op jit(solution)/shard_map/ppermute | solution.py:32
  65.5 33.6 %collective-permute-start.15 = (f32[4,4,16,256]{3,2,1,0:T(8,128)S(1)}, f32[4,4,16,256]{3,2,1,0:T(8,128)S(1)}, u32[]{:S(2)}, u32[]{:S(2)}) collective-permute-start(f32[4,4,16,256]{3,2,1,0:T(8,128)S(1)} %get-tuple-element.143), channel_id=1, source_target_pairs={{0,1},{1,2},{2,3},{3,4},{4,5},{5,6},{6,7},{7,0},{8,9},{9,10},{10,1... | collective-permute-start | bytes 786440 | tf_op jit(solution)/shard_map/ppermute | solution.py:32
  72.3 29.3 %collective-permute-start.16 = (f32[4,4,16,256]{3,2,1,0:T(8,128)S(1)}, f32[4,4,16,256]{3,2,1,0:T(8,128)S(1)}, u32[]{:S(2)}, u32[]{:S(2)}) collective-permute-start(f32[4,4,16,256]{3,2,1,0:T(8,128)S(1)} %get-tuple-element.142), channel_id=1, source_target_pairs={{0,2},{1,3},{2,4},{3,5},{4,6},{5,7},{6,0},{7,1},{8,10},{9,11},{10,... | collective-permute-start | bytes 786440 | tf_op jit(solution)/shard_map/ppermute | solution.py:32
  99.1 32.3 %collective-permute-start.19 = (f32[4,4,16,256]{3,2,1,0:T(8,128)}, f32[4,4,16,256]{3,2,1,0:T(8,128)}, u32[]{:S(2)}, u32[]{:S(2)}) collective-permute-start(f32[4,4,16,256]{3,2,1,0:T(8,128)} %get-tuple-element.139), channel_id=1, source_target_pairs={{0,5},{1,6},{2,7},{3,0},{4,1},{5,2},{6,3},{7,4},{8,13},{9,14},{10,... | collective-permute-start | bytes 786440 | tf_op jit(solution)/shard_map/ppermute | solution.py:32
  99.2 32.2 %collective-permute-start.20 = (f32[4,4,16,256]{3,2,1,0:T(8,128)S(1)}, f32[4,4,16,256]{3,2,1,0:T(8,128)}, u32[]{:S(2)}, u32[]{:S(2)}) collective-permute-start(f32[4,4,16,256]{3,2,1,0:T(8,128)S(1)} %get-tuple-element.138), channel_id=1, source_target_pairs={{0,6},{1,7},{2,0},{3,1},{4,2},{5,3},{6,4},{7,5},{8,14},{9,15},{10,... | collective-permute-start | bytes 786440 | tf_op jit(solution)/shard_map/ppermute | solution.py:32
  101.6 38.2 %collective-permute-start.21 = (f32[4,4,16,256]{3,2,1,0:T(8,128)S(1)}, f32[4,4,16,256]{3,2,1,0:T(8,128)}, u32[]{:S(2)}, u32[]{:S(2)}) collective-permute-start(f32[4,4,16,256]{3,2,1,0:T(8,128)S(1)} %get-tuple-element.137), channel_id=1, source_target_pairs={{0,7},{1,0},{2,1},{3,2},{4,3},{5,4},{6,5},{7,6},{8,15},{9,8},{10,9... | collective-permute-start | bytes 786440 | tf_op jit(solution)/shard_map/ppermute | solution.py:32
  106.1 36.5 %collective-permute-start.26 = (f32[4,4,16,256]{3,2,1,0:T(8,128)}, f32[4,4,16,256]{3,2,1,0:T(8,128)S(1)}, u32[]{:S(2)}, u32[]{:S(2)}) collective-permute-start(f32[4,4,16,256]{3,2,1,0:T(8,128)} %get-tuple-element.135), channel_id=1, source_target_pairs={{0,1},{1,2},{2,3},{3,4},{4,5},{5,6},{6,7},{7,0},{8,9},{9,10},{10,1... | collective-permute-start | bytes 786440 | tf_op jit(solution)/shard_map/ppermute | solution.py:32
  131.3 45.5 %collective-permute-start.28 = (f32[4,4,16,256]{3,2,1,0:T(8,128)}, f32[4,4,16,256]{3,2,1,0:T(8,128)S(1)}, u32[]{:S(2)}, u32[]{:S(2)}) collective-permute-start(f32[4,4,16,256]{3,2,1,0:T(8,128)} %get-tuple-element.133), channel_id=1, source_target_pairs={{0,3},{1,4},{2,5},{3,6},{4,7},{5,0},{6,1},{7,2},{8,11},{9,12},{10,... | collective-permute-start | bytes 786440 | tf_op jit(solution)/shard_map/ppermute | solution.py:32
  131.3 45.7 %collective-permute-start.29 = (f32[4,4,16,256]{3,2,1,0:T(8,128)}, f32[4,4,16,256]{3,2,1,0:T(8,128)S(1)}, u32[]{:S(2)}, u32[]{:S(2)}) collective-permute-start(f32[4,4,16,256]{3,2,1,0:T(8,128)} %get-tuple-element.132), channel_id=1, source_target_pairs={{0,4},{1,5},{2,6},{3,7},{4,0},{5,1},{6,2},{7,3},{8,12},{9,13},{10,... | collective-permute-start | bytes 786440 | tf_op jit(solution)/shard_map/ppermute | solution.py:32
  139.8 37.3 %collective-permute-start.30 = (f32[4,4,16,256]{3,2,1,0:T(8,128)}, f32[4,4,16,256]{3,2,1,0:T(8,128)S(1)}, u32[]{:S(2)}, u32[]{:S(2)}) collective-permute-start(f32[4,4,16,256]{3,2,1,0:T(8,128)} %get-tuple-element.131), channel_id=1, source_target_pairs={{0,5},{1,6},{2,7},{3,0},{4,1},{5,2},{6,3},{7,4},{8,13},{9,14},{10,... | collective-permute-start | bytes 786440 | tf_op jit(solution)/shard_map/ppermute | solution.py:32
  142.5 56.5 %collective-permute-start.8 = (f32[4,4,16,256]{3,2,1,0:T(8,128)}, f32[4,4,16,256]{3,2,1,0:T(8,128)S(1)}, u32[]{:S(2)}, u32[]{:S(2)}) collective-permute-start(f32[4,4,16,256]{3,2,1,0:T(8,128)} %get-tuple-element.150), channel_id=1, source_target_pairs={{0,2},{1,3},{2,4},{3,5},{4,6},{5,7},{6,0},{7,1},{8,10},{9,11},{10,... | collective-permute-start | bytes 786440 | tf_op jit(solution)/shard_map/ppermute | solution.py:32
  142.7 66.0 %collective-permute-start.9 = (f32[4,4,16,256]{3,2,1,0:T(8,128)}, f32[4,4,16,256]{3,2,1,0:T(8,128)S(1)}, u32[]{:S(2)}, u32[]{:S(2)}) collective-permute-start(f32[4,4,16,256]{3,2,1,0:T(8,128)} %get-tuple-element.149), channel_id=1, source_target_pairs={{0,3},{1,4},{2,5},{3,6},{4,7},{5,0},{6,1},{7,2},{8,11},{9,12},{10,... | collective-permute-start | bytes 786440 | tf_op jit(solution)/shard_map/ppermute | solution.py:32
  176.9 35.0 %collective-permute-start.10 = (f32[4,4,16,256]{3,2,1,0:T(8,128)}, f32[4,4,16,256]{3,2,1,0:T(8,128)}, u32[]{:S(2)}, u32[]{:S(2)}) collective-permute-start(f32[4,4,16,256]{3,2,1,0:T(8,128)} %get-tuple-element.148), channel_id=1, source_target_pairs={{0,4},{1,5},{2,6},{3,7},{4,0},{5,1},{6,2},{7,3},{8,12},{9,13},{10,... | collective-permute-start | bytes 786440 | tf_op jit(solution)/shard_map/ppermute | solution.py:32
  199.1 35.2 %collective-permute-start.11 = (f32[4,4,16,256]{3,2,1,0:T(8,128)S(1)}, f32[4,4,16,256]{3,2,1,0:T(8,128)S(1)}, u32[]{:S(2)}, u32[]{:S(2)}) collective-permute-start(f32[4,4,16,256]{3,2,1,0:T(8,128)S(1)} %copy-done.16), channel_id=1, source_target_pairs={{0,5},{1,6},{2,7},{3,0},{4,1},{5,2},{6,3},{7,4},{8,13},{9,14},{10,... | collective-permute-start | bytes 786440 | tf_op jit(solution)/shard_map/ppermute | solution.py:32
  208.7 28.5 %collective-permute-start.12 = (f32[4,4,16,256]{3,2,1,0:T(8,128)S(1)}, f32[4,4,16,256]{3,2,1,0:T(8,128)S(1)}, u32[]{:S(2)}, u32[]{:S(2)}) collective-permute-start(f32[4,4,16,256]{3,2,1,0:T(8,128)S(1)} %get-tuple-element.146), channel_id=1, source_target_pairs={{0,6},{1,7},{2,0},{3,1},{4,2},{5,3},{6,4},{7,5},{8,14},{9,15},{10,... | collective-permute-start | bytes 786440 | tf_op jit(solution)/shard_map/ppermute | solution.py:32
  262.8 50.3 %collective-permute-start.33 = (f32[32,1,16,256]{3,2,1,0:T(8,128)}, f32[32,1,16,256]{3,2,1,0:T(8,128)S(1)}, u32[]{:S(2)}, u32[]{:S(2)}) collective-permute-start(f32[32,1,16,256]{3,2,1,0:T(8,128)} %get-tuple-element.74), channel_id=1, source_target_pairs={{1,0},{2,1},{3,2},{4,3},{5,4},{6,5},{7,6},{9,8},{10,9},{11,10},{12... | collective-permute-start | bytes 1572872 | tf_op jit(solution)/shard_map/ppermute | solution.py:27
  269.7 30.4 %collective-permute-start.59 = (f32[16,3072]{1,0:T(8,128)}, f32[16,3072]{1,0:T(8,128)S(1)}, u32[]{:S(2)}, u32[]{:S(2)}) collective-permute-start(f32[16,3072]{1,0:T(8,128)} %get-tuple-element.108), channel_id=1, source_target_pairs={{0,4},{1,5},{2,6},{3,7},{4,0},{5,1},{6,2},{7,3},{8,12},{9,13},{10,... | collective-permute-start | bytes 589832 | tf_op jit(solution)/shard_map/ppermute | solution.py:32
  271.0 29.1 %collective-permute-start.60 = (f32[16,3072]{1,0:T(8,128)}, f32[16,3072]{1,0:T(8,128)S(1)}, u32[]{:S(2)}, u32[]{:S(2)}) collective-permute-start(f32[16,3072]{1,0:T(8,128)} %get-tuple-element.109), channel_id=1, source_target_pairs={{0,3},{1,4},{2,5},{3,6},{4,7},{5,0},{6,1},{7,2},{8,11},{9,12},{10,... | collective-permute-start | bytes 589832 | tf_op jit(solution)/shard_map/ppermute | solution.py:32
  271.0 32.7 %collective-permute-start.61 = (f32[16,3072]{1,0:T(8,128)}, f32[16,3072]{1,0:T(8,128)S(1)}, u32[]{:S(2)}, u32[]{:S(2)}) collective-permute-start(f32[16,3072]{1,0:T(8,128)} %get-tuple-element.110), channel_id=1, source_target_pairs={{0,2},{1,3},{2,4},{3,5},{4,6},{5,7},{6,0},{7,1},{8,10},{9,11},{10,... | collective-permute-start | bytes 589832 | tf_op jit(solution)/shard_map/ppermute | solution.py:32
  274.4 66.2 %collective-permute-start.14 = (f32[32,1,16,256]{3,2,1,0:T(8,128)}, f32[32,1,16,256]{3,2,1,0:T(8,128)}, u32[]{:S(2)}, u32[]{:S(2)}) collective-permute-start(f32[32,1,16,256]{3,2,1,0:T(8,128)} %get-tuple-element.71), channel_id=1, source_target_pairs={{0,1},{1,2},{2,3},{3,4},{4,5},{5,6},{6,7},{8,9},{9,10},{10,11},{11... | collective-permute-start | bytes 1572872 | tf_op jit(solution)/shard_map/ppermute | solution.py:27
  309.0 28.8 %collective-permute-start.66 = (f32[16,3072]{1,0:T(8,128)}, f32[16,3072]{1,0:T(8,128)S(1)}, u32[]{:S(2)}, u32[]{:S(2)}) collective-permute-start(f32[16,3072]{1,0:T(8,128)} %get-tuple-element.116), channel_id=1, source_target_pairs={{0,4},{1,5},{2,6},{3,7},{4,0},{5,1},{6,2},{7,3},{8,12},{9,13},{10,... | collective-permute-start | bytes 589832 | tf_op jit(solution)/shard_map/ppermute | solution.py:32
  362.8 34.1 %collective-permute-start.40 = (f32[16,3328]{1,0:T(8,128)}, f32[16,3328]{1,0:T(8,128)S(1)}, u32[]{:S(2)}, u32[]{:S(2)}) collective-permute-start(f32[16,3328]{1,0:T(8,128)} %get-tuple-element.85), channel_id=1, source_target_pairs={{0,7},{1,0},{2,1},{3,2},{4,3},{5,4},{6,5},{7,6},{8,15},{9,8},{10,9... | collective-permute-start | bytes 638984 | tf_op jit(solution)/shard_map/ppermute | solution.py:32
  364.0 33.0 %collective-permute-start.41 = (f32[16,3328]{1,0:T(8,128)}, f32[16,3328]{1,0:T(8,128)S(1)}, u32[]{:S(2)}, u32[]{:S(2)}) collective-permute-start(f32[16,3328]{1,0:T(8,128)} %get-tuple-element.86), channel_id=1, source_target_pairs={{0,6},{1,7},{2,0},{3,1},{4,2},{5,3},{6,4},{7,5},{8,14},{9,15},{10,... | collective-permute-start | bytes 638984 | tf_op jit(solution)/shard_map/ppermute | solution.py:32
  386.7 30.4 %collective-permute-start.42 = (f32[16,3328]{1,0:T(8,128)}, f32[16,3328]{1,0:T(8,128)S(1)}, u32[]{:S(2)}, u32[]{:S(2)}) collective-permute-start(f32[16,3328]{1,0:T(8,128)} %get-tuple-element.87), channel_id=1, source_target_pairs={{0,5},{1,6},{2,7},{3,0},{4,1},{5,2},{6,3},{7,4},{8,13},{9,14},{10,... | collective-permute-start | bytes 638984 | tf_op jit(solution)/shard_map/ppermute | solution.py:32
  386.7 30.4 %collective-permute-start.43 = (f32[16,3328]{1,0:T(8,128)}, f32[16,3328]{1,0:T(8,128)S(1)}, u32[]{:S(2)}, u32[]{:S(2)}) collective-permute-start(f32[16,3328]{1,0:T(8,128)} %get-tuple-element.88), channel_id=1, source_target_pairs={{0,4},{1,5},{2,6},{3,7},{4,0},{5,1},{6,2},{7,3},{8,12},{9,13},{10,... | collective-permute-start | bytes 638984 | tf_op jit(solution)/shard_map/ppermute | solution.py:32
  386.8 30.4 %collective-permute-start.44 = (f32[16,3328]{1,0:T(8,128)}, f32[16,3328]{1,0:T(8,128)S(1)}, u32[]{:S(2)}, u32[]{:S(2)}) collective-permute-start(f32[16,3328]{1,0:T(8,128)} %get-tuple-element.89), channel_id=1, source_target_pairs={{0,3},{1,4},{2,5},{3,6},{4,7},{5,0},{6,1},{7,2},{8,11},{9,12},{10,... | collective-permute-start | bytes 638984 | tf_op jit(solution)/shard_map/ppermute | solution.py:32
  (105 other events, 3036.8 us)
